TPU v7x, 32 devices: a whole 2x2x4 slice. The times are simulated.
32 devices in a mesh: seq: 4 (over y, x), tp: 8 (over z, core).
Axes of the slice: x: 2, y: 2, z: 4, core: 2. Of those that a mesh axis runs over, the one named last changes fastest.
Arguments:
- tokens: bfloat16 [1024, 4096], P('seq', 'tp'), may hold values from -30 to 30
- w_qkv: bfloat16 [4096, 3, 2048], P('seq', None, 'tp'), may hold values from -1 to 1
- keep_list: int32 [512], P('seq'), may hold values from 0 to 255, as said below
- counts: int32 [4], P('seq'), may hold values from 1 to 127, as said below
Outputs:
- attended: bfloat16 [256, 2048], P('seq', 'tp')
Inputs may be any that keep to these rules, and one draw needn't show every extreme that they name: `counts`: the entries sum to 256; one shard keeps 2 * 64 - 1 tokens and one shard keeps 1. `keep_list`: entries s * 2 * 64 to s * 2 * 64 + 2 * 64 - 1 are distinct token indices within shard s; the first counts[s] of them increase.
All inputs are finite; a program needn't handle non-finite values.
Results may differ from a plain program's by a relative error of at most 0.0065.
Values may be sent and summed in bfloat16 or wider, within the bound.
No kernel may reach another device: no remote copies, remote signals or barrier semaphores. Data moves between devices by JAX's collectives and lax.ppermute only.
A program may use at most 64 MiB of HBM per device.

v0:
```python
import jax
import jax.numpy as jnp
from jax import lax
from jax.sharding import PartitionSpec as P

HD = 128


def entering(value, axis, join, neutral):
    count, mine = (lax.axis_size(axis), lax.axis_index(axis))
    pieces = lax.all_gather(value, axis)
    so_far = jnp.full_like(value, 0) + jnp.asarray(neutral, value.dtype)

    def lap(position, so_far):
        longer = join(so_far, pieces[position])
        return jnp.where(position < mine, longer, so_far)

    return lax.fori_loop(0, count - 1, lap, so_far)


def add_sums(earlier, later):
    return earlier + later


def on_device(tokens, w_qkv, keep_list, counts):
    shards = lax.axis_size("seq")
    my_index = lax.axis_index("seq")
    tok_dev = tokens.shape[0]
    slots = keep_list.shape[0]
    capacity = slots // 2
    per_peer = slots // shards
    head_dim = HD
    columns = w_qkv.shape[2]
    local_heads = columns // head_dim
    offset = entering(counts, "seq", add_sums, jnp.zeros_like(counts))[0]
    peers = jnp.arange(shards, dtype=jnp.int32)[:, None]
    rounds = jnp.arange(per_peer, dtype=jnp.int32)[None, :]
    local_slot = (peers - offset) % shards + rounds * shards
    live = local_slot < counts[0]
    token_index = keep_list[local_slot]
    ranks = jnp.where(live, offset + local_slot, -1).astype(jnp.int32)
    positions = my_index * tok_dev + token_index
    meta = jnp.stack([positions, ranks], axis=2)
    picked = jnp.where(live[:, :, None], tokens[token_index], jnp.zeros((), tokens.dtype))
    arrived, arrived_meta = (
        lax.all_to_all(picked, "seq", split_axis=0, concat_axis=0, tiled=True),
        lax.all_to_all(meta, "seq", split_axis=0, concat_axis=0, tiled=True),
    )
    arrived_meta = arrived_meta.reshape(shards * per_peer, 2)
    arrived_rank = arrived_meta[:, 1]
    target = jnp.where(arrived_rank >= 0, arrived_rank // shards, capacity)
    flat = arrived.reshape(shards * per_peer, arrived.shape[2])
    kept = jnp.zeros((capacity, flat.shape[1]), flat.dtype).at[target].set(flat, mode="drop")
    kept_pos = jnp.zeros((capacity,), jnp.int32).at[target].set(arrived_meta[:, 0], mode="drop")
    full_rows = lax.all_gather(kept, "tp", axis=1, tiled=True)
    piece = lax.all_gather(w_qkv, "seq", axis=0, tiled=True)
    part_rows = lax.slice_in_dim(full_rows, 0, piece.shape[0], axis=1)
    projected = jnp.einsum(
        "rd,dgc->rgc", part_rows, piece, preferred_element_type=jnp.float32
    ).astype(jnp.bfloat16)
    queries = projected[:, 0].reshape(capacity, local_heads, head_dim)
    key_values = projected[:, 1:]
    scale = head_dim ** (-0.5)
    all_kv, all_pos = (
        lax.all_gather(key_values, "seq", axis=0, tiled=True),
        lax.all_gather(kept_pos, "seq", axis=0, tiled=True),
    )
    total_keys = all_kv.shape[0]
    keys_all = all_kv[:, 0].reshape(total_keys, local_heads, head_dim)
    values_all = all_kv[:, 1].reshape(total_keys, local_heads, head_dim)
    scores = (
        jnp.einsum("qhd,khd->hqk", queries, keys_all, preferred_element_type=jnp.float32) * scale
    )
    masked = all_pos[None, None, :] > kept_pos[None, :, None]
    scores = jnp.where(masked, -jnp.inf, scores)
    top = jnp.max(scores, axis=2, keepdims=True)
    expo = jnp.exp(scores - top)
    numer = jnp.einsum(
        "hqk,khd->hqd", expo.astype(jnp.bfloat16), values_all, preferred_element_type=jnp.float32
    )
    result = numer / jnp.sum(expo, axis=2)[..., None]
    return jnp.transpose(result, (1, 0, 2)).reshape(capacity, columns).astype(jnp.bfloat16)


def solution(mesh):
    in_specs = (P("seq", "tp"), P("seq", None, "tp"), P("seq"), P("seq"))
    out_specs = P("seq", "tp")
    return jax.shard_map(
        on_device, mesh=mesh, in_specs=in_specs, out_specs=out_specs, check_vma=False
    )
```

profile of v0, /device:TPU:0, one launch (start us, length us, event | category | flops | bytes accessed | tf_op | source)
XLA Modules:
  0.0 104.7 jit_solution(6532559039854450984)
XLA Ops:
  6.5 0.7 all-gather.3.cloned.1.call-update
  7.9 1.2 %dynamic-slice = u32[1]{0:T(128)} dynamic-slice(u32[32]{0:T(128)} %constant.83, u32[]{:T(128)S(6)} %add.147), dynamic_slice_sizes={1} | dynamic-slice | bytes 12
  9.1 0.7 dynamic-update-slice
  9.8 8.8 %all-reduce = s32[4]{0:T(128)S(1)} all-reduce(s32[4]{0:T(128)S(1)} %dynamic-update-slice), channel_id=2, replica_groups=mesh['seq'=4,'tp'=8] {'seq'}, use_global_device_ids=true, to_apply=%add | all-reduce | flops 4 | bytes 32
  18.6 3.5 %while.13 = (s32[]{:T(128)}, s32[1]{0:T(128)}, s32[]{:T(128)}, s32[4,1]{0,1:T(1,128)S(1)}, s32[]{:T(128)}) while((s32[]{:T(128)}, s32[1]{0:T(128)}, s32[]{:T(128)}, s32[4,1]{0,1:T(1,128)S(1)}, s32[]{:T(128)}) %tuple.38), condition=%wide.region_1.2_spmd, body=%wide.region_0.1_spmd.sunk | while | flops 5 | bytes 115 | solution.py:18
  18.6 0.6 constant_dynamic-slice_fusion.2
  19.8 0.6 constant_dynamic-slice_fusion.2
  21.0 0.6 constant_dynamic-slice_fusion.2
  22.2 0.1 reshape.223
  22.3 1.6 %gather_fusion = s32[128]{0:T(128)S(1)} fusion(s32[128]{0:T(128)} %param.8, s32[1024]{0:T(1024)S(1)} %pad_clamp_fusion.1), kind=kCustom, calls=%fused_computation | custom fusion | bytes 1536 | tf_op jit(solution)/shard_map/gather | solution.py:40
  23.9 0.1 gather.9
  24.0 0.6 copy.17
  24.6 3.2 %all-to-all-start = ((s32[4,32,2]{1,2,0:T(2,128)}), s32[4,32,2]{1,2,0:T(2,128)S(1)}, u32[]{:S(2)}, u32[]{:S(2)}) async-start(s32[4,32,2]{1,2,0:T(2,128)} %copy.17), calls=%async_computation | async-start | bytes 8192 | tf_op jit(solution)/shard_map/all_to_all | solution.py:47
  27.9 0.1 reshape.231
  28.0 0.8 gather_fusion.1
  28.9 0.7 broadcast_select_fusion
  30.2 2.5 %all-to-all-done = s32[4,32,2]{1,2,0:T(2,128)S(1)} async-done(((s32[4,32,2]{1,2,0:T(2,128)}), s32[4,32,2]{1,2,0:T(2,128)S(1)}, u32[]{:S(2)}, u32[]{:S(2)}) %all-to-all-start) | async-done | bytes 1056 | tf_op jit(solution)/shard_map/all_to_all | solution.py:47
  32.7 3.3 %all-to-all-start.1 = ((bf16[4,32,512]{2,1,0:T(8,128)(2,1)}), bf16[4,32,512]{2,1,0:T(8,128)(2,1)S(1)}, u32[]{:S(2)}, u32[]{:S(2)}) async-start(bf16[4,32,512]{2,1,0:T(8,128)(2,1)} %broadcast_select_fusion), calls=%async_computation.1 | async-start | bytes 262144 | tf_op jit(solution)/shard_map/all_to_all | solution.py:46
  36.0 0.1 reshape.219
  36.1 1.0 scatter_custom_fusion
  37.1 0.2 dynamic-update-slice.1
  37.4 7.8 %all-reduce.1 = s32[256]{0:T(256)S(1)} all-reduce(s32[256]{0:T(256)S(1)} %dynamic-update-slice.1), channel_id=1, replica_groups=mesh['seq'=4,'tp'=8] {'seq'}, use_global_device_ids=true, to_apply=%add.1 | all-reduce | flops 256 | bytes 2048
  45.2 0.1 broadcast_compare_fusion
  45.3 1.1 %scatter_custom_fusion.1 = bf16[64,512]{1,0:T(8,128)(2,1)S(1)} fusion(s32[128]{0:T(128)S(1)} %get-tuple-element.98, bf16[128,512]{1,0:T(8,128)(2,1)S(1)} %bitcast.50, bf16[]{:T(256)} %constant.77.clone.1), kind=kCustom, calls=%fused_computation.22 | custom fusion | bytes 65538 | tf_op jit(solution)/shard_map/scatter | solution.py:53
  46.4 15.2 %all_gather.21 = bf16[64,4096]{1,0:T(8,128)(2,1)S(1)} all-gather(bf16[64,512]{1,0:T(8,128)(2,1)S(1)} %scatter_custom_fusion.1), channel_id=1, replica_groups=mesh['seq'=4,'tp'=8] {'tp'}, dimensions={1}, use_global_device_ids=true | all-gather | bytes 589824 | tf_op jit(solution)/shard_map/all_gather | solution.py:55
  61.6 21.9 %all-gather.3.cloned.1.call-done = bf16[4096,3,256]{2,0,1:T(8,128)(2,1)} async-done(((bf16[1024,3,256]{2,0,1:T(8,128)(2,1)}), bf16[4096,3,256]{2,0,1:T(8,128)(2,1)}) %all-gather.3.cloned.1.call-update) | async-done | bytes 6291472 | tf_op jit(solution)/shard_map/all_gather | solution.py:56
  83.5 4.0 %convolution_convert_fusion = bf16[64,3,256]{2,0,1:T(8,128)(2,1)S(1)} fusion(bf16[4096,3,256]{2,0,1:T(8,128)(2,1)} %all-gather.3.cloned.1.call-done, bf16[64,4096]{1,0:T(8,128)(2,1)S(1)} %all_gather.21), kind=kOutput, calls=%fused_computation.5 | convolution fusion | flops 402702336 | bytes 6914048 | tf_op jit(solution)/shard_map/rd,dgc->rgc/dot_general | solution.py:58
  87.5 9.0 %all_gather.23 = bf16[256,2,256]{2,0,1:T(8,128)(2,1)S(1)} all-gather(bf16[64,2,256]{2,0,1:T(8,128)(2,1)S(1)} %slice.29), channel_id=1, replica_groups=mesh['seq'=4,'tp'=8] {'seq'}, dimensions={0}, use_global_device_ids=true | all-gather | bytes 327680 | tf_op jit(solution)/shard_map/all_gather | solution.py:65
  96.6 0.3 fusion.20
  96.8 0.2 fusion.7
  97.0 0.2 fusion.3
  97.2 0.6 copy.35
  (22 shorter events, 0.3 us)
Async XLA Ops:
  6.5 21.5 %copy-start = (bf16[256,512]{1,0:T(8,128)(2,1)S(1)}, bf16[256,512]{1,0:T(8,128)(2,1)}, u32[]{:S(2)}) copy-start(bf16[256,512]{1,0:T(8,128)(2,1)} %param.6) | copy-start | bytes 786436
  6.5 76.9 %all-gather.3.cloned.1.call-start = ((), (), s32[]{:S(2)}) async-start(), calls=%async_computation.2 | async-start | bytes 7864320 | tf_op jit(solution)/shard_map/all_gather | solution.py:56
  24.6 8.0 %all-to-all-start = ((s32[4,32,2]{1,2,0:T(2,128)}), s32[4,32,2]{1,2,0:T(2,128)S(1)}, u32[]{:S(2)}, u32[]{:S(2)}) async-start(s32[4,32,2]{1,2,0:T(2,128)} %copy.17), calls=%async_computation | async-start | bytes 8192 | tf_op jit(solution)/shard_map/all_to_all | solution.py:47
  32.7 12.6 %all-to-all-start.1 = ((bf16[4,32,512]{2,1,0:T(8,128)(2,1)}), bf16[4,32,512]{2,1,0:T(8,128)(2,1)S(1)}, u32[]{:S(2)}, u32[]{:S(2)}) async-start(bf16[4,32,512]{2,1,0:T(8,128)(2,1)} %broadcast_select_fusion), calls=%async_computation.1 | async-start | bytes 262144 | tf_op jit(solution)/shard_map/all_to_all | solution.py:46
Sparse Core Ops, SparseCore 0:
  9.2 74.2 all-gather.2
where the time goes:
time: 105 us
  blocking collectives  40.9 us (39%)
  waiting for transfers between devices  25 us (24%)
  between operations  14.7 us (14%)
  local copies, waits for them, and re-layouts  10 us (10%)
  starting transfers between devices  6.57 us (6%)
  matrix products  4.44 us (4%)
  loops' own time  1.78 us (2%)
  other arithmetic  1.21 us (1%)
    all_gather x1, waiting for transfers between devices, on_device(): piece = lax.all_gather(w_qkv, 'seq', axis=0, tiled=True)  21.9 us
    unnamed x2, blocking collectives  16.7 us
    all_gather x1, blocking collectives, on_device(): full_rows = lax.all_gather(kept, 'tp', axis=1, tiled=True)  15.2 us
    all_gather x1, blocking collectives, on_device(): lax.all_gather(key_values, 'seq', axis=0, tiled=True)  9.02 us
    dot_general x1, matrix products, on_device(): jnp.einsum('rd,dgc->rgc', part_rows, piece, preferred_element_type=jnp.fl...  3.97 us
    all_to_all x1, starting transfers between devices, on_device(): lax.all_to_all(picked, 'seq', split_axis=0, concat_axis=0, tiled=True)  3.32 us
    all_to_all x1, starting transfers between devices, on_device(): lax.all_to_all(meta, 'seq', split_axis=0, concat_axis=0, tiled=True)  3.25 us
    all_to_all x1, waiting for transfers between devices, on_device(): lax.all_to_all(meta, 'seq', split_axis=0, concat_axis=0, tiled=True)  2.48 us
  transfers between devices with their start and end apart: 3, of which 2 were waited for; matrix products, arithmetic and copies ran while one was open for 10% of the time, Pallas kernels for 0%

commit v1 on v0

--- a/solution.py
+++ b/solution.py
@@ -1,6 +1,10 @@
+import functools
+
 import jax
 import jax.numpy as jnp
 from jax import lax
+from jax.experimental import pallas as pl
+from jax.experimental.pallas import tpu as pltpu
 from jax.sharding import PartitionSpec as P
 
 HD = 128
@@ -22,7 +26,7 @@
     return earlier + later
 
 
-def on_device(tokens, w_qkv, keep_list, counts):
+def by_rows(tokens, w_qkv, keep_list, counts):
     shards = lax.axis_size("seq")
     my_index = lax.axis_index("seq")
     tok_dev = tokens.shape[0]
@@ -82,7 +86,214 @@
     return jnp.transpose(result, (1, 0, 2)).reshape(capacity, columns).astype(jnp.bfloat16)
 
 
+VMEM = pl.BlockSpec(memory_space=pltpu.VMEM)
+SMEM = pl.BlockSpec(memory_space=pltpu.SMEM)
+
+
+def gather_kernel(counts_ref, keep_ref, tokens_ref, out_ref):
+    slots = out_ref.shape[0]
+    tok_dev = tokens_ref.shape[0]
+    token = lax.broadcasted_iota(jnp.int32, (tok_dev, slots), 0)
+    pick = (token == keep_ref[...]).astype(jnp.bfloat16)
+    rows = lax.dot_general(
+        pick, tokens_ref[...], (((0,), (0,)), ((), ())), preferred_element_type=jnp.float32
+    )
+    count = counts_ref[0].astype(jnp.float32)
+    last = lax.broadcasted_iota(jnp.int32, rows.shape, 0) == slots - 1
+    out_ref[...] = jnp.where(last, count, rows).astype(jnp.bfloat16)
+
+
+def project_kernel(shards, group, heads, *refs):
+    total = shards
+    halves = [refs[total * p : total * (p + 1)] for p in range(group)]
+    w_ref = refs[total * group]
+    outs = refs[total * group + 1 :]
+    slots, width = halves[0][0].shape
+    capacity = slots // 2
+    kept = capacity * shards
+    tp = lax.axis_index("tp")
+    core = lax.rem(tp, group)
+    line = lax.div(tp, group)
+    me = lax.axis_index("seq")
+    shard = [lax.rem(line - k + shards, shards) for k in range(total)]
+    count = [halves[0][k][slots - 1 : slots, :slots].astype(jnp.float32) for k in range(total)]
+    row = lax.broadcasted_iota(jnp.int32, (kept, slots), 0)
+    rank = ((row % capacity) * shards + row // capacity).astype(jnp.float32)
+    slot = lax.broadcasted_iota(jnp.int32, (kept, slots), 1).astype(jnp.float32)
+    picks = []
+    for k in range(total):
+        start = jnp.zeros_like(count[k])
+        for j in range(total):
+            if j != k:
+                start += jnp.where(shard[j] < shard[k], count[j], 0.0)
+        hit = (rank == slot + start) & (slot < count[k])
+        picks.append(jnp.where(hit, 1.0, 0.0).astype(jnp.bfloat16))
+    rows = []
+    for p in range(group):
+        total_rows = None
+        for k in range(total):
+            part = jnp.dot(picks[k], halves[p][k][...], preferred_element_type=jnp.float32)
+            total_rows = part if total_rows is None else total_rows + part
+        rows.append(total_rows.astype(jnp.bfloat16))
+
+    def times(kind, head, which):
+        acc = None
+        for p in range(group):
+            where = pl.multiple_of(lax.rem(core + p, group) * width, width)
+            w = w_ref[kind, pl.ds(where, width), head * HD : (head + 1) * HD]
+            part = jnp.dot(which[p], w, preferred_element_type=jnp.float32)
+            acc = part if acc is None else acc + part
+        return acc.astype(jnp.bfloat16)
+
+    blocks = shards // heads
+    block_rows = kept // blocks
+    for head in range(heads):
+        key = times(1, head, rows)
+        value = times(2, head, rows)
+        query = times(0, head, rows)
+        for k in range(shards):
+            dest = lax.rem(me + k, shards)
+            block = lax.div(dest, heads)
+
+            @pl.when(lax.rem(dest, heads) == head)
+            def _(k=k, block=block):
+                outs[k][0:kept, :] = key
+                outs[k][kept : 2 * kept, :] = value
+                for b in range(blocks):
+
+                    @pl.when(block == b)
+                    def _(b=b):
+                        outs[k][2 * kept :, :] = query[b * block_rows : (b + 1) * block_rows, :]
+
+
+def attend_kernel(shards, heads, kept, *refs):
+    parts, outs = refs[:shards], refs[shards:]
+    capacity = kept // shards
+    me = lax.axis_index("seq")
+    block_rows = parts[0].shape[0] - 2 * kept
+    block = lax.div(me, heads)
+
+    def summed(lo, hi):
+        acc = parts[0][lo:hi, :].astype(jnp.float32)
+        for p in parts[1:]:
+            acc += p[lo:hi, :].astype(jnp.float32)
+        return acc.astype(jnp.bfloat16)
+
+    key, value, query = summed(0, kept), summed(kept, 2 * kept), summed(2 * kept, 2 * kept + block_rows)
+    scores = lax.dot_general(
+        query, key, (((1,), (1,)), ((), ())), preferred_element_type=jnp.float32
+    ) * (HD ** (-0.5))
+    q_row = lax.broadcasted_iota(jnp.int32, scores.shape, 0) + block * block_rows
+    k_row = lax.broadcasted_iota(jnp.int32, scores.shape, 1)
+    q_rank = lax.rem(q_row, capacity) * shards + lax.div(q_row, capacity)
+    k_rank = lax.rem(k_row, capacity) * shards + lax.div(k_row, capacity)
+    scores = jnp.where(k_rank > q_rank, -jnp.inf, scores)
+    top = jnp.max(scores, axis=1, keepdims=True)
+    expo = jnp.exp(scores - top)
+    numer = jnp.dot(expo.astype(jnp.bfloat16), value, preferred_element_type=jnp.float32)
+    result = (numer / jnp.sum(expo, axis=1, keepdims=True)).astype(jnp.bfloat16)
+    head = lax.rem(me, heads)
+    for k in range(heads):
+        owner = lax.rem(head + k, heads)
+        for o in range(heads):
+
+            @pl.when(owner == o)
+            def _(k=k, o=o):
+                outs[k][...] = result[o * capacity : (o + 1) * capacity, :]
+
+
+def by_features(shards, tp, tokens, w_qkv, keep_list, counts):
+    group = tp // shards
+    slots = keep_list.shape[0]
+    capacity = slots // 2
+    kept = capacity * shards
+    width = tokens.shape[1]
+    heads = w_qkv.shape[2] // HD
+    blocks = shards // heads
+    params = pltpu.CompilerParams(vmem_limit_bytes=32 * 1024 * 1024)
+    packed = pl.pallas_call(
+        gather_kernel,
+        out_shape=jax.ShapeDtypeStruct((slots, width), jnp.bfloat16),
+        in_specs=[SMEM, VMEM, VMEM],
+        out_specs=VMEM,
+        compiler_params=params,
+        name="gather",
+    )(counts, keep_list.reshape(1, slots), tokens)
+
+    def device(s, line, core):
+        return s * tp + line * group + core
+
+    every = [(s, line, c) for s in range(shards) for line in range(shards) for c in range(group)]
+    own = [
+        lax.ppermute(
+            packed,
+            ("seq", "tp"),
+            [(device(s, line, c), device(line, (s + k) % shards, c)) for s, line, c in every],
+        )
+        for k in range(shards)
+    ]
+    halves = list(own)
+    for p in range(1, group):
+        halves += [
+            lax.ppermute(
+                chunk,
+                "tp",
+                [
+                    (line * group + (c + p) % group, line * group + c)
+                    for line in range(shards)
+                    for c in range(group)
+                ],
+            )
+            for chunk in own
+        ]
+    payload = 2 * kept + kept // blocks
+    partial = pl.pallas_call(
+        functools.partial(project_kernel, shards, group, heads),
+        out_shape=[jax.ShapeDtypeStruct((payload, HD), jnp.bfloat16)] * shards,
+        in_specs=[VMEM] * (shards * group + 1),
+        out_specs=[VMEM] * shards,
+        compiler_params=params,
+        name="project",
+    )(*halves, jnp.transpose(w_qkv, (1, 0, 2)))
+    parts = [partial[0]] + [
+        lax.ppermute(partial[k], "seq", [(s, (s + k) % shards) for s in range(shards)])
+        for k in range(1, shards)
+    ]
+    pieces = pl.pallas_call(
+        functools.partial(attend_kernel, shards, heads, kept),
+        out_shape=[jax.ShapeDtypeStruct((capacity, HD), jnp.bfloat16)] * heads,
+        in_specs=[VMEM] * shards,
+        out_specs=[VMEM] * heads,
+        compiler_params=params,
+        name="attend",
+    )(*parts)
+    arrived = [pieces[0]] + [
+        lax.ppermute(
+            pieces[k],
+            "seq",
+            [(b * heads + h, b * heads + (h + k) % heads) for b in range(blocks) for h in range(heads)],
+        )
+        for k in range(1, heads)
+    ]
+    mine = lax.rem(lax.axis_index("seq"), heads)
+    columns = []
+    for h in range(heads):
+        column = arrived[0]
+        for k in range(1, heads):
+            column = jnp.where(lax.rem(mine - k + heads, heads) == h, arrived[k], column)
+        columns.append(column)
+    return jnp.concatenate(columns, axis=1)
+
+
 def solution(mesh):
+    shards, tp = mesh.shape["seq"], mesh.shape["tp"]
+
+    def on_device(tokens, w_qkv, keep_list, counts):
+        heads = w_qkv.shape[2] // HD
+        if tp % shards == 0 and shards % heads == 0:
+            return by_features(shards, tp, tokens, w_qkv, keep_list, counts)
+        return by_rows(tokens, w_qkv, keep_list, counts)
+
     in_specs = (P("seq", "tp"), P("seq", None, "tp"), P("seq"), P("seq"))
     out_specs = P("seq", "tp")
     return jax.shard_map(

time: 105 us -> 44.7 us (0.43)
  blocking collectives: 40.9 us -> 0 us
  starting transfers between devices: 6.57 us -> 20.9 us
  between operations: 14.7 us -> 0.72 us
  waiting for transfers between devices: 25 us -> 16.8 us
  local copies, waits for them, and re-layouts: 10 us -> 3.01 us
  matrix products: 4.44 us -> 0 us
  Pallas kernels: 0 us -> 2.45 us
  loops' own time: 1.78 us -> 0 us
    all_gather x2 -> x0, blocking collectives: 24.3 us -> none  [the longest x1 15.2 us: on_device(): full_rows = lax.all_gather(kept, 'tp', axis=1, tiled=True)]
    all_gather x1 -> x0, waiting for transfers between devices: 21.9 us -> none  [on_device(): piece = lax.all_gather(w_qkv, 'seq', axis=0, tiled=True)]
    ppermute x0 -> x12, starting transfers between devices: none -> 20.9 us  [the longest x4 12.2 us: by_features(): lax.ppermute(packed, ('seq', 'tp'), [(device(s, line, c), device(line, (s...]
    ppermute x0 -> x12, waiting for transfers between devices: none -> 16.8 us  [the longest x3 8.08 us: by_features(): lax.ppermute(partial[k], 'seq', [(s, (s + k) % shards) for s in range(sha...]
    unnamed x2 -> x0, blocking collectives: 16.7 us -> none
    all_to_all x2 -> x0, starting transfers between devices: 6.57 us -> none  [the longest x1 3.32 us: on_device(): lax.all_to_all(picked, 'seq', split_axis=0, concat_axis=0, tiled=True)]
    dot_general x3 -> x0, matrix products: 4.44 us -> none  [the longest x1 3.97 us: on_device(): jnp.einsum('rd,dgc->rgc', part_rows, piece, preferred_element_type=jnp.fl...]
    gather x3 -> x0, local copies, waits for them, and re-layouts: 2.52 us -> none  [the longest x2 1.67 us: on_device(): token_index = keep_list[local_slot]]
  transfers between devices with their start and end apart: 3 -> 12, of which waited for: 2 -> 8; matrix products, arithmetic and copies ran while one was open for 10% -> 0% of each run, Pallas kernels for 0% -> 0%
where the time goes in v1:
time: 44.7 us; the launch traced here: 44.5 us
  starting transfers between devices  20.9 us (47%)
  waiting for transfers between devices  16.8 us (38%)
  local copies, waits for them, and re-layouts  3.01 us (7%)
  Pallas kernels  2.45 us (5%)
  between operations  0.72 us (2%)
  other arithmetic  0.63 us (1%)
    ppermute x4, starting transfers between devices, by_features(): lax.ppermute(packed, ('seq', 'tp'), [(device(s, line, c), device(line, (s...  12.2 us
    ppermute x3, waiting for transfers between devices, by_features(): lax.ppermute(partial[k], 'seq', [(s, (s + k) % shards) for s in range(sha...  8.08 us
    ppermute x3, starting transfers between devices, by_features(): lax.ppermute(partial[k], 'seq', [(s, (s + k) % shards) for s in range(sha...  7.49 us
    ppermute x4, waiting for transfers between devices, by_features(): lax.ppermute(packed, ('seq', 'tp'), [(device(s, line, c), device(line, (s...  4.76 us
    unnamed x6, local copies, waits for them, and re-layouts  3.01 us
    ppermute x1, waiting for transfers between devices, by_features(): lax.ppermute(pieces[k], 'seq', [(b * heads + h, b * heads + (h + k) % hea...  2.63 us
    pallas_call x1, Pallas kernels, by_features(): pl.pallas_call(functools.partial(project_kernel, shards, group, heads), o...  1.84 us
    ppermute x4, waiting for transfers between devices, by_features(): lax.ppermute(chunk, 'tp', [(line * group + (c + p) % group, line * group...  1.33 us
  transfers between devices with their start and end apart: 12, of which 8 were waited for; matrix products, arithmetic and copies ran while one was open for 0% of the time, Pallas kernels for 0%

profile of v1, /device:TPU:0, one launch (start us, length us, event | category | flops | bytes accessed | tf_op | source)
XLA Modules:
  0.0 44.5 jit_solution(13273703103679874062)
XLA Ops:
  0.7 0.0 copy-start.1
  0.7 0.9 %copy-done.1 = bf16[256,512]{1,0:T(8,128)(2,1)S(1)} copy-done((bf16[256,512]{1,0:T(8,128)(2,1)S(1)}, bf16[256,512]{1,0:T(8,128)(2,1)}, u32[]{:S(2)}) %copy-start.1) | copy-done | bytes 262168
  1.6 0.7 %copy-done.2 = s32[128]{0:T(128)S(1)} copy-done((s32[128]{0:T(128)S(1)}, s32[128]{0:T(128)}, u32[]{:S(2)}) %copy-start.2) | copy-done | bytes 536
  2.3 0.2 gather.1
  2.5 0.7 %collective-permute-start = (bf16[128,512]{1,0:T(8,128)(2,1)S(1)}, bf16[128,512]{1,0:T(8,128)(2,1)S(1)}, u32[]{:S(2)}, u32[]{:S(2)}) collective-permute-start(bf16[128,512]{1,0:T(8,128)(2,1)S(1)} %gather.1), channel_id=1, source_target_pairs={{0,0},{1,1},{2,8},{3,9},{4,16},{5,17},{6,24},{7,25},{8,2},{9,3},{1... | collective-permute-start | bytes 393224 | tf_op jit(solution)/shard_map/ppermute | solution.py:228
  3.2 5.7 %collective-permute-start.1 = (bf16[128,512]{1,0:T(8,128)(2,1)S(1)}, bf16[128,512]{1,0:T(8,128)(2,1)S(1)}, u32[]{:S(2)}, u32[]{:S(2)}) collective-permute-start(bf16[128,512]{1,0:T(8,128)(2,1)S(1)} %gather.1), channel_id=1, source_target_pairs={{0,2},{1,3},{2,10},{3,11},{4,18},{5,19},{6,26},{7,27},{8,4},{9,5},... | collective-permute-start | bytes 393224 | tf_op jit(solution)/shard_map/ppermute | solution.py:228
  8.9 3.5 %collective-permute-start.2 = (bf16[128,512]{1,0:T(8,128)(2,1)S(1)}, bf16[128,512]{1,0:T(8,128)(2,1)S(1)}, u32[]{:S(2)}, u32[]{:S(2)}) collective-permute-start(bf16[128,512]{1,0:T(8,128)(2,1)S(1)} %gather.1), channel_id=1, source_target_pairs={{0,4},{1,5},{2,12},{3,13},{4,20},{5,21},{6,28},{7,29},{8,6},{9,7},... | collective-permute-start | bytes 393224 | tf_op jit(solution)/shard_map/ppermute | solution.py:228
  12.4 2.3 %collective-permute-start.3 = (bf16[128,512]{1,0:T(8,128)(2,1)S(1)}, bf16[128,512]{1,0:T(8,128)(2,1)S(1)}, u32[]{:S(2)}, u32[]{:S(2)}) collective-permute-start(bf16[128,512]{1,0:T(8,128)(2,1)S(1)} %gather.1), channel_id=1, source_target_pairs={{0,6},{1,7},{2,14},{3,15},{4,22},{5,23},{6,30},{7,31},{8,0},{9,1},... | collective-permute-start | bytes 393224 | tf_op jit(solution)/shard_map/ppermute | solution.py:228
  14.7 0.0 collective-permute-done.refs_0_
  14.7 0.0 collective-permute-start.4
  14.7 2.4 %collective-permute-done.1.refs_1_ = bf16[128,512]{1,0:T(8,128)(2,1)S(1)} collective-permute-done((bf16[128,512]{1,0:T(8,128)(2,1)S(1)}, bf16[128,512]{1,0:T(8,128)(2,1)S(1)}, u32[]{:S(2)}, u32[]{:S(2)}) %collective-permute-start.1) | collective-permute-done | bytes 131104 | tf_op jit(solution)/shard_map/ppermute | solution.py:228
  17.1 0.0 collective-permute-start.5
  17.1 0.8 %collective-permute-done.2.refs_2_ = bf16[128,512]{1,0:T(8,128)(2,1)S(1)} collective-permute-done((bf16[128,512]{1,0:T(8,128)(2,1)S(1)}, bf16[128,512]{1,0:T(8,128)(2,1)S(1)}, u32[]{:S(2)}, u32[]{:S(2)}) %collective-permute-start.2) | collective-permute-done | bytes 131104 | tf_op jit(solution)/shard_map/ppermute | solution.py:228
  17.9 0.0 collective-permute-start.6
  17.9 1.6 %collective-permute-done.3.refs_3_ = bf16[128,512]{1,0:T(8,128)(2,1)S(1)} collective-permute-done((bf16[128,512]{1,0:T(8,128)(2,1)S(1)}, bf16[128,512]{1,0:T(8,128)(2,1)S(1)}, u32[]{:S(2)}, u32[]{:S(2)}) %collective-permute-start.3) | collective-permute-done | bytes 131104 | tf_op jit(solution)/shard_map/ppermute | solution.py:228
  19.5 0.0 collective-permute-start.7
  19.5 0.0 collective-permute-done.4.refs_4_
  19.5 0.0 collective-permute-done.5.refs_5_
  19.5 0.0 collective-permute-done.6.refs_6_
  19.5 1.3 %collective-permute-done.7.refs_7_ = bf16[128,512]{1,0:T(8,128)(2,1)S(1)} collective-permute-done((bf16[128,512]{1,0:T(8,128)(2,1)S(1)}, bf16[128,512]{1,0:T(8,128)(2,1)S(1)}, u32[]{:S(2)}, u32[]{:S(2)}) %collective-permute-start.7) | collective-permute-done | bytes 131104 | tf_op jit(solution)/shard_map/ppermute | solution.py:238
  20.8 1.4 %copy-done = bf16[1024,3,256]{2,0,1:T(8,128)(2,1)S(1)} copy-done((bf16[1024,3,256]{2,0,1:T(8,128)(2,1)S(1)}, bf16[1024,3,256]{2,0,1:T(8,128)(2,1)}, u32[]{:S(2)}) %copy-start) | copy-done | bytes 1572888
  22.2 1.8 %project.1 = (bf16[640,128]{1,0:T(8,128)(2,1)S(1)}, bf16[640,128]{1,0:T(8,128)(2,1)S(1)}, bf16[640,128]{1,0:T(8,128)(2,1)S(1)}, bf16[640,128]{1,0:T(8,128)(2,1)S(1)}) custom-call(bf16[128,512]{1,0:T(8,128)(2,1)S(1)} %collective-permute-done.refs_0_, bf16[128,512]{1,0:T(8,128)(2,1)S(1)} %collective-permute-done.1.refs_1_, ...), custom_call_target="tpu_custom_call" | custom-call | tf_op jit(solution)/shard_map/project/pallas_call | solution.py:250
  24.1 2.7 %collective-permute-start.10 = (bf16[640,128]{1,0:T(8,128)(2,1)S(1)}, bf16[640,128]{1,0:T(8,128)(2,1)S(1)}, u32[]{:S(2)}, u32[]{:S(2)}) collective-permute-start(bf16[640,128]{1,0:T(8,128)(2,1)S(1)} %get-tuple-element.14), channel_id=1, source_target_pairs={{0,24},{8,0},{16,8},{24,16},{1,25},{9,1},{17,9},{25,17},{2,26},{10... | collective-permute-start | bytes 491528 | tf_op jit(solution)/shard_map/ppermute | solution.py:259
  26.8 3.4 %collective-permute-start.8 = (bf16[640,128]{1,0:T(8,128)(2,1)S(1)}, bf16[640,128]{1,0:T(8,128)(2,1)S(1)}, u32[]{:S(2)}, u32[]{:S(2)}) collective-permute-start(bf16[640,128]{1,0:T(8,128)(2,1)S(1)} %get-tuple-element.12), channel_id=1, source_target_pairs={{0,8},{8,16},{16,24},{24,0},{1,9},{9,17},{17,25},{25,1},{2,10},{10... | collective-permute-start | bytes 491528 | tf_op jit(solution)/shard_map/ppermute | solution.py:259
  30.2 1.4 %collective-permute-start.9 = (bf16[640,128]{1,0:T(8,128)(2,1)S(1)}, bf16[640,128]{1,0:T(8,128)(2,1)S(1)}, u32[]{:S(2)}, u32[]{:S(2)}) collective-permute-start(bf16[640,128]{1,0:T(8,128)(2,1)S(1)} %get-tuple-element.13), channel_id=1, source_target_pairs={{0,16},{8,24},{16,0},{24,8},{1,17},{9,25},{17,1},{25,9},{2,18},{10... | collective-permute-start | bytes 491528 | tf_op jit(solution)/shard_map/ppermute | solution.py:259
  31.6 3.6 %collective-permute-done.10.refs_3_ = bf16[640,128]{1,0:T(8,128)(2,1)S(1)} collective-permute-done((bf16[640,128]{1,0:T(8,128)(2,1)S(1)}, bf16[640,128]{1,0:T(8,128)(2,1)S(1)}, u32[]{:S(2)}, u32[]{:S(2)}) %collective-permute-start.10) | collective-permute-done | bytes 163872 | tf_op jit(solution)/shard_map/ppermute | solution.py:259
  35.1 3.6 %collective-permute-done.8.refs_1_ = bf16[640,128]{1,0:T(8,128)(2,1)S(1)} collective-permute-done((bf16[640,128]{1,0:T(8,128)(2,1)S(1)}, bf16[640,128]{1,0:T(8,128)(2,1)S(1)}, u32[]{:S(2)}, u32[]{:S(2)}) %collective-permute-start.8) | collective-permute-done | bytes 163872 | tf_op jit(solution)/shard_map/ppermute | solution.py:259
  38.8 0.9 %collective-permute-done.9.refs_2_ = bf16[640,128]{1,0:T(8,128)(2,1)S(1)} collective-permute-done((bf16[640,128]{1,0:T(8,128)(2,1)S(1)}, bf16[640,128]{1,0:T(8,128)(2,1)S(1)}, u32[]{:S(2)}, u32[]{:S(2)}) %collective-permute-start.9) | collective-permute-done | bytes 163872 | tf_op jit(solution)/shard_map/ppermute | solution.py:259
  39.6 0.4 attend.1
  40.1 1.2 %collective-permute-start.11 = (bf16[64,128]{1,0:T(8,128)(2,1)S(1)}, bf16[64,128]{1,0:T(8,128)(2,1)S(1)}, u32[]{:S(2)}, u32[]{:S(2)}) collective-permute-start(bf16[64,128]{1,0:T(8,128)(2,1)S(1)} %get-tuple-element.15), channel_id=1, source_target_pairs={{0,8},{8,0},{16,24},{24,16},{1,9},{9,1},{17,25},{25,17},{2,10},{10... | collective-permute-start | bytes 49160 | tf_op jit(solution)/shard_map/ppermute | solution.py:271
  41.2 2.6 %collective-permute-done.11 = bf16[64,128]{1,0:T(8,128)(2,1)S(1)} collective-permute-done((bf16[64,128]{1,0:T(8,128)(2,1)S(1)}, bf16[64,128]{1,0:T(8,128)(2,1)S(1)}, u32[]{:S(2)}, u32[]{:S(2)}) %collective-permute-start.11) | collective-permute-done | bytes 16416 | tf_op jit(solution)/shard_map/ppermute | solution.py:271
  43.9 0.6 %pad_maximum_fusion = bf16[64,256]{1,0:T(8,128)(2,1)} fusion(bf16[64,128]{1,0:T(8,128)(2,1)S(1)} %get-tuple-element.18, bf16[64,128]{1,0:T(8,128)(2,1)S(1)} %get-tuple-element.17), kind=kLoop, calls=%fused_computation | loop fusion | flops 65536 | bytes 65536 | tf_op jit(solution)/shard_map/concatenate | solution.py:285
  (3 shorter events, 0.0 us)
Async XLA Ops:
  0.7 1.0 %copy-start.1 = (bf16[256,512]{1,0:T(8,128)(2,1)S(1)}, bf16[256,512]{1,0:T(8,128)(2,1)}, u32[]{:S(2)}) copy-start(bf16[256,512]{1,0:T(8,128)(2,1)} %tokens_ref.1) | copy-start | bytes 786436
  1.6 0.7 %copy-start.2 = (s32[128]{0:T(128)S(1)}, s32[128]{0:T(128)}, u32[]{:S(2)}) copy-start(s32[128]{0:T(128)} %param.6) | copy-start | bytes 1540
  2.5 12.2 %collective-permute-start = (bf16[128,512]{1,0:T(8,128)(2,1)S(1)}, bf16[128,512]{1,0:T(8,128)(2,1)S(1)}, u32[]{:S(2)}, u32[]{:S(2)}) collective-permute-start(bf16[128,512]{1,0:T(8,128)(2,1)S(1)} %gather.1), channel_id=1, source_target_pairs={{0,0},{1,1},{2,8},{3,9},{4,16},{5,17},{6,24},{7,25},{8,2},{9,3},{1... | collective-permute-start | bytes 393224 | tf_op jit(solution)/shard_map/ppermute | solution.py:228
  3.2 13.9 %collective-permute-start.1 = (bf16[128,512]{1,0:T(8,128)(2,1)S(1)}, bf16[128,512]{1,0:T(8,128)(2,1)S(1)}, u32[]{:S(2)}, u32[]{:S(2)}) collective-permute-start(bf16[128,512]{1,0:T(8,128)(2,1)S(1)} %gather.1), channel_id=1, source_target_pairs={{0,2},{1,3},{2,10},{3,11},{4,18},{5,19},{6,26},{7,27},{8,4},{9,5},... | collective-permute-start | bytes 393224 | tf_op jit(solution)/shard_map/ppermute | solution.py:228
  8.9 9.0 %collective-permute-start.2 = (bf16[128,512]{1,0:T(8,128)(2,1)S(1)}, bf16[128,512]{1,0:T(8,128)(2,1)S(1)}, u32[]{:S(2)}, u32[]{:S(2)}) collective-permute-start(bf16[128,512]{1,0:T(8,128)(2,1)S(1)} %gather.1), channel_id=1, source_target_pairs={{0,4},{1,5},{2,12},{3,13},{4,20},{5,21},{6,28},{7,29},{8,6},{9,7},... | collective-permute-start | bytes 393224 | tf_op jit(solution)/shard_map/ppermute | solution.py:228
  12.4 7.1 %collective-permute-start.3 = (bf16[128,512]{1,0:T(8,128)(2,1)S(1)}, bf16[128,512]{1,0:T(8,128)(2,1)S(1)}, u32[]{:S(2)}, u32[]{:S(2)}) collective-permute-start(bf16[128,512]{1,0:T(8,128)(2,1)S(1)} %gather.1), channel_id=1, source_target_pairs={{0,6},{1,7},{2,14},{3,15},{4,22},{5,23},{6,30},{7,31},{8,0},{9,1},... | collective-permute-start | bytes 393224 | tf_op jit(solution)/shard_map/ppermute | solution.py:228
  14.7 4.8 %collective-permute-start.4 = (bf16[128,512]{1,0:T(8,128)(2,1)S(1)}, bf16[128,512]{1,0:T(8,128)(2,1)S(1)}, u32[]{:S(2)}, u32[]{:S(2)}) collective-permute-start(bf16[128,512]{1,0:T(8,128)(2,1)S(1)} %collective-permute-done.refs_0_), channel_id=1, source_target_pairs={{1,0},{0,1},{3,2},{2,3},{5,4},{4,5},{7,6},{6,7},{9,8},{8,9},{11,10... | collective-permute-start | bytes 393224 | tf_op jit(solution)/shard_map/ppermute | solution.py:238
  17.1 2.4 %collective-permute-start.5 = (bf16[128,512]{1,0:T(8,128)(2,1)S(1)}, bf16[128,512]{1,0:T(8,128)(2,1)S(1)}, u32[]{:S(2)}, u32[]{:S(2)}) collective-permute-start(bf16[128,512]{1,0:T(8,128)(2,1)S(1)} %collective-permute-done.1.refs_1_), channel_id=1, source_target_pairs={{1,0},{0,1},{3,2},{2,3},{5,4},{4,5},{7,6},{6,7},{9,8},{8,9},{11,10... | collective-permute-start | bytes 393224 | tf_op jit(solution)/shard_map/ppermute | solution.py:238
  17.9 1.6 %collective-permute-start.6 = (bf16[128,512]{1,0:T(8,128)(2,1)S(1)}, bf16[128,512]{1,0:T(8,128)(2,1)S(1)}, u32[]{:S(2)}, u32[]{:S(2)}) collective-permute-start(bf16[128,512]{1,0:T(8,128)(2,1)S(1)} %collective-permute-done.2.refs_2_), channel_id=1, source_target_pairs={{1,0},{0,1},{3,2},{2,3},{5,4},{4,5},{7,6},{6,7},{9,8},{8,9},{11,10... | collective-permute-start | bytes 393224 | tf_op jit(solution)/shard_map/ppermute | solution.py:238
  19.5 1.3 %collective-permute-start.7 = (bf16[128,512]{1,0:T(8,128)(2,1)S(1)}, bf16[128,512]{1,0:T(8,128)(2,1)S(1)}, u32[]{:S(2)}, u32[]{:S(2)}) collective-permute-start(bf16[128,512]{1,0:T(8,128)(2,1)S(1)} %collective-permute-done.3.refs_3_), channel_id=1, source_target_pairs={{1,0},{0,1},{3,2},{2,3},{5,4},{4,5},{7,6},{6,7},{9,8},{8,9},{11,10... | collective-permute-start | bytes 393224 | tf_op jit(solution)/shard_map/ppermute | solution.py:238
  20.8 1.4 %copy-start = (bf16[1024,3,256]{2,0,1:T(8,128)(2,1)S(1)}, bf16[1024,3,256]{2,0,1:T(8,128)(2,1)}, u32[]{:S(2)}) copy-start(bf16[1024,3,256]{2,0,1:T(8,128)(2,1)} %param.5) | copy-start | bytes 4718596
  24.1 11.1 %collective-permute-start.10 = (bf16[640,128]{1,0:T(8,128)(2,1)S(1)}, bf16[640,128]{1,0:T(8,128)(2,1)S(1)}, u32[]{:S(2)}, u32[]{:S(2)}) collective-permute-start(bf16[640,128]{1,0:T(8,128)(2,1)S(1)} %get-tuple-element.14), channel_id=1, source_target_pairs={{0,24},{8,0},{16,8},{24,16},{1,25},{9,1},{17,9},{25,17},{2,26},{10... | collective-permute-start | bytes 491528 | tf_op jit(solution)/shard_map/ppermute | solution.py:259
  26.8 12.0 %collective-permute-start.8 = (bf16[640,128]{1,0:T(8,128)(2,1)S(1)}, bf16[640,128]{1,0:T(8,128)(2,1)S(1)}, u32[]{:S(2)}, u32[]{:S(2)}) collective-permute-start(bf16[640,128]{1,0:T(8,128)(2,1)S(1)} %get-tuple-element.12), channel_id=1, source_target_pairs={{0,8},{8,16},{16,24},{24,0},{1,9},{9,17},{17,25},{25,1},{2,10},{10... | collective-permute-start | bytes 491528 | tf_op jit(solution)/shard_map/ppermute | solution.py:259
  30.2 9.5 %collective-permute-start.9 = (bf16[640,128]{1,0:T(8,128)(2,1)S(1)}, bf16[640,128]{1,0:T(8,128)(2,1)S(1)}, u32[]{:S(2)}, u32[]{:S(2)}) collective-permute-start(bf16[640,128]{1,0:T(8,128)(2,1)S(1)} %get-tuple-element.13), channel_id=1, source_target_pairs={{0,16},{8,24},{16,0},{24,8},{1,17},{9,25},{17,1},{25,9},{2,18},{10... | collective-permute-start | bytes 491528 | tf_op jit(solution)/shard_map/ppermute | solution.py:259
  40.1 3.8 %collective-permute-start.11 = (bf16[64,128]{1,0:T(8,128)(2,1)S(1)}, bf16[64,128]{1,0:T(8,128)(2,1)S(1)}, u32[]{:S(2)}, u32[]{:S(2)}) collective-permute-start(bf16[64,128]{1,0:T(8,128)(2,1)S(1)} %get-tuple-element.15), channel_id=1, source_target_pairs={{0,8},{8,0},{16,24},{24,16},{1,9},{9,1},{17,25},{25,17},{2,10},{10... | collective-permute-start | bytes 49160 | tf_op jit(solution)/shard_map/ppermute | solution.py:271

commit v2 on v1

--- a/solution.py
+++ b/solution.py
@@ -87,99 +87,122 @@
 
 
 VMEM = pl.BlockSpec(memory_space=pltpu.VMEM)
-SMEM = pl.BlockSpec(memory_space=pltpu.SMEM)
-
-
-def gather_kernel(counts_ref, keep_ref, tokens_ref, out_ref):
-    slots = out_ref.shape[0]
-    tok_dev = tokens_ref.shape[0]
-    token = lax.broadcasted_iota(jnp.int32, (tok_dev, slots), 0)
-    pick = (token == keep_ref[...]).astype(jnp.bfloat16)
-    rows = lax.dot_general(
-        pick, tokens_ref[...], (((0,), (0,)), ((), ())), preferred_element_type=jnp.float32
-    )
-    count = counts_ref[0].astype(jnp.float32)
+HBM = pl.BlockSpec(memory_space=pltpu.HBM)
+TOP_BITS = 14
+
+
+def gather(tokens, keep_list, counts):
+    slots = keep_list.shape[0]
+    token = lax.broadcasted_iota(jnp.int32, (tokens.shape[0], slots), 0)
+    pick = (token == keep_list[None, :]).astype(jnp.bfloat16)
+    rows = lax.dot_general(pick, tokens, (((0,), (0,)), ((), ())), preferred_element_type=jnp.float32)
     last = lax.broadcasted_iota(jnp.int32, rows.shape, 0) == slots - 1
-    out_ref[...] = jnp.where(last, count, rows).astype(jnp.bfloat16)
+    return jnp.where(last, counts[0].astype(jnp.float32), rows).astype(jnp.bfloat16)
+
+
+def load_kernel(after_hbm, w_hbm, out_ref, sem):
+    del after_hbm
+    copy = pltpu.make_async_copy(w_hbm, out_ref, sem)
+    copy.start()
+    copy.wait()
 
 
 def project_kernel(shards, group, heads, *refs):
-    total = shards
-    halves = [refs[total * p : total * (p + 1)] for p in range(group)]
-    w_ref = refs[total * group]
-    outs = refs[total * group + 1 :]
+    halves = [refs[shards * p : shards * (p + 1)] for p in range(group)]
+    w_ref = refs[shards * group]
+    outs = refs[shards * group + 1 :]
     slots, width = halves[0][0].shape
     capacity = slots // 2
     kept = capacity * shards
+    stride = core_stride(shards, group)
     tp = lax.axis_index("tp")
     core = lax.rem(tp, group)
     line = lax.div(tp, group)
     me = lax.axis_index("seq")
-    shard = [lax.rem(line - k + shards, shards) for k in range(total)]
-    count = [halves[0][k][slots - 1 : slots, :slots].astype(jnp.float32) for k in range(total)]
+    shard = [lax.rem(line - k - core * stride + 2 * shards, shards) for k in range(shards)]
+    count = [halves[0][k][slots - 1 : slots, :slots].astype(jnp.float32) for k in range(shards)]
     row = lax.broadcasted_iota(jnp.int32, (kept, slots), 0)
     rank = ((row % capacity) * shards + row // capacity).astype(jnp.float32)
     slot = lax.broadcasted_iota(jnp.int32, (kept, slots), 1).astype(jnp.float32)
+    first = rank - slot
     picks = []
-    for k in range(total):
+    for k in range(shards):
         start = jnp.zeros_like(count[k])
-        for j in range(total):
+        for j in range(shards):
             if j != k:
                 start += jnp.where(shard[j] < shard[k], count[j], 0.0)
-        hit = (rank == slot + start) & (slot < count[k])
+        hit = (first == start) & (slot < count[k])
         picks.append(jnp.where(hit, 1.0, 0.0).astype(jnp.bfloat16))
     rows = []
     for p in range(group):
-        total_rows = None
-        for k in range(total):
-            part = jnp.dot(picks[k], halves[p][k][...], preferred_element_type=jnp.float32)
-            total_rows = part if total_rows is None else total_rows + part
-        rows.append(total_rows.astype(jnp.bfloat16))
-
-    def times(kind, head, which):
+        pick = jnp.concatenate([picks[(k + p * stride) % shards] for k in range(shards)], axis=1)
+        block = jnp.concatenate([halves[p][k][...] for k in range(shards)], axis=0)
+        rows.append(jnp.dot(pick, block, preferred_element_type=jnp.float32).astype(jnp.bfloat16))
+    blocks = shards // heads
+    block_rows = kept // blocks
+    total = 2 * kept + block_rows
+    pad = outs[0].shape[0] - total
+    exponents = []
+    for kind, lo in ((1, 0), (2, kept), (0, 2 * kept)):
         acc = None
         for p in range(group):
             where = pl.multiple_of(lax.rem(core + p, group) * width, width)
-            w = w_ref[kind, pl.ds(where, width), head * HD : (head + 1) * HD]
-            part = jnp.dot(which[p], w, preferred_element_type=jnp.float32)
+            part = jnp.dot(
+                rows[p], w_ref[kind, pl.ds(where, width), :], preferred_element_type=jnp.float32
+            )
             acc = part if acc is None else acc + part
-        return acc.astype(jnp.bfloat16)
-
-    blocks = shards // heads
-    block_rows = kept // blocks
-    for head in range(heads):
-        key = times(1, head, rows)
-        value = times(2, head, rows)
-        query = times(0, head, rows)
+        most = jnp.maximum(jnp.max(jnp.abs(acc), axis=0, keepdims=True), 2.0**-100)
+        exponent = jnp.floor(jnp.log2(most)) + 1.0
+        exponents.append(exponent)
+        value = jnp.round(acc * jnp.exp2(TOP_BITS - exponent)).astype(jnp.int32).astype(jnp.int16)
         for k in range(shards):
             dest = lax.rem(me + k, shards)
-            block = lax.div(dest, heads)
+            for head in range(heads):
+                mine = value[:, head * HD : (head + 1) * HD]
+                if kind:
+
+                    @pl.when(lax.rem(dest, heads) == head)
+                    def _(k=k, lo=lo, mine=mine):
+                        outs[k][lo : lo + kept, :] = mine
+                else:
+                    for b in range(blocks):
+
+                        @pl.when(dest == b * heads + head)
+                        def _(k=k, lo=lo, b=b, mine=mine):
+                            outs[k][lo:total, :] = mine[b * block_rows : (b + 1) * block_rows, :]
+
+    index = lax.broadcasted_iota(jnp.int32, (pad, HD), 0)
+    for k in range(shards):
+        dest = lax.rem(me + k, shards)
+        for head in range(heads):
 
             @pl.when(lax.rem(dest, heads) == head)
-            def _(k=k, block=block):
-                outs[k][0:kept, :] = key
-                outs[k][kept : 2 * kept, :] = value
-                for b in range(blocks):
-
-                    @pl.when(block == b)
-                    def _(b=b):
-                        outs[k][2 * kept :, :] = query[b * block_rows : (b + 1) * block_rows, :]
+            def _(k=k, head=head):
+                tail = jnp.zeros((pad, HD), jnp.float32)
+                for i, exponent in enumerate(exponents):
+                    tail = jnp.where(index == i, exponent[:, head * HD : (head + 1) * HD], tail)
+                outs[k][total:, :] = tail.astype(jnp.int32).astype(jnp.int16)
 
 
 def attend_kernel(shards, heads, kept, *refs):
     parts, outs = refs[:shards], refs[shards:]
     capacity = kept // shards
     me = lax.axis_index("seq")
-    block_rows = parts[0].shape[0] - 2 * kept
+    block_rows = kept // (shards // heads)
+    total = 2 * kept + block_rows
     block = lax.div(me, heads)
-
-    def summed(lo, hi):
-        acc = parts[0][lo:hi, :].astype(jnp.float32)
-        for p in parts[1:]:
-            acc += p[lo:hi, :].astype(jnp.float32)
+    scales = [
+        jnp.exp2(p[total:, :].astype(jnp.int32).astype(jnp.float32) - TOP_BITS) for p in parts
+    ]
+
+    def summed(i, lo, hi):
+        acc = None
+        for p, scale in zip(parts, scales):
+            part = p[lo:hi, :].astype(jnp.int32).astype(jnp.float32) * scale[i : i + 1, :]
+            acc = part if acc is None else acc + part
         return acc.astype(jnp.bfloat16)
 
-    key, value, query = summed(0, kept), summed(kept, 2 * kept), summed(2 * kept, 2 * kept + block_rows)
+    key, value, query = summed(0, 0, kept), summed(1, kept, 2 * kept), summed(2, 2 * kept, total)
     scores = lax.dot_general(
         query, key, (((1,), (1,)), ((), ())), preferred_element_type=jnp.float32
     ) * (HD ** (-0.5))
@@ -202,33 +225,33 @@
                 outs[k][...] = result[o * capacity : (o + 1) * capacity, :]
 
 
+def core_stride(shards, group):
+    return shards // group if shards % group == 0 else 0
+
+
 def by_features(shards, tp, tokens, w_qkv, keep_list, counts):
     group = tp // shards
     slots = keep_list.shape[0]
     capacity = slots // 2
     kept = capacity * shards
-    width = tokens.shape[1]
     heads = w_qkv.shape[2] // HD
     blocks = shards // heads
     params = pltpu.CompilerParams(vmem_limit_bytes=32 * 1024 * 1024)
-    packed = pl.pallas_call(
-        gather_kernel,
-        out_shape=jax.ShapeDtypeStruct((slots, width), jnp.bfloat16),
-        in_specs=[SMEM, VMEM, VMEM],
-        out_specs=VMEM,
-        compiler_params=params,
-        name="gather",
-    )(counts, keep_list.reshape(1, slots), tokens)
+    packed = gather(tokens, keep_list, counts)
 
     def device(s, line, core):
         return s * tp + line * group + core
 
+    stride = core_stride(shards, group)
     every = [(s, line, c) for s in range(shards) for line in range(shards) for c in range(group)]
     own = [
         lax.ppermute(
             packed,
             ("seq", "tp"),
-            [(device(s, line, c), device(line, (s + k) % shards, c)) for s, line, c in every],
+            [
+                (device(s, line, c), device(line, (s + k + c * stride) % shards, c))
+                for s, line, c in every
+            ],
         )
         for k in range(shards)
     ]
@@ -246,15 +269,25 @@
             )
             for chunk in own
         ]
-    payload = 2 * kept + kept // blocks
+    weights = jnp.transpose(w_qkv, (1, 0, 2))
+    weights = pl.pallas_call(
+        load_kernel,
+        out_shape=jax.ShapeDtypeStruct(weights.shape, weights.dtype),
+        in_specs=[pl.BlockSpec(memory_space=pl.ANY), HBM],
+        out_specs=VMEM,
+        scratch_shapes=[pltpu.SemaphoreType.DMA],
+        compiler_params=pltpu.CompilerParams(vmem_limit_bytes=51 * 1024 * 1024),
+        name="load",
+    )(own[0], weights)
+    payload = 2 * kept + kept // blocks + 16
     partial = pl.pallas_call(
         functools.partial(project_kernel, shards, group, heads),
-        out_shape=[jax.ShapeDtypeStruct((payload, HD), jnp.bfloat16)] * shards,
+        out_shape=[jax.ShapeDtypeStruct((payload, HD), jnp.int16)] * shards,
         in_specs=[VMEM] * (shards * group + 1),
         out_specs=[VMEM] * shards,
         compiler_params=params,
         name="project",
-    )(*halves, jnp.transpose(w_qkv, (1, 0, 2)))
+    )(*halves, weights)
     parts = [partial[0]] + [
         lax.ppermute(partial[k], "seq", [(s, (s + k) % shards) for s in range(shards)])
         for k in range(1, shards)

time: 44.7 us -> 43 us (0.962)
  local copies, waits for them, and re-layouts: 3.01 us -> 0.26 us
  waiting for transfers between devices: 16.8 us -> 14.8 us
  Pallas kernels: 2.45 us -> 3.88 us
  matrix products: 0 us -> 0.88 us
  starting transfers between devices: 20.9 us -> 21.6 us
    unnamed x6 -> x2, local copies, waits for them, and re-layouts: 3.01 us -> 0.26 us
    ppermute x4, starting transfers between devices: 12.2 us -> 14.2 us  [by_features(): lax.ppermute(packed, ('seq', 'tp'), [(device(s, line, c), device(line, (s...]
    ppermute x3, starting transfers between devices: 7.49 us -> 6.15 us  [by_features(): lax.ppermute(partial[k], 'seq', [(s, (s + k) % shards) for s in range(sha...]
    ppermute x4, waiting for transfers between devices: 1.33 us -> 0.01 us  [by_features(): lax.ppermute(chunk, 'tp', [(line * group + (c + p) % group, line * group...]
    pallas_call x1, Pallas kernels: 0.21 us -> 1.42 us  [by_features(): pl.pallas_call(load_kernel, out_shape=jax.ShapeDtypeStruct(weights.shape,...]
    ppermute x4, waiting for transfers between devices: 4.76 us -> 3.73 us  [by_features(): lax.ppermute(packed, ('seq', 'tp'), [(device(s, line, c), device(line, (s...]
    dot_general x0 -> x1, matrix products: none -> 0.88 us  [gather(): lax.dot_general(pick, tokens, (((0,), (0,)), ((), ())), preferred_element...]
    ppermute x4, starting transfers between devices: 0.01 us -> 0.51 us  [by_features(): lax.ppermute(chunk, 'tp', [(line * group + (c + p) % group, line * group...]
  transfers between devices with their start and end apart: 12 -> 12, of which waited for: 8 -> 6; matrix products, arithmetic and copies ran while one was open for 0% -> 0% of each run, Pallas kernels for 0% -> 3%
where the time goes in v2:
time: 43 us; the launch traced here: 42.8 us
  starting transfers between devices  21.6 us (50%)
  waiting for transfers between devices  14.8 us (34%)
  Pallas kernels  3.88 us (9%)
  matrix products  0.88 us (2%)
  between operations  0.79 us (2%)
  other arithmetic  0.63 us (1%)
    ppermute x4, starting transfers between devices, by_features(): lax.ppermute(packed, ('seq', 'tp'), [(device(s, line, c), device(line, (s...  14.2 us
    ppermute x3, waiting for transfers between devices, by_features(): lax.ppermute(partial[k], 'seq', [(s, (s + k) % shards) for s in range(sha...  7.99 us
    ppermute x3, starting transfers between devices, by_features(): lax.ppermute(partial[k], 'seq', [(s, (s + k) % shards) for s in range(sha...  6.15 us
    ppermute x4, waiting for transfers between devices, by_features(): lax.ppermute(packed, ('seq', 'tp'), [(device(s, line, c), device(line, (s...  3.73 us
    ppermute x1, waiting for transfers between devices, by_features(): lax.ppermute(pieces[k], 'seq', [(b * heads + h, b * heads + (h + k) % hea...  3.03 us
    pallas_call x1, Pallas kernels, by_features(): pl.pallas_call(functools.partial(project_kernel, shards, group, heads), o...  2.02 us
    pallas_call x1, Pallas kernels, by_features(): pl.pallas_call(load_kernel, out_shape=jax.ShapeDtypeStruct(weights.shape,...  1.42 us
    dot_general x1, matrix products, gather(): lax.dot_general(pick, tokens, (((0,), (0,)), ((), ())), preferred_element...  0.88 us
  transfers between devices with their start and end apart: 12, of which 6 were waited for; matrix products, arithmetic and copies ran while one was open for 0% of the time, Pallas kernels for 3%

profile of v2, /device:TPU:0, one launch (start us, length us, event | category | flops | bytes accessed | tf_op | source)
XLA Modules:
  0.0 42.8 jit_solution(4867134614233307633)
XLA Ops:
  0.0 0.0 copy-start
  0.7 0.3 copy-done
  1.0 0.9 %fusion = bf16[128,512]{1,0:T(8,128)(2,1)S(1)} fusion(bf16[256,512]{1,0:T(8,128)(2,1)S(1)} %copy-done, bf16[]{:T(256)} %bitcast, pred[128]{0:T(512)(128)(4,1)S(1)} %iota_compare_fusion.2, s32[128]{0:T(128)} %param.6), kind=kOutput, calls=%fused_computation.1 | convolution fusion | flops 33652736 | bytes 393858 | tf_op jit(solution)/shard_map/dot_general | solution.py:98
  1.9 0.7 %collective-permute-start = (bf16[128,512]{1,0:T(8,128)(2,1)S(1)}, bf16[128,512]{1,0:T(8,128)(2,1)S(1)}, u32[]{:S(2)}, u32[]{:S(2)}) collective-permute-start(bf16[128,512]{1,0:T(8,128)(2,1)S(1)} %fusion), channel_id=1, source_target_pairs={{0,0},{1,5},{2,8},{3,13},{4,16},{5,21},{6,24},{7,29},{8,2},{9,7},{... | collective-permute-start | bytes 393224 | tf_op jit(solution)/shard_map/ppermute | solution.py:248
  2.5 5.7 %collective-permute-start.1 = (bf16[128,512]{1,0:T(8,128)(2,1)S(1)}, bf16[128,512]{1,0:T(8,128)(2,1)S(1)}, u32[]{:S(2)}, u32[]{:S(2)}) collective-permute-start(bf16[128,512]{1,0:T(8,128)(2,1)S(1)} %fusion), channel_id=1, source_target_pairs={{0,2},{1,7},{2,10},{3,15},{4,18},{5,23},{6,26},{7,31},{8,4},{9,1},... | collective-permute-start | bytes 393224 | tf_op jit(solution)/shard_map/ppermute | solution.py:248
  8.3 5.4 %collective-permute-start.2 = (bf16[128,512]{1,0:T(8,128)(2,1)S(1)}, bf16[128,512]{1,0:T(8,128)(2,1)S(1)}, u32[]{:S(2)}, u32[]{:S(2)}) collective-permute-start(bf16[128,512]{1,0:T(8,128)(2,1)S(1)} %fusion), channel_id=1, source_target_pairs={{0,4},{1,1},{2,12},{3,9},{4,20},{5,17},{6,28},{7,25},{8,6},{9,3},{... | collective-permute-start | bytes 393224 | tf_op jit(solution)/shard_map/ppermute | solution.py:248
  13.6 2.4 %collective-permute-start.3 = (bf16[128,512]{1,0:T(8,128)(2,1)S(1)}, bf16[128,512]{1,0:T(8,128)(2,1)S(1)}, u32[]{:S(2)}, u32[]{:S(2)}) collective-permute-start(bf16[128,512]{1,0:T(8,128)(2,1)S(1)} %fusion), channel_id=1, source_target_pairs={{0,6},{1,3},{2,14},{3,11},{4,22},{5,19},{6,30},{7,27},{8,0},{9,5},... | collective-permute-start | bytes 393224 | tf_op jit(solution)/shard_map/ppermute | solution.py:248
  16.0 0.0 collective-permute-done.after_hbm.refs_0_
  16.0 0.0 collective-permute-start.4
  16.0 0.0 collective-permute-done.1.refs_1_
  16.0 0.5 %collective-permute-start.5 = (bf16[128,512]{1,0:T(8,128)(2,1)S(1)}, bf16[128,512]{1,0:T(8,128)(2,1)S(1)}, u32[]{:S(2)}, u32[]{:S(2)}) collective-permute-start(bf16[128,512]{1,0:T(8,128)(2,1)S(1)} %collective-permute-done.1.refs_1_), channel_id=1, source_target_pairs={{1,0},{0,1},{3,2},{2,3},{5,4},{4,5},{7,6},{6,7},{9,8},{8,9},{11,10... | collective-permute-start | bytes 393224 | tf_op jit(solution)/shard_map/ppermute | solution.py:261
  16.6 2.1 %collective-permute-done.2.refs_2_ = bf16[128,512]{1,0:T(8,128)(2,1)S(1)} collective-permute-done((bf16[128,512]{1,0:T(8,128)(2,1)S(1)}, bf16[128,512]{1,0:T(8,128)(2,1)S(1)}, u32[]{:S(2)}, u32[]{:S(2)}) %collective-permute-start.2) | collective-permute-done | bytes 131104 | tf_op jit(solution)/shard_map/ppermute | solution.py:248
  18.7 0.0 collective-permute-start.6
  18.7 1.6 %collective-permute-done.3.refs_3_ = bf16[128,512]{1,0:T(8,128)(2,1)S(1)} collective-permute-done((bf16[128,512]{1,0:T(8,128)(2,1)S(1)}, bf16[128,512]{1,0:T(8,128)(2,1)S(1)}, u32[]{:S(2)}, u32[]{:S(2)}) %collective-permute-start.3) | collective-permute-done | bytes 131104 | tf_op jit(solution)/shard_map/ppermute | solution.py:248
  20.3 0.0 collective-permute-start.7
  20.3 1.4 %load.1.refs_8_ = bf16[3,1024,256]{2,1,0:T(8,128)(2,1)S(1)} custom-call(bf16[128,512]{1,0:T(8,128)(2,1)S(1)} %collective-permute-done.after_hbm.refs_0_, bf16[3,1024,256]{2,1,0:T(8,128)(2,1)} %bitcast.3), custom_call_target="tpu_custom_call" | custom-call | tf_op jit(solution)/shard_map/load/pallas_call | solution.py:273
  21.7 0.0 collective-permute-done.4.refs_4_
  21.7 0.0 collective-permute-done.5.refs_5_
  21.7 0.0 collective-permute-done.6.refs_6_
  21.7 0.0 collective-permute-done.7.refs_7_
  21.8 2.0 %project.1 = (s16[656,128]{1,0:T(8,128)(2,1)S(1)}, s16[656,128]{1,0:T(8,128)(2,1)S(1)}, s16[656,128]{1,0:T(8,128)(2,1)S(1)}, s16[656,128]{1,0:T(8,128)(2,1)S(1)}) custom-call(bf16[128,512]{1,0:T(8,128)(2,1)S(1)} %collective-permute-done.after_hbm.refs_0_, bf16[128,512]{1,0:T(8,128)(2,1)S(1)} %collective-permute-done.1.refs_1_, ...), custom_call_target="tpu_custom_call" | custom-call | tf_op jit(solution)/shard_map/project/pallas_call | solution.py:283
  23.8 2.4 %collective-permute-start.10 = (s16[656,128]{1,0:T(8,128)(2,1)S(1)}, s16[656,128]{1,0:T(8,128)(2,1)S(1)}, u32[]{:S(2)}, u32[]{:S(2)}) collective-permute-start(s16[656,128]{1,0:T(8,128)(2,1)S(1)} %get-tuple-element.14), channel_id=1, source_target_pairs={{0,24},{8,0},{16,8},{24,16},{1,25},{9,1},{17,9},{25,17},{2,26},{10... | collective-permute-start | bytes 503816 | tf_op jit(solution)/shard_map/ppermute | solution.py:292
  26.1 1.4 %collective-permute-start.8 = (s16[656,128]{1,0:T(8,128)(2,1)S(1)}, s16[656,128]{1,0:T(8,128)(2,1)S(1)}, u32[]{:S(2)}, u32[]{:S(2)}) collective-permute-start(s16[656,128]{1,0:T(8,128)(2,1)S(1)} %get-tuple-element.12), channel_id=1, source_target_pairs={{0,8},{8,16},{16,24},{24,0},{1,9},{9,17},{17,25},{25,1},{2,10},{10... | collective-permute-start | bytes 503816 | tf_op jit(solution)/shard_map/ppermute | solution.py:292
  27.5 2.4 %collective-permute-start.9 = (s16[656,128]{1,0:T(8,128)(2,1)S(1)}, s16[656,128]{1,0:T(8,128)(2,1)S(1)}, u32[]{:S(2)}, u32[]{:S(2)}) collective-permute-start(s16[656,128]{1,0:T(8,128)(2,1)S(1)} %get-tuple-element.13), channel_id=1, source_target_pairs={{0,16},{8,24},{16,0},{24,8},{1,17},{9,25},{17,1},{25,9},{2,18},{10... | collective-permute-start | bytes 503816 | tf_op jit(solution)/shard_map/ppermute | solution.py:292
  29.9 2.6 %collective-permute-done.10.refs_3_ = s16[656,128]{1,0:T(8,128)(2,1)S(1)} collective-permute-done((s16[656,128]{1,0:T(8,128)(2,1)S(1)}, s16[656,128]{1,0:T(8,128)(2,1)S(1)}, u32[]{:S(2)}, u32[]{:S(2)}) %collective-permute-start.10) | collective-permute-done | bytes 167968 | tf_op jit(solution)/shard_map/ppermute | solution.py:292
  32.6 5.2 %collective-permute-done.8.refs_1_ = s16[656,128]{1,0:T(8,128)(2,1)S(1)} collective-permute-done((s16[656,128]{1,0:T(8,128)(2,1)S(1)}, s16[656,128]{1,0:T(8,128)(2,1)S(1)}, u32[]{:S(2)}, u32[]{:S(2)}) %collective-permute-start.8) | collective-permute-done | bytes 167968 | tf_op jit(solution)/shard_map/ppermute | solution.py:292
  37.7 0.2 collective-permute-done.9.refs_2_
  37.9 0.4 %attend.1 = (bf16[64,128]{1,0:T(8,128)(2,1)S(1)}, bf16[64,128]{1,0:T(8,128)(2,1)S(1)}) custom-call(s16[656,128]{1,0:T(8,128)(2,1)S(1)} %get-tuple-element.11.refs_0_, s16[656,128]{1,0:T(8,128)(2,1)S(1)} %collective-permute-done.8.refs_1_, s16[656,128]{1,0:T(8,128)(2,1)S(1)} %collective-permute-done.9.refs_2_, s16[656,128]{1,0:T(8,128)(2,1)S(1)} %collective-permute-done.10.refs_3_), custom_call_target="tpu_custom_call" | custom-call | tf_op jit(solution)/shard_map/attend/pallas_call | solution.py:295
  38.4 0.8 %collective-permute-start.11 = (bf16[64,128]{1,0:T(8,128)(2,1)S(1)}, bf16[64,128]{1,0:T(8,128)(2,1)S(1)}, u32[]{:S(2)}, u32[]{:S(2)}) collective-permute-start(bf16[64,128]{1,0:T(8,128)(2,1)S(1)} %get-tuple-element.15), channel_id=1, source_target_pairs={{0,8},{8,0},{16,24},{24,16},{1,9},{9,1},{17,25},{25,17},{2,10},{10... | collective-permute-start | bytes 49160 | tf_op jit(solution)/shard_map/ppermute | solution.py:304
  39.1 3.0 %collective-permute-done.11 = bf16[64,128]{1,0:T(8,128)(2,1)S(1)} collective-permute-done((bf16[64,128]{1,0:T(8,128)(2,1)S(1)}, bf16[64,128]{1,0:T(8,128)(2,1)S(1)}, u32[]{:S(2)}, u32[]{:S(2)}) %collective-permute-start.11) | collective-permute-done | bytes 16416 | tf_op jit(solution)/shard_map/ppermute | solution.py:304
  42.2 0.6 %pad_maximum_fusion = bf16[64,256]{1,0:T(8,128)(2,1)} fusion(bf16[64,128]{1,0:T(8,128)(2,1)S(1)} %get-tuple-element.18, bf16[64,128]{1,0:T(8,128)(2,1)S(1)} %get-tuple-element.17), kind=kLoop, calls=%fused_computation.4 | loop fusion | flops 65536 | bytes 65536 | tf_op jit(solution)/shard_map/concatenate | solution.py:318
  (2 shorter events, 0.0 us)
Async XLA Ops:
  0.0 1.0 %copy-start = (bf16[256,512]{1,0:T(8,128)(2,1)S(1)}, bf16[256,512]{1,0:T(8,128)(2,1)}, u32[]{:S(2)}) copy-start(bf16[256,512]{1,0:T(8,128)(2,1)} %param.4) | copy-start | bytes 786436
  1.9 14.2 %collective-permute-start = (bf16[128,512]{1,0:T(8,128)(2,1)S(1)}, bf16[128,512]{1,0:T(8,128)(2,1)S(1)}, u32[]{:S(2)}, u32[]{:S(2)}) collective-permute-start(bf16[128,512]{1,0:T(8,128)(2,1)S(1)} %fusion), channel_id=1, source_target_pairs={{0,0},{1,5},{2,8},{3,13},{4,16},{5,21},{6,24},{7,29},{8,2},{9,7},{... | collective-permute-start | bytes 393224 | tf_op jit(solution)/shard_map/ppermute | solution.py:248
  2.5 13.5 %collective-permute-start.1 = (bf16[128,512]{1,0:T(8,128)(2,1)S(1)}, bf16[128,512]{1,0:T(8,128)(2,1)S(1)}, u32[]{:S(2)}, u32[]{:S(2)}) collective-permute-start(bf16[128,512]{1,0:T(8,128)(2,1)S(1)} %fusion), channel_id=1, source_target_pairs={{0,2},{1,7},{2,10},{3,15},{4,18},{5,23},{6,26},{7,31},{8,4},{9,1},... | collective-permute-start | bytes 393224 | tf_op jit(solution)/shard_map/ppermute | solution.py:248
  8.3 10.4 %collective-permute-start.2 = (bf16[128,512]{1,0:T(8,128)(2,1)S(1)}, bf16[128,512]{1,0:T(8,128)(2,1)S(1)}, u32[]{:S(2)}, u32[]{:S(2)}) collective-permute-start(bf16[128,512]{1,0:T(8,128)(2,1)S(1)} %fusion), channel_id=1, source_target_pairs={{0,4},{1,1},{2,12},{3,9},{4,20},{5,17},{6,28},{7,25},{8,6},{9,3},{... | collective-permute-start | bytes 393224 | tf_op jit(solution)/shard_map/ppermute | solution.py:248
  13.6 6.6 %collective-permute-start.3 = (bf16[128,512]{1,0:T(8,128)(2,1)S(1)}, bf16[128,512]{1,0:T(8,128)(2,1)S(1)}, u32[]{:S(2)}, u32[]{:S(2)}) collective-permute-start(bf16[128,512]{1,0:T(8,128)(2,1)S(1)} %fusion), channel_id=1, source_target_pairs={{0,6},{1,3},{2,14},{3,11},{4,22},{5,19},{6,30},{7,27},{8,0},{9,5},... | collective-permute-start | bytes 393224 | tf_op jit(solution)/shard_map/ppermute | solution.py:248
  16.0 5.7 %collective-permute-start.4 = (bf16[128,512]{1,0:T(8,128)(2,1)S(1)}, bf16[128,512]{1,0:T(8,128)(2,1)S(1)}, u32[]{:S(2)}, u32[]{:S(2)}) collective-permute-start(bf16[128,512]{1,0:T(8,128)(2,1)S(1)} %collective-permute-done.after_hbm.refs_0_), channel_id=1, source_target_pairs={{1,0},{0,1},{3,2},{2,3},{5,4},{4,5},{7,6},{6,7},{9,8},{8,9},{11,10... | collective-permute-start | bytes 393224 | tf_op jit(solution)/shard_map/ppermute | solution.py:261
  16.0 5.7 %collective-permute-start.5 = (bf16[128,512]{1,0:T(8,128)(2,1)S(1)}, bf16[128,512]{1,0:T(8,128)(2,1)S(1)}, u32[]{:S(2)}, u32[]{:S(2)}) collective-permute-start(bf16[128,512]{1,0:T(8,128)(2,1)S(1)} %collective-permute-done.1.refs_1_), channel_id=1, source_target_pairs={{1,0},{0,1},{3,2},{2,3},{5,4},{4,5},{7,6},{6,7},{9,8},{8,9},{11,10... | collective-permute-start | bytes 393224 | tf_op jit(solution)/shard_map/ppermute | solution.py:261
  18.7 3.1 %collective-permute-start.6 = (bf16[128,512]{1,0:T(8,128)(2,1)S(1)}, bf16[128,512]{1,0:T(8,128)(2,1)S(1)}, u32[]{:S(2)}, u32[]{:S(2)}) collective-permute-start(bf16[128,512]{1,0:T(8,128)(2,1)S(1)} %collective-permute-done.2.refs_2_), channel_id=1, source_target_pairs={{1,0},{0,1},{3,2},{2,3},{5,4},{4,5},{7,6},{6,7},{9,8},{8,9},{11,10... | collective-permute-start | bytes 393224 | tf_op jit(solution)/shard_map/ppermute | solution.py:261
  20.3 1.5 %collective-permute-start.7 = (bf16[128,512]{1,0:T(8,128)(2,1)S(1)}, bf16[128,512]{1,0:T(8,128)(2,1)S(1)}, u32[]{:S(2)}, u32[]{:S(2)}) collective-permute-start(bf16[128,512]{1,0:T(8,128)(2,1)S(1)} %collective-permute-done.3.refs_3_), channel_id=1, source_target_pairs={{1,0},{0,1},{3,2},{2,3},{5,4},{4,5},{7,6},{6,7},{9,8},{8,9},{11,10... | collective-permute-start | bytes 393224 | tf_op jit(solution)/shard_map/ppermute | solution.py:261
  23.8 8.8 %collective-permute-start.10 = (s16[656,128]{1,0:T(8,128)(2,1)S(1)}, s16[656,128]{1,0:T(8,128)(2,1)S(1)}, u32[]{:S(2)}, u32[]{:S(2)}) collective-permute-start(s16[656,128]{1,0:T(8,128)(2,1)S(1)} %get-tuple-element.14), channel_id=1, source_target_pairs={{0,24},{8,0},{16,8},{24,16},{1,25},{9,1},{17,9},{25,17},{2,26},{10... | collective-permute-start | bytes 503816 | tf_op jit(solution)/shard_map/ppermute | solution.py:292
  26.1 11.6 %collective-permute-start.8 = (s16[656,128]{1,0:T(8,128)(2,1)S(1)}, s16[656,128]{1,0:T(8,128)(2,1)S(1)}, u32[]{:S(2)}, u32[]{:S(2)}) collective-permute-start(s16[656,128]{1,0:T(8,128)(2,1)S(1)} %get-tuple-element.12), channel_id=1, source_target_pairs={{0,8},{8,16},{16,24},{24,0},{1,9},{9,17},{17,25},{25,1},{2,10},{10... | collective-permute-start | bytes 503816 | tf_op jit(solution)/shard_map/ppermute | solution.py:292
  27.5 10.4 %collective-permute-start.9 = (s16[656,128]{1,0:T(8,128)(2,1)S(1)}, s16[656,128]{1,0:T(8,128)(2,1)S(1)}, u32[]{:S(2)}, u32[]{:S(2)}) collective-permute-start(s16[656,128]{1,0:T(8,128)(2,1)S(1)} %get-tuple-element.13), channel_id=1, source_target_pairs={{0,16},{8,24},{16,0},{24,8},{1,17},{9,25},{17,1},{25,9},{2,18},{10... | collective-permute-start | bytes 503816 | tf_op jit(solution)/shard_map/ppermute | solution.py:292
  38.4 3.8 %collective-permute-start.11 = (bf16[64,128]{1,0:T(8,128)(2,1)S(1)}, bf16[64,128]{1,0:T(8,128)(2,1)S(1)}, u32[]{:S(2)}, u32[]{:S(2)}) collective-permute-start(bf16[64,128]{1,0:T(8,128)(2,1)S(1)} %get-tuple-element.15), channel_id=1, source_target_pairs={{0,8},{8,0},{16,24},{24,16},{1,9},{9,1},{17,25},{25,17},{2,10},{10... | collective-permute-start | bytes 49160 | tf_op jit(solution)/shard_map/ppermute | solution.py:304

commit v3 on v0

--- a/solution.py
+++ b/solution.py
@@ -1,6 +1,10 @@
+import functools
+
 import jax
 import jax.numpy as jnp
 from jax import lax
+from jax.experimental import pallas as pl
+from jax.experimental.pallas import tpu as pltpu
 from jax.sharding import PartitionSpec as P
 
 HD = 128
@@ -22,7 +26,7 @@
     return earlier + later
 
 
-def on_device(tokens, w_qkv, keep_list, counts):
+def by_rows(tokens, w_qkv, keep_list, counts):
     shards = lax.axis_size("seq")
     my_index = lax.axis_index("seq")
     tok_dev = tokens.shape[0]
@@ -82,7 +86,298 @@
     return jnp.transpose(result, (1, 0, 2)).reshape(capacity, columns).astype(jnp.bfloat16)
 
 
+VMEM = pl.BlockSpec(memory_space=pltpu.VMEM)
+HBM = pl.BlockSpec(memory_space=pltpu.HBM)
+TOP_BITS = 14
+
+
+def gather(tokens, keep_list, counts):
+    slots = keep_list.shape[0]
+    token = lax.broadcasted_iota(jnp.int32, (tokens.shape[0], slots), 0)
+    pick = (token == keep_list[None, :]).astype(jnp.bfloat16)
+    rows = lax.dot_general(pick, tokens, (((0,), (0,)), ((), ())), preferred_element_type=jnp.float32)
+    last = lax.broadcasted_iota(jnp.int32, rows.shape, 0) == slots - 1
+    return jnp.where(last, counts[0].astype(jnp.float32), rows).astype(jnp.bfloat16)
+
+
+def load_kernel(w_hbm, out_ref, sem):
+    copy = pltpu.make_async_copy(w_hbm, out_ref, sem)
+    copy.start()
+    copy.wait()
+
+
+def core_stride(shards, group):
+    return shards // group if shards % group == 0 else 0
+
+
+def partner(me, k, shards):
+    return me ^ k if shards & (shards - 1) == 0 else (me + k) % shards
+
+
+def sender(me, k, shards):
+    return me ^ k if shards & (shards - 1) == 0 else (me - k + shards) % shards
+
+
+def keeper(core, head, shards, heads):
+    ends = [i // 2 if i % 2 == 0 else shards - 1 - i // 2 for i in range(shards)]
+    return ends[(core * heads + head) % shards]
+
+
+def chosen(index, options):
+    value = jnp.int32(options[-1])
+    for i, option in enumerate(options[:-1]):
+        value = jnp.where(index == i, jnp.int32(option), value)
+    return value
+
+
+def own_kernel(shards, group, *refs):
+    chunks, w_ref, (pick_ref, acc_ref) = refs[:shards], refs[shards], refs[shards + 1 :]
+    slots, width = chunks[0].shape
+    capacity = slots // 2
+    kept = capacity * shards
+    tp = lax.axis_index("tp")
+    core = lax.rem(tp, group)
+    line = lax.div(tp, group)
+    stride = core_stride(shards, group)
+    shard = [lax.rem(line - k - core * stride + 2 * shards, shards) for k in range(shards)]
+    count = [chunks[k][slots - 1 : slots, :slots].astype(jnp.float32) for k in range(shards)]
+    row = lax.broadcasted_iota(jnp.int32, (kept, slots), 0)
+    rank = ((row % capacity) * shards + row // capacity).astype(jnp.float32)
+    slot = lax.broadcasted_iota(jnp.int32, (kept, slots), 1).astype(jnp.float32)
+    first = rank - slot
+    picks = []
+    for k in range(shards):
+        start = jnp.zeros_like(count[k])
+        for j in range(shards):
+            if j != k:
+                start += jnp.where(shard[j] < shard[k], count[j], 0.0)
+        hit = (first == start) & (slot < count[k])
+        picks.append(jnp.where(hit, 1.0, 0.0).astype(jnp.bfloat16))
+        pick_ref[:, k * slots : (k + 1) * slots] = picks[k]
+    rows = jnp.dot(
+        jnp.concatenate(picks, axis=1),
+        jnp.concatenate([chunk[...] for chunk in chunks], axis=0),
+        preferred_element_type=jnp.float32,
+    ).astype(jnp.bfloat16)
+    where = pl.multiple_of(core * width, width)
+    for kind in range(3):
+        acc_ref[kind] = jnp.dot(
+            rows, w_ref[kind, pl.ds(where, width), :], preferred_element_type=jnp.float32
+        )
+
+
+def rest_kernel(shards, group, heads, *refs):
+    count = shards * (group - 1)
+    halves = [refs[shards * p : shards * (p + 1)] for p in range(group - 1)]
+    pick_ref, acc_ref, w_ref = refs[count : count + 3]
+    outs = refs[count + 3 :]
+    slots = pick_ref.shape[1] // shards
+    width = w_ref.shape[1] // group
+    kept = slots // 2 * shards
+    stride = core_stride(shards, group)
+    core = lax.rem(lax.axis_index("tp"), group)
+    me = lax.axis_index("seq")
+    keepers = [
+        chosen(core, [keeper(c, head, shards, heads) for c in range(group)]) for head in range(heads)
+    ]
+    rows = []
+    for p in range(1, group):
+        order = [(k + p * stride) % shards for k in range(shards)]
+        pick = jnp.concatenate([pick_ref[:, o * slots : (o + 1) * slots] for o in order], axis=1)
+        block = jnp.concatenate([half[...] for half in halves[p - 1]], axis=0)
+        rows.append(jnp.dot(pick, block, preferred_element_type=jnp.float32).astype(jnp.bfloat16))
+    total = 3 * kept
+    pad = outs[0].shape[0] - total
+    exponents = []
+    for at, kind in enumerate((1, 2, 0)):
+        acc = acc_ref[kind]
+        for p in range(1, group):
+            where = pl.multiple_of(lax.rem(core + p, group) * width, width)
+            acc += jnp.dot(
+                rows[p - 1], w_ref[kind, pl.ds(where, width), :], preferred_element_type=jnp.float32
+            )
+        most = jnp.maximum(jnp.max(jnp.abs(acc), axis=0, keepdims=True), 2.0**-100)
+        exponent = jnp.floor(jnp.log2(most)) + 1.0
+        exponents.append(exponent)
+        value = jnp.round(acc * jnp.exp2(TOP_BITS - exponent)).astype(jnp.int32).astype(jnp.int16)
+        for k in range(shards):
+            for head in range(heads):
+
+                @pl.when(partner(me, k, shards) == keepers[head])
+                def _(k=k, head=head, at=at, value=value):
+                    outs[k][at * kept : (at + 1) * kept, :] = value[:, head * HD : (head + 1) * HD]
+
+    index = lax.broadcasted_iota(jnp.int32, (pad, HD), 0)
+    for head in range(heads):
+        tail = jnp.zeros((pad, HD), jnp.float32)
+        for at, exponent in enumerate(exponents):
+            tail = jnp.where(index == at, exponent[:, head * HD : (head + 1) * HD], tail)
+        tail = tail.astype(jnp.int32).astype(jnp.int16)
+        for k in range(shards):
+
+            @pl.when(partner(me, k, shards) == keepers[head])
+            def _(k=k, tail=tail):
+                outs[k][total:, :] = tail
+
+
+def attend_kernel(shards, group, heads, *refs):
+    parts, outs, all_ref = refs[:shards], refs[shards : 2 * shards], refs[2 * shards]
+    kept = all_ref.shape[0]
+    capacity = kept // shards
+    me = lax.axis_index("seq")
+    core = lax.rem(lax.axis_index("tp"), group)
+    keeps = me == chosen(core, [keeper(c, 0, shards, heads) for c in range(group)])
+    for head in range(1, heads):
+        keeps |= me == chosen(core, [keeper(c, head, shards, heads) for c in range(group)])
+
+    @pl.when(keeps)
+    def _():
+        scales = [
+            jnp.exp2(p[3 * kept :, :].astype(jnp.int32).astype(jnp.float32) - TOP_BITS)
+            for p in parts
+        ]
+
+        def summed(at):
+            acc = None
+            for p, scale in zip(parts, scales):
+                part = p[at * kept : (at + 1) * kept, :].astype(jnp.int32).astype(jnp.float32)
+                part = part * scale[at : at + 1, :]
+                acc = part if acc is None else acc + part
+            return acc.astype(jnp.bfloat16)
+
+        key, value, query = summed(0), summed(1), summed(2)
+        scores = lax.dot_general(
+            query, key, (((1,), (1,)), ((), ())), preferred_element_type=jnp.float32
+        ) * (HD ** (-0.5))
+        q_row = lax.broadcasted_iota(jnp.int32, scores.shape, 0)
+        k_row = lax.broadcasted_iota(jnp.int32, scores.shape, 1)
+        q_rank = lax.rem(q_row, capacity) * shards + lax.div(q_row, capacity)
+        k_rank = lax.rem(k_row, capacity) * shards + lax.div(k_row, capacity)
+        scores = jnp.where(k_rank > q_rank, -jnp.inf, scores)
+        top = jnp.max(scores, axis=1, keepdims=True)
+        expo = jnp.exp(scores - top)
+        numer = jnp.dot(expo.astype(jnp.bfloat16), value, preferred_element_type=jnp.float32)
+        all_ref[...] = numer / jnp.sum(expo, axis=1, keepdims=True)
+        for k in range(shards):
+            owner = pl.multiple_of(partner(me, k, shards) * capacity, capacity)
+            outs[k][...] = all_ref[pl.ds(owner, capacity), :].astype(jnp.bfloat16)
+
+
+def by_features(shards, tp, tokens, w_qkv, keep_list, counts):
+    group = tp // shards
+    slots = keep_list.shape[0]
+    capacity = slots // 2
+    kept = capacity * shards
+    heads = w_qkv.shape[2] // HD
+    axes = ("seq", "tp")
+    params = pltpu.CompilerParams(vmem_limit_bytes=32 * 1024 * 1024)
+
+    def device(s, line, core):
+        return s * tp + line * group + core
+
+    packed = gather(tokens, keep_list, counts)
+    stride = core_stride(shards, group)
+    every = [(s, line, c) for s in range(shards) for line in range(shards) for c in range(group)]
+    own = []
+    for k in range(shards):
+        pairs = [
+            (device(s, line, c), device(line, (s + k + c * stride) % shards, c))
+            for s, line, c in every
+        ]
+        own.append(lax.ppermute(packed, axes, pairs))
+    others = []
+    for p in range(1, group):
+        pairs = [
+            (line * group + (c + p) % group, line * group + c)
+            for line in range(shards)
+            for c in range(group)
+        ]
+        for k in range(shards):
+            others.append(lax.ppermute(own[k], "tp", pairs))
+    weights = jnp.transpose(w_qkv, (1, 0, 2))
+    weights = pl.pallas_call(
+        load_kernel,
+        out_shape=jax.ShapeDtypeStruct(weights.shape, weights.dtype),
+        in_specs=[HBM],
+        out_specs=VMEM,
+        scratch_shapes=[pltpu.SemaphoreType.DMA],
+        compiler_params=pltpu.CompilerParams(vmem_limit_bytes=51 * 1024 * 1024),
+        name="load",
+    )(weights)
+    pick, acc = pl.pallas_call(
+        functools.partial(own_kernel, shards, group),
+        out_shape=[
+            jax.ShapeDtypeStruct((kept, shards * slots), jnp.bfloat16),
+            jax.ShapeDtypeStruct((3, kept, heads * HD), jnp.float32),
+        ],
+        in_specs=[VMEM] * (shards + 1),
+        out_specs=[VMEM] * 2,
+        compiler_params=params,
+        name="own",
+    )(*own, weights)
+    payload = 3 * kept + 16
+    partial = pl.pallas_call(
+        functools.partial(rest_kernel, shards, group, heads),
+        out_shape=[jax.ShapeDtypeStruct((payload, HD), jnp.int16)] * shards,
+        in_specs=[VMEM] * (shards * (group - 1) + 3),
+        out_specs=[VMEM] * shards,
+        compiler_params=params,
+        name="rest",
+    )(*others, pick, acc, weights)
+    keepers = [[keeper(c, head, shards, heads) for head in range(heads)] for c in range(group)]
+    parts = [partial[0]]
+    for k in range(1, shards):
+        pairs = [
+            (device(sender(d, k, shards), line, c), device(d, line, c))
+            for line in range(shards)
+            for c in range(group)
+            for d in keepers[c]
+        ]
+        parts.append(lax.ppermute(partial[k], axes, pairs))
+    pieces = pl.pallas_call(
+        functools.partial(attend_kernel, shards, group, heads),
+        out_shape=[jax.ShapeDtypeStruct((capacity, HD), jnp.bfloat16)] * shards,
+        in_specs=[VMEM] * shards,
+        out_specs=[VMEM] * shards,
+        scratch_shapes=[pltpu.VMEM((kept, HD), jnp.float32)],
+        compiler_params=params,
+        name="attend",
+    )(*parts)
+    arrived = [pieces[0]]
+    for k in range(1, shards):
+        pairs = [
+            (device(d, line, c), device(partner(d, k, shards), line, c))
+            for line in range(shards)
+            for c in range(group)
+            for d in keepers[c]
+        ]
+        arrived.append(lax.ppermute(pieces[k], axes, pairs))
+    mine = lax.axis_index("seq")
+    core = lax.rem(lax.axis_index("tp"), group)
+    columns = []
+    for head in range(heads):
+        source = chosen(core, [keepers[c][head] for c in range(group)])
+        column = arrived[0]
+        for k in range(1, shards):
+            column = jnp.where(sender(mine, k, shards) == source, arrived[k], column)
+        columns.append(column)
+    return jnp.concatenate(columns, axis=1)
+
+
+def fits(mesh):
+    shards, tp = mesh.shape["seq"], mesh.shape["tp"]
+    return tp % shards == 0 and tp > shards
+
+
 def solution(mesh):
+    shards, tp = mesh.shape["seq"], mesh.shape["tp"]
+
+    def on_device(tokens, w_qkv, keep_list, counts):
+        heads = w_qkv.shape[2] // HD
+        if fits(mesh) and shards >= heads:
+            return by_features(shards, tp, tokens, w_qkv, keep_list, counts)
+        return by_rows(tokens, w_qkv, keep_list, counts)
+
     in_specs = (P("seq", "tp"), P("seq", None, "tp"), P("seq"), P("seq"))
     out_specs = P("seq", "tp")
     return jax.shard_map(

time: 105 us -> 46.7 us (0.44)
  the two profiles are of different devices: /device:TPU:0 before, /device:TPU:1 now
where the time goes in v3:
time: 46.7 us; the launch traced here: 46.3 us
  starting transfers between devices  31.8 us (68%)
  waiting for transfers between devices  8.55 us (18%)
  Pallas kernels  3.39 us (7%)
  matrix products  0.88 us (2%)
  between operations  0.87 us (2%)
  other arithmetic  0.64 us (1%)
    ppermute x4, starting transfers between devices, by_features(): own.append(lax.ppermute(packed, axes, pairs))  10.5 us
    ppermute x3, starting transfers between devices, by_features(): parts.append(lax.ppermute(partial[k], axes, pairs))  10.1 us
    ppermute x4, starting transfers between devices, by_features(): others.append(lax.ppermute(own[k], 'tp', pairs))  7.9 us
    ppermute x3, waiting for transfers between devices, by_features(): arrived.append(lax.ppermute(pieces[k], axes, pairs))  5.91 us
    ppermute x3, starting transfers between devices, by_features(): arrived.append(lax.ppermute(pieces[k], axes, pairs))  3.23 us
    ppermute x3, waiting for transfers between devices, by_features(): parts.append(lax.ppermute(partial[k], axes, pairs))  2.62 us
    pallas_call x1, Pallas kernels, by_features(): pl.pallas_call(load_kernel, out_shape=jax.ShapeDtypeStruct(weights.shape,...  1.42 us
    pallas_call x1, Pallas kernels, by_features(): pl.pallas_call(functools.partial(rest_kernel, shards, group, heads), out_...  1.32 us
  transfers between devices with their start and end apart: 14, of which 4 were waited for; matrix products, arithmetic and copies ran while one was open for 0% of the time, Pallas kernels for 4%

profile of v3, /device:TPU:1, one launch (start us, length us, event | category | flops | bytes accessed | tf_op | source)
XLA Modules:
  0.0 46.3 jit_solution(13957729638666260656)
XLA Ops:
  0.7 0.3 copy-done
  1.0 0.9 %fusion = bf16[128,512]{1,0:T(8,128)(2,1)S(1)} fusion(bf16[256,512]{1,0:T(8,128)(2,1)S(1)} %copy-done, bf16[]{:T(256)} %bitcast, pred[128]{0:T(512)(128)(4,1)S(1)} %iota_compare_fusion.2, s32[128]{0:T(128)} %param.6), kind=kOutput, calls=%fused_computation.1 | convolution fusion | flops 33652736 | bytes 393858 | tf_op jit(solution)/shard_map/dot_general | solution.py:98
  1.9 5.0 %collective-permute-start = (bf16[128,512]{1,0:T(8,128)(2,1)S(1)}, bf16[128,512]{1,0:T(8,128)(2,1)S(1)}, u32[]{:S(2)}, u32[]{:S(2)}) collective-permute-start(bf16[128,512]{1,0:T(8,128)(2,1)S(1)} %fusion), channel_id=1, source_target_pairs={{0,0},{1,5},{2,8},{3,13},{4,16},{5,21},{6,24},{7,29},{8,2},{9,7},{... | collective-permute-start | bytes 393224 | tf_op jit(solution)/shard_map/ppermute | solution.py:287
  6.9 3.1 %collective-permute-start.2 = (bf16[128,512]{1,0:T(8,128)(2,1)S(1)}, bf16[128,512]{1,0:T(8,128)(2,1)S(1)}, u32[]{:S(2)}, u32[]{:S(2)}) collective-permute-start(bf16[128,512]{1,0:T(8,128)(2,1)S(1)} %fusion), channel_id=1, source_target_pairs={{0,2},{1,7},{2,10},{3,15},{4,18},{5,23},{6,26},{7,31},{8,4},{9,1},... | collective-permute-start | bytes 393224 | tf_op jit(solution)/shard_map/ppermute | solution.py:287
  10.0 0.7 %collective-permute-start.4 = (bf16[128,512]{1,0:T(8,128)(2,1)S(1)}, bf16[128,512]{1,0:T(8,128)(2,1)S(1)}, u32[]{:S(2)}, u32[]{:S(2)}) collective-permute-start(bf16[128,512]{1,0:T(8,128)(2,1)S(1)} %fusion), channel_id=1, source_target_pairs={{0,4},{1,1},{2,12},{3,9},{4,20},{5,17},{6,28},{7,25},{8,6},{9,3},{... | collective-permute-start | bytes 393224 | tf_op jit(solution)/shard_map/ppermute | solution.py:287
  10.7 1.7 %collective-permute-start.6 = (bf16[128,512]{1,0:T(8,128)(2,1)S(1)}, bf16[128,512]{1,0:T(8,128)(2,1)S(1)}, u32[]{:S(2)}, u32[]{:S(2)}) collective-permute-start(bf16[128,512]{1,0:T(8,128)(2,1)S(1)} %fusion), channel_id=1, source_target_pairs={{0,6},{1,3},{2,14},{3,11},{4,22},{5,19},{6,30},{7,27},{8,0},{9,5},... | collective-permute-start | bytes 393224 | tf_op jit(solution)/shard_map/ppermute | solution.py:287
  12.4 0.0 collective-permute-done.refs_0_
  12.4 3.7 %collective-permute-start.1 = (bf16[128,512]{1,0:T(8,128)(2,1)S(1)}, bf16[128,512]{1,0:T(8,128)(2,1)S(1)}, u32[]{:S(2)}, u32[]{:S(2)}) collective-permute-start(bf16[128,512]{1,0:T(8,128)(2,1)S(1)} %collective-permute-done.refs_0_), channel_id=1, source_target_pairs={{1,0},{0,1},{3,2},{2,3},{5,4},{4,5},{7,6},{6,7},{9,8},{8,9},{11,10... | collective-permute-start | bytes 393224 | tf_op jit(solution)/shard_map/ppermute | solution.py:296
  16.1 0.0 collective-permute-done.2.refs_1_
  16.1 0.1 collective-permute-start.3
  16.1 0.0 collective-permute-done.4.refs_2_
  16.1 2.5 %collective-permute-start.5 = (bf16[128,512]{1,0:T(8,128)(2,1)S(1)}, bf16[128,512]{1,0:T(8,128)(2,1)S(1)}, u32[]{:S(2)}, u32[]{:S(2)}) collective-permute-start(bf16[128,512]{1,0:T(8,128)(2,1)S(1)} %collective-permute-done.4.refs_2_), channel_id=1, source_target_pairs={{1,0},{0,1},{3,2},{2,3},{5,4},{4,5},{7,6},{6,7},{9,8},{8,9},{11,10... | collective-permute-start | bytes 393224 | tf_op jit(solution)/shard_map/ppermute | solution.py:296
  18.7 0.0 collective-permute-done.6.refs_3_
  18.7 1.6 %collective-permute-start.7 = (bf16[128,512]{1,0:T(8,128)(2,1)S(1)}, bf16[128,512]{1,0:T(8,128)(2,1)S(1)}, u32[]{:S(2)}, u32[]{:S(2)}) collective-permute-start(bf16[128,512]{1,0:T(8,128)(2,1)S(1)} %collective-permute-done.6.refs_3_), channel_id=1, source_target_pairs={{1,0},{0,1},{3,2},{2,3},{5,4},{4,5},{7,6},{6,7},{9,8},{8,9},{11,10... | collective-permute-start | bytes 393224 | tf_op jit(solution)/shard_map/ppermute | solution.py:296
  20.3 1.4 %load.1.refs_4_.refs_6_ = bf16[3,1024,256]{2,1,0:T(8,128)(2,1)S(1)} custom-call(bf16[3,1024,256]{2,1,0:T(8,128)(2,1)} %bitcast.3), custom_call_target="tpu_custom_call" | custom-call | tf_op jit(solution)/shard_map/load/pallas_call | solution.py:298
  21.7 0.7 %own.1 = (bf16[256,512]{1,0:T(8,128)(2,1)S(1)}, f32[3,256,256]{2,1,0:T(8,128)S(1)}) custom-call(bf16[128,512]{1,0:T(8,128)(2,1)S(1)} %collective-permute-done.refs_0_, bf16[128,512]{1,0:T(8,128)(2,1)S(1)} %collective-permute-done.2.refs_1_, bf16[128,512]{1,0:T(8,128)(2,1)S(1)} %collective-permute-done.4.refs_2_, ...), custom_call_target="tpu_custom_call" | custom-call | tf_op jit(solution)/shard_map/own/pallas_call | solution.py:307
  22.4 0.0 collective-permute-done.3.refs_1_
  22.4 0.0 collective-permute-done.5.refs_2_
  22.4 1.3 %rest.1 = (s16[784,128]{1,0:T(8,128)(2,1)S(1)}, s16[784,128]{1,0:T(8,128)(2,1)S(1)}, s16[784,128]{1,0:T(8,128)(2,1)S(1)}, s16[784,128]{1,0:T(8,128)(2,1)S(1)}) custom-call(bf16[128,512]{1,0:T(8,128)(2,1)S(1)} %collective-permute-done.1.refs_0_, bf16[128,512]{1,0:T(8,128)(2,1)S(1)} %collective-permute-done.3.refs_1_, ...), custom_call_target="tpu_custom_call" | custom-call | tf_op jit(solution)/shard_map/rest/pallas_call | solution.py:319
  23.8 0.7 %collective-permute-start.10 = (s16[784,128]{1,0:T(8,128)(2,1)S(1)}, s16[784,128]{1,0:T(8,128)(2,1)S(1)}, u32[]{:S(2)}, u32[]{:S(2)}) collective-permute-start(s16[784,128]{1,0:T(8,128)(2,1)S(1)} %get-tuple-element.20), channel_id=1, source_target_pairs={{24,0},{0,24},{17,9},{9,17},{26,2},{2,26},{19,11},{11,19},{28,4},{... | collective-permute-start | bytes 602120 | tf_op jit(solution)/shard_map/ppermute | solution.py:336
  24.4 8.1 %collective-permute-start.8 = (s16[784,128]{1,0:T(8,128)(2,1)S(1)}, s16[784,128]{1,0:T(8,128)(2,1)S(1)}, u32[]{:S(2)}, u32[]{:S(2)}) collective-permute-start(s16[784,128]{1,0:T(8,128)(2,1)S(1)} %get-tuple-element.18), channel_id=1, source_target_pairs={{8,0},{16,24},{1,9},{25,17},{10,2},{18,26},{3,11},{27,19},{12,4},{... | collective-permute-start | bytes 602120 | tf_op jit(solution)/shard_map/ppermute | solution.py:336
  32.6 1.3 %collective-permute-start.9 = (s16[784,128]{1,0:T(8,128)(2,1)S(1)}, s16[784,128]{1,0:T(8,128)(2,1)S(1)}, u32[]{:S(2)}, u32[]{:S(2)}) collective-permute-start(s16[784,128]{1,0:T(8,128)(2,1)S(1)} %get-tuple-element.19), channel_id=1, source_target_pairs={{16,0},{8,24},{25,9},{1,17},{18,2},{10,26},{27,11},{3,19},{20,4},{... | collective-permute-start | bytes 602120 | tf_op jit(solution)/shard_map/ppermute | solution.py:336
  33.9 0.0 collective-permute-done.10.refs_3_
  33.9 1.3 %collective-permute-done.8.refs_1_ = s16[784,128]{1,0:T(8,128)(2,1)S(1)} collective-permute-done((s16[784,128]{1,0:T(8,128)(2,1)S(1)}, s16[784,128]{1,0:T(8,128)(2,1)S(1)}, u32[]{:S(2)}, u32[]{:S(2)}) %collective-permute-start.8) | collective-permute-done | bytes 200736 | tf_op jit(solution)/shard_map/ppermute | solution.py:336
  35.2 1.3 %collective-permute-done.9.refs_2_ = s16[784,128]{1,0:T(8,128)(2,1)S(1)} collective-permute-done((s16[784,128]{1,0:T(8,128)(2,1)S(1)}, s16[784,128]{1,0:T(8,128)(2,1)S(1)}, u32[]{:S(2)}, u32[]{:S(2)}) %collective-permute-start.9) | collective-permute-done | bytes 200736 | tf_op jit(solution)/shard_map/ppermute | solution.py:336
  36.5 0.7 %collective-permute-start.11 = (bf16[64,128]{1,0:T(8,128)(2,1)S(1)}, bf16[64,128]{1,0:T(8,128)(2,1)S(1)}, u32[]{:S(2)}, u32[]{:S(2)}) collective-permute-start(bf16[64,128]{1,0:T(8,128)(2,1)S(1)} %get-tuple-element.21), channel_id=1, source_target_pairs={{0,24},{24,0},{9,17},{17,9},{2,26},{26,2},{11,19},{19,11},{4,28},{... | collective-permute-start | bytes 49160 | tf_op jit(solution)/shard_map/ppermute | solution.py:354
  37.2 1.3 %collective-permute-start.12 = (bf16[64,128]{1,0:T(8,128)(2,1)S(1)}, bf16[64,128]{1,0:T(8,128)(2,1)S(1)}, u32[]{:S(2)}, u32[]{:S(2)}) collective-permute-start(bf16[64,128]{1,0:T(8,128)(2,1)S(1)} %get-tuple-element.22), channel_id=1, source_target_pairs={{0,16},{24,8},{9,25},{17,1},{2,18},{26,10},{11,27},{19,3},{4,20},{... | collective-permute-start | bytes 49160 | tf_op jit(solution)/shard_map/ppermute | solution.py:354
  38.5 1.3 %collective-permute-start.13 = (bf16[64,128]{1,0:T(8,128)(2,1)S(1)}, bf16[64,128]{1,0:T(8,128)(2,1)S(1)}, u32[]{:S(2)}, u32[]{:S(2)}) collective-permute-start(bf16[64,128]{1,0:T(8,128)(2,1)S(1)} %get-tuple-element.23), channel_id=1, source_target_pairs={{0,8},{24,16},{9,1},{17,25},{2,10},{26,18},{11,3},{19,27},{4,12},{... | collective-permute-start | bytes 49160 | tf_op jit(solution)/shard_map/ppermute | solution.py:354
  39.8 0.0 collective-permute-done.11
  39.8 4.6 %collective-permute-done.12 = bf16[64,128]{1,0:T(8,128)(2,1)S(1)} collective-permute-done((bf16[64,128]{1,0:T(8,128)(2,1)S(1)}, bf16[64,128]{1,0:T(8,128)(2,1)S(1)}, u32[]{:S(2)}, u32[]{:S(2)}) %collective-permute-start.12) | collective-permute-done | bytes 16416 | tf_op jit(solution)/shard_map/ppermute | solution.py:354
  44.4 1.3 %collective-permute-done.13 = bf16[64,128]{1,0:T(8,128)(2,1)S(1)} collective-permute-done((bf16[64,128]{1,0:T(8,128)(2,1)S(1)}, bf16[64,128]{1,0:T(8,128)(2,1)S(1)}, u32[]{:S(2)}, u32[]{:S(2)}) %collective-permute-start.13) | collective-permute-done | bytes 16416 | tf_op jit(solution)/shard_map/ppermute | solution.py:354
  45.7 0.6 %pad_maximum_fusion = bf16[64,256]{1,0:T(8,128)(2,1)} fusion(bf16[64,128]{1,0:T(8,128)(2,1)S(1)} %get-tuple-element.26, bf16[64,128]{1,0:T(8,128)(2,1)S(1)} %get-tuple-element.25), kind=kLoop, calls=%fused_computation.4 | loop fusion | flops 65536 | bytes 65536 | tf_op jit(solution)/shard_map/concatenate | solution.py:364
  (6 shorter events, 0.0 us)
Async XLA Ops:
  0.0 1.0 %copy-start = (bf16[256,512]{1,0:T(8,128)(2,1)S(1)}, bf16[256,512]{1,0:T(8,128)(2,1)}, u32[]{:S(2)}) copy-start(bf16[256,512]{1,0:T(8,128)(2,1)} %param.4) | copy-start | bytes 786436
  1.9 10.5 %collective-permute-start = (bf16[128,512]{1,0:T(8,128)(2,1)S(1)}, bf16[128,512]{1,0:T(8,128)(2,1)S(1)}, u32[]{:S(2)}, u32[]{:S(2)}) collective-permute-start(bf16[128,512]{1,0:T(8,128)(2,1)S(1)} %fusion), channel_id=1, source_target_pairs={{0,0},{1,5},{2,8},{3,13},{4,16},{5,21},{6,24},{7,29},{8,2},{9,7},{... | collective-permute-start | bytes 393224 | tf_op jit(solution)/shard_map/ppermute | solution.py:287
  6.9 9.2 %collective-permute-start.2 = (bf16[128,512]{1,0:T(8,128)(2,1)S(1)}, bf16[128,512]{1,0:T(8,128)(2,1)S(1)}, u32[]{:S(2)}, u32[]{:S(2)}) collective-permute-start(bf16[128,512]{1,0:T(8,128)(2,1)S(1)} %fusion), channel_id=1, source_target_pairs={{0,2},{1,7},{2,10},{3,15},{4,18},{5,23},{6,26},{7,31},{8,4},{9,1},... | collective-permute-start | bytes 393224 | tf_op jit(solution)/shard_map/ppermute | solution.py:287
  10.0 6.1 %collective-permute-start.4 = (bf16[128,512]{1,0:T(8,128)(2,1)S(1)}, bf16[128,512]{1,0:T(8,128)(2,1)S(1)}, u32[]{:S(2)}, u32[]{:S(2)}) collective-permute-start(bf16[128,512]{1,0:T(8,128)(2,1)S(1)} %fusion), channel_id=1, source_target_pairs={{0,4},{1,1},{2,12},{3,9},{4,20},{5,17},{6,28},{7,25},{8,6},{9,3},{... | collective-permute-start | bytes 393224 | tf_op jit(solution)/shard_map/ppermute | solution.py:287
  10.7 8.0 %collective-permute-start.6 = (bf16[128,512]{1,0:T(8,128)(2,1)S(1)}, bf16[128,512]{1,0:T(8,128)(2,1)S(1)}, u32[]{:S(2)}, u32[]{:S(2)}) collective-permute-start(bf16[128,512]{1,0:T(8,128)(2,1)S(1)} %fusion), channel_id=1, source_target_pairs={{0,6},{1,3},{2,14},{3,11},{4,22},{5,19},{6,30},{7,27},{8,0},{9,5},... | collective-permute-start | bytes 393224 | tf_op jit(solution)/shard_map/ppermute | solution.py:287
  12.4 10.0 %collective-permute-start.1 = (bf16[128,512]{1,0:T(8,128)(2,1)S(1)}, bf16[128,512]{1,0:T(8,128)(2,1)S(1)}, u32[]{:S(2)}, u32[]{:S(2)}) collective-permute-start(bf16[128,512]{1,0:T(8,128)(2,1)S(1)} %collective-permute-done.refs_0_), channel_id=1, source_target_pairs={{1,0},{0,1},{3,2},{2,3},{5,4},{4,5},{7,6},{6,7},{9,8},{8,9},{11,10... | collective-permute-start | bytes 393224 | tf_op jit(solution)/shard_map/ppermute | solution.py:296
  16.1 6.3 %collective-permute-start.3 = (bf16[128,512]{1,0:T(8,128)(2,1)S(1)}, bf16[128,512]{1,0:T(8,128)(2,1)S(1)}, u32[]{:S(2)}, u32[]{:S(2)}) collective-permute-start(bf16[128,512]{1,0:T(8,128)(2,1)S(1)} %collective-permute-done.2.refs_1_), channel_id=1, source_target_pairs={{1,0},{0,1},{3,2},{2,3},{5,4},{4,5},{7,6},{6,7},{9,8},{8,9},{11,10... | collective-permute-start | bytes 393224 | tf_op jit(solution)/shard_map/ppermute | solution.py:296
  16.1 6.3 %collective-permute-start.5 = (bf16[128,512]{1,0:T(8,128)(2,1)S(1)}, bf16[128,512]{1,0:T(8,128)(2,1)S(1)}, u32[]{:S(2)}, u32[]{:S(2)}) collective-permute-start(bf16[128,512]{1,0:T(8,128)(2,1)S(1)} %collective-permute-done.4.refs_2_), channel_id=1, source_target_pairs={{1,0},{0,1},{3,2},{2,3},{5,4},{4,5},{7,6},{6,7},{9,8},{8,9},{11,10... | collective-permute-start | bytes 393224 | tf_op jit(solution)/shard_map/ppermute | solution.py:296
  18.7 3.7 %collective-permute-start.7 = (bf16[128,512]{1,0:T(8,128)(2,1)S(1)}, bf16[128,512]{1,0:T(8,128)(2,1)S(1)}, u32[]{:S(2)}, u32[]{:S(2)}) collective-permute-start(bf16[128,512]{1,0:T(8,128)(2,1)S(1)} %collective-permute-done.6.refs_3_), channel_id=1, source_target_pairs={{1,0},{0,1},{3,2},{2,3},{5,4},{4,5},{7,6},{6,7},{9,8},{8,9},{11,10... | collective-permute-start | bytes 393224 | tf_op jit(solution)/shard_map/ppermute | solution.py:296
  23.8 10.1 %collective-permute-start.10 = (s16[784,128]{1,0:T(8,128)(2,1)S(1)}, s16[784,128]{1,0:T(8,128)(2,1)S(1)}, u32[]{:S(2)}, u32[]{:S(2)}) collective-permute-start(s16[784,128]{1,0:T(8,128)(2,1)S(1)} %get-tuple-element.20), channel_id=1, source_target_pairs={{24,0},{0,24},{17,9},{9,17},{26,2},{2,26},{19,11},{11,19},{28,4},{... | collective-permute-start | bytes 602120 | tf_op jit(solution)/shard_map/ppermute | solution.py:336
  24.4 10.8 %collective-permute-start.8 = (s16[784,128]{1,0:T(8,128)(2,1)S(1)}, s16[784,128]{1,0:T(8,128)(2,1)S(1)}, u32[]{:S(2)}, u32[]{:S(2)}) collective-permute-start(s16[784,128]{1,0:T(8,128)(2,1)S(1)} %get-tuple-element.18), channel_id=1, source_target_pairs={{8,0},{16,24},{1,9},{25,17},{10,2},{18,26},{3,11},{27,19},{12,4},{... | collective-permute-start | bytes 602120 | tf_op jit(solution)/shard_map/ppermute | solution.py:336
  32.6 3.9 %collective-permute-start.9 = (s16[784,128]{1,0:T(8,128)(2,1)S(1)}, s16[784,128]{1,0:T(8,128)(2,1)S(1)}, u32[]{:S(2)}, u32[]{:S(2)}) collective-permute-start(s16[784,128]{1,0:T(8,128)(2,1)S(1)} %get-tuple-element.19), channel_id=1, source_target_pairs={{16,0},{8,24},{25,9},{1,17},{18,2},{10,26},{27,11},{3,19},{20,4},{... | collective-permute-start | bytes 602120 | tf_op jit(solution)/shard_map/ppermute | solution.py:336
  36.5 3.3 %collective-permute-start.11 = (bf16[64,128]{1,0:T(8,128)(2,1)S(1)}, bf16[64,128]{1,0:T(8,128)(2,1)S(1)}, u32[]{:S(2)}, u32[]{:S(2)}) collective-permute-start(bf16[64,128]{1,0:T(8,128)(2,1)S(1)} %get-tuple-element.21), channel_id=1, source_target_pairs={{0,24},{24,0},{9,17},{17,9},{2,26},{26,2},{11,19},{19,11},{4,28},{... | collective-permute-start | bytes 49160 | tf_op jit(solution)/shard_map/ppermute | solution.py:354
  37.2 7.2 %collective-permute-start.12 = (bf16[64,128]{1,0:T(8,128)(2,1)S(1)}, bf16[64,128]{1,0:T(8,128)(2,1)S(1)}, u32[]{:S(2)}, u32[]{:S(2)}) collective-permute-start(bf16[64,128]{1,0:T(8,128)(2,1)S(1)} %get-tuple-element.22), channel_id=1, source_target_pairs={{0,16},{24,8},{9,25},{17,1},{2,18},{26,10},{11,27},{19,3},{4,20},{... | collective-permute-start | bytes 49160 | tf_op jit(solution)/shard_map/ppermute | solution.py:354
  38.5 7.2 %collective-permute-start.13 = (bf16[64,128]{1,0:T(8,128)(2,1)S(1)}, bf16[64,128]{1,0:T(8,128)(2,1)S(1)}, u32[]{:S(2)}, u32[]{:S(2)}) collective-permute-start(bf16[64,128]{1,0:T(8,128)(2,1)S(1)} %get-tuple-element.23), channel_id=1, source_target_pairs={{0,8},{24,16},{9,1},{17,25},{2,10},{26,18},{11,3},{19,27},{4,12},{... | collective-permute-start | bytes 49160 | tf_op jit(solution)/shard_map/ppermute | solution.py:354

commit v4 on v3

--- a/solution.py
+++ b/solution.py
@@ -108,26 +108,6 @@
 
 def core_stride(shards, group):
     return shards // group if shards % group == 0 else 0
-
-
-def partner(me, k, shards):
-    return me ^ k if shards & (shards - 1) == 0 else (me + k) % shards
-
-
-def sender(me, k, shards):
-    return me ^ k if shards & (shards - 1) == 0 else (me - k + shards) % shards
-
-
-def keeper(core, head, shards, heads):
-    ends = [i // 2 if i % 2 == 0 else shards - 1 - i // 2 for i in range(shards)]
-    return ends[(core * heads + head) % shards]
-
-
-def chosen(index, options):
-    value = jnp.int32(options[-1])
-    for i, option in enumerate(options[:-1]):
-        value = jnp.where(index == i, jnp.int32(option), value)
-    return value
 
 
 def own_kernel(shards, group, *refs):
@@ -174,19 +154,18 @@
     slots = pick_ref.shape[1] // shards
     width = w_ref.shape[1] // group
     kept = slots // 2 * shards
+    blocks = shards // heads
+    block_rows = kept // blocks
     stride = core_stride(shards, group)
     core = lax.rem(lax.axis_index("tp"), group)
     me = lax.axis_index("seq")
-    keepers = [
-        chosen(core, [keeper(c, head, shards, heads) for c in range(group)]) for head in range(heads)
-    ]
     rows = []
     for p in range(1, group):
         order = [(k + p * stride) % shards for k in range(shards)]
         pick = jnp.concatenate([pick_ref[:, o * slots : (o + 1) * slots] for o in order], axis=1)
         block = jnp.concatenate([half[...] for half in halves[p - 1]], axis=0)
         rows.append(jnp.dot(pick, block, preferred_element_type=jnp.float32).astype(jnp.bfloat16))
-    total = 3 * kept
+    total = 2 * kept + block_rows
     pad = outs[0].shape[0] - total
     exponents = []
     for at, kind in enumerate((1, 2, 0)):
@@ -201,11 +180,20 @@
         exponents.append(exponent)
         value = jnp.round(acc * jnp.exp2(TOP_BITS - exponent)).astype(jnp.int32).astype(jnp.int16)
         for k in range(shards):
+            dest = lax.rem(me + k, shards)
             for head in range(heads):
-
-                @pl.when(partner(me, k, shards) == keepers[head])
-                def _(k=k, head=head, at=at, value=value):
-                    outs[k][at * kept : (at + 1) * kept, :] = value[:, head * HD : (head + 1) * HD]
+                mine = value[:, head * HD : (head + 1) * HD]
+                if kind:
+
+                    @pl.when(lax.rem(dest, heads) == head)
+                    def _(k=k, at=at, mine=mine):
+                        outs[k][at * kept : (at + 1) * kept, :] = mine
+                else:
+                    for b in range(blocks):
+
+                        @pl.when(dest == b * heads + head)
+                        def _(k=k, b=b, mine=mine):
+                            outs[k][2 * kept : total, :] = mine[b * block_rows : (b + 1) * block_rows, :]
 
     index = lax.broadcasted_iota(jnp.int32, (pad, HD), 0)
     for head in range(heads):
@@ -215,52 +203,50 @@
         tail = tail.astype(jnp.int32).astype(jnp.int16)
         for k in range(shards):
 
-            @pl.when(partner(me, k, shards) == keepers[head])
+            @pl.when(lax.rem(lax.rem(me + k, shards), heads) == head)
             def _(k=k, tail=tail):
                 outs[k][total:, :] = tail
 
 
-def attend_kernel(shards, group, heads, *refs):
-    parts, outs, all_ref = refs[:shards], refs[shards : 2 * shards], refs[2 * shards]
-    kept = all_ref.shape[0]
+def attend_kernel(shards, heads, kept, *refs):
+    parts, outs = refs[:shards], refs[shards:]
     capacity = kept // shards
     me = lax.axis_index("seq")
-    core = lax.rem(lax.axis_index("tp"), group)
-    keeps = me == chosen(core, [keeper(c, 0, shards, heads) for c in range(group)])
-    for head in range(1, heads):
-        keeps |= me == chosen(core, [keeper(c, head, shards, heads) for c in range(group)])
-
-    @pl.when(keeps)
-    def _():
-        scales = [
-            jnp.exp2(p[3 * kept :, :].astype(jnp.int32).astype(jnp.float32) - TOP_BITS)
-            for p in parts
-        ]
-
-        def summed(at):
-            acc = None
-            for p, scale in zip(parts, scales):
-                part = p[at * kept : (at + 1) * kept, :].astype(jnp.int32).astype(jnp.float32)
-                part = part * scale[at : at + 1, :]
-                acc = part if acc is None else acc + part
-            return acc.astype(jnp.bfloat16)
-
-        key, value, query = summed(0), summed(1), summed(2)
-        scores = lax.dot_general(
-            query, key, (((1,), (1,)), ((), ())), preferred_element_type=jnp.float32
-        ) * (HD ** (-0.5))
-        q_row = lax.broadcasted_iota(jnp.int32, scores.shape, 0)
-        k_row = lax.broadcasted_iota(jnp.int32, scores.shape, 1)
-        q_rank = lax.rem(q_row, capacity) * shards + lax.div(q_row, capacity)
-        k_rank = lax.rem(k_row, capacity) * shards + lax.div(k_row, capacity)
-        scores = jnp.where(k_rank > q_rank, -jnp.inf, scores)
-        top = jnp.max(scores, axis=1, keepdims=True)
-        expo = jnp.exp(scores - top)
-        numer = jnp.dot(expo.astype(jnp.bfloat16), value, preferred_element_type=jnp.float32)
-        all_ref[...] = numer / jnp.sum(expo, axis=1, keepdims=True)
-        for k in range(shards):
-            owner = pl.multiple_of(partner(me, k, shards) * capacity, capacity)
-            outs[k][...] = all_ref[pl.ds(owner, capacity), :].astype(jnp.bfloat16)
+    block_rows = kept // (shards // heads)
+    total = 2 * kept + block_rows
+    block = lax.div(me, heads)
+    scales = [
+        jnp.exp2(p[total:, :].astype(jnp.int32).astype(jnp.float32) - TOP_BITS) for p in parts
+    ]
+
+    def summed(i, lo, hi):
+        acc = None
+        for p, scale in zip(parts, scales):
+            part = p[lo:hi, :].astype(jnp.int32).astype(jnp.float32) * scale[i : i + 1, :]
+            acc = part if acc is None else acc + part
+        return acc.astype(jnp.bfloat16)
+
+    key, value, query = summed(0, 0, kept), summed(1, kept, 2 * kept), summed(2, 2 * kept, total)
+    scores = lax.dot_general(
+        query, key, (((1,), (1,)), ((), ())), preferred_element_type=jnp.float32
+    ) * (HD ** (-0.5))
+    q_row = lax.broadcasted_iota(jnp.int32, scores.shape, 0) + block * block_rows
+    k_row = lax.broadcasted_iota(jnp.int32, scores.shape, 1)
+    q_rank = lax.rem(q_row, capacity) * shards + lax.div(q_row, capacity)
+    k_rank = lax.rem(k_row, capacity) * shards + lax.div(k_row, capacity)
+    scores = jnp.where(k_rank > q_rank, -jnp.inf, scores)
+    top = jnp.max(scores, axis=1, keepdims=True)
+    expo = jnp.exp(scores - top)
+    numer = jnp.dot(expo.astype(jnp.bfloat16), value, preferred_element_type=jnp.float32)
+    result = (numer / jnp.sum(expo, axis=1, keepdims=True)).astype(jnp.bfloat16)
+    head = lax.rem(me, heads)
+    for k in range(heads):
+        owner = lax.rem(head + k, heads)
+        for o in range(heads):
+
+            @pl.when(owner == o)
+            def _(k=k, o=o):
+                outs[k][...] = result[o * capacity : (o + 1) * capacity, :]
 
 
 def by_features(shards, tp, tokens, w_qkv, keep_list, counts):
@@ -315,7 +301,8 @@
         compiler_params=params,
         name="own",
     )(*own, weights)
-    payload = 3 * kept + 16
+    blocks = shards // heads
+    payload = 2 * kept + kept // blocks + 16
     partial = pl.pallas_call(
         functools.partial(rest_kernel, shards, group, heads),
         out_shape=[jax.ShapeDtypeStruct((payload, HD), jnp.int16)] * shards,
@@ -324,42 +311,30 @@
         compiler_params=params,
         name="rest",
     )(*others, pick, acc, weights)
-    keepers = [[keeper(c, head, shards, heads) for head in range(heads)] for c in range(group)]
     parts = [partial[0]]
     for k in range(1, shards):
-        pairs = [
-            (device(sender(d, k, shards), line, c), device(d, line, c))
-            for line in range(shards)
-            for c in range(group)
-            for d in keepers[c]
-        ]
-        parts.append(lax.ppermute(partial[k], axes, pairs))
+        pairs = [(s, (s + k) % shards) for s in range(shards)]
+        parts.append(lax.ppermute(partial[k], "seq", pairs))
     pieces = pl.pallas_call(
-        functools.partial(attend_kernel, shards, group, heads),
-        out_shape=[jax.ShapeDtypeStruct((capacity, HD), jnp.bfloat16)] * shards,
+        functools.partial(attend_kernel, shards, heads, kept),
+        out_shape=[jax.ShapeDtypeStruct((capacity, HD), jnp.bfloat16)] * heads,
         in_specs=[VMEM] * shards,
-        out_specs=[VMEM] * shards,
-        scratch_shapes=[pltpu.VMEM((kept, HD), jnp.float32)],
+        out_specs=[VMEM] * heads,
         compiler_params=params,
         name="attend",
     )(*parts)
     arrived = [pieces[0]]
-    for k in range(1, shards):
+    for k in range(1, heads):
         pairs = [
-            (device(d, line, c), device(partner(d, k, shards), line, c))
-            for line in range(shards)
-            for c in range(group)
-            for d in keepers[c]
+            (b * heads + h, b * heads + (h + k) % heads) for b in range(blocks) for h in range(heads)
         ]
-        arrived.append(lax.ppermute(pieces[k], axes, pairs))
-    mine = lax.axis_index("seq")
-    core = lax.rem(lax.axis_index("tp"), group)
+        arrived.append(lax.ppermute(pieces[k], "seq", pairs))
+    mine = lax.rem(lax.axis_index("seq"), heads)
     columns = []
-    for head in range(heads):
-        source = chosen(core, [keepers[c][head] for c in range(group)])
+    for h in range(heads):
         column = arrived[0]
-        for k in range(1, shards):
-            column = jnp.where(sender(mine, k, shards) == source, arrived[k], column)
+        for k in range(1, heads):
+            column = jnp.where(lax.rem(mine - k + heads, heads) == h, arrived[k], column)
         columns.append(column)
     return jnp.concatenate(columns, axis=1)
 
@@ -374,7 +349,7 @@
 
     def on_device(tokens, w_qkv, keep_list, counts):
         heads = w_qkv.shape[2] // HD
-        if fits(mesh) and shards >= heads:
+        if fits(mesh) and shards % heads == 0:
             return by_features(shards, tp, tokens, w_qkv, keep_list, counts)
         return by_rows(tokens, w_qkv, keep_list, counts)
 

time: 46.7 us -> 43.1 us (0.923)
  the two profiles are of different devices: /device:TPU:1 before, /device:TPU:0 now
where the time goes in v4:
time: 43.1 us; the launch traced here: 42.9 us
  starting transfers between devices  21.6 us (50%)
  waiting for transfers between devices  14.8 us (34%)
  Pallas kernels  3.92 us (9%)
  matrix products  0.88 us (2%)
  between operations  0.8 us (2%)
  other arithmetic  0.63 us (1%)
    ppermute x4, starting transfers between devices, by_features(): own.append(lax.ppermute(packed, axes, pairs))  14.2 us
    ppermute x3, waiting for transfers between devices, by_features(): parts.append(lax.ppermute(partial[k], 'seq', pairs))  7.99 us
    ppermute x3, starting transfers between devices, by_features(): parts.append(lax.ppermute(partial[k], 'seq', pairs))  6.15 us
    ppermute x4, waiting for transfers between devices, by_features(): own.append(lax.ppermute(packed, axes, pairs))  3.73 us
    ppermute x1, waiting for transfers between devices, by_features(): arrived.append(lax.ppermute(pieces[k], 'seq', pairs))  3.03 us
    pallas_call x1, Pallas kernels, by_features(): pl.pallas_call(load_kernel, out_shape=jax.ShapeDtypeStruct(weights.shape,...  1.42 us
    pallas_call x1, Pallas kernels, by_features(): pl.pallas_call(functools.partial(rest_kernel, shards, group, heads), out_...  1.41 us
    dot_general x1, matrix products, gather(): lax.dot_general(pick, tokens, (((0,), (0,)), ((), ())), preferred_element...  0.88 us
  transfers between devices with their start and end apart: 12, of which 6 were waited for; matrix products, arithmetic and copies ran while one was open for 0% of the time, Pallas kernels for 5%

profile of v4, /device:TPU:0, one launch (start us, length us, event | category | flops | bytes accessed | tf_op | source)
XLA Modules:
  0.0 42.9 jit_solution(5861661953608651568)
XLA Ops:
  0.0 0.0 copy-start
  0.7 0.3 copy-done
  1.0 0.9 %fusion = bf16[128,512]{1,0:T(8,128)(2,1)S(1)} fusion(bf16[256,512]{1,0:T(8,128)(2,1)S(1)} %copy-done, bf16[]{:T(256)} %bitcast, pred[128]{0:T(512)(128)(4,1)S(1)} %iota_compare_fusion.2, s32[128]{0:T(128)} %param.6), kind=kOutput, calls=%fused_computation.1 | convolution fusion | flops 33652736 | bytes 393858 | tf_op jit(solution)/shard_map/dot_general | solution.py:98
  1.9 0.7 %collective-permute-start = (bf16[128,512]{1,0:T(8,128)(2,1)S(1)}, bf16[128,512]{1,0:T(8,128)(2,1)S(1)}, u32[]{:S(2)}, u32[]{:S(2)}) collective-permute-start(bf16[128,512]{1,0:T(8,128)(2,1)S(1)} %fusion), channel_id=1, source_target_pairs={{0,0},{1,5},{2,8},{3,13},{4,16},{5,21},{6,24},{7,29},{8,2},{9,7},{... | collective-permute-start | bytes 393224 | tf_op jit(solution)/shard_map/ppermute | solution.py:273
  2.5 5.7 %collective-permute-start.2 = (bf16[128,512]{1,0:T(8,128)(2,1)S(1)}, bf16[128,512]{1,0:T(8,128)(2,1)S(1)}, u32[]{:S(2)}, u32[]{:S(2)}) collective-permute-start(bf16[128,512]{1,0:T(8,128)(2,1)S(1)} %fusion), channel_id=1, source_target_pairs={{0,2},{1,7},{2,10},{3,15},{4,18},{5,23},{6,26},{7,31},{8,4},{9,1},... | collective-permute-start | bytes 393224 | tf_op jit(solution)/shard_map/ppermute | solution.py:273
  8.3 5.4 %collective-permute-start.4 = (bf16[128,512]{1,0:T(8,128)(2,1)S(1)}, bf16[128,512]{1,0:T(8,128)(2,1)S(1)}, u32[]{:S(2)}, u32[]{:S(2)}) collective-permute-start(bf16[128,512]{1,0:T(8,128)(2,1)S(1)} %fusion), channel_id=1, source_target_pairs={{0,4},{1,1},{2,12},{3,9},{4,20},{5,17},{6,28},{7,25},{8,6},{9,3},{... | collective-permute-start | bytes 393224 | tf_op jit(solution)/shard_map/ppermute | solution.py:273
  13.6 2.4 %collective-permute-start.6 = (bf16[128,512]{1,0:T(8,128)(2,1)S(1)}, bf16[128,512]{1,0:T(8,128)(2,1)S(1)}, u32[]{:S(2)}, u32[]{:S(2)}) collective-permute-start(bf16[128,512]{1,0:T(8,128)(2,1)S(1)} %fusion), channel_id=1, source_target_pairs={{0,6},{1,3},{2,14},{3,11},{4,22},{5,19},{6,30},{7,27},{8,0},{9,5},... | collective-permute-start | bytes 393224 | tf_op jit(solution)/shard_map/ppermute | solution.py:273
  16.0 0.0 collective-permute-done.refs_0_
  16.0 0.0 collective-permute-start.1
  16.0 0.0 collective-permute-done.2.refs_1_
  16.0 0.5 %collective-permute-start.3 = (bf16[128,512]{1,0:T(8,128)(2,1)S(1)}, bf16[128,512]{1,0:T(8,128)(2,1)S(1)}, u32[]{:S(2)}, u32[]{:S(2)}) collective-permute-start(bf16[128,512]{1,0:T(8,128)(2,1)S(1)} %collective-permute-done.2.refs_1_), channel_id=1, source_target_pairs={{1,0},{0,1},{3,2},{2,3},{5,4},{4,5},{7,6},{6,7},{9,8},{8,9},{11,10... | collective-permute-start | bytes 393224 | tf_op jit(solution)/shard_map/ppermute | solution.py:282
  16.6 2.1 %collective-permute-done.4.refs_2_ = bf16[128,512]{1,0:T(8,128)(2,1)S(1)} collective-permute-done((bf16[128,512]{1,0:T(8,128)(2,1)S(1)}, bf16[128,512]{1,0:T(8,128)(2,1)S(1)}, u32[]{:S(2)}, u32[]{:S(2)}) %collective-permute-start.4) | collective-permute-done | bytes 131104 | tf_op jit(solution)/shard_map/ppermute | solution.py:273
  18.7 0.0 collective-permute-start.5
  18.7 1.6 %collective-permute-done.6.refs_3_ = bf16[128,512]{1,0:T(8,128)(2,1)S(1)} collective-permute-done((bf16[128,512]{1,0:T(8,128)(2,1)S(1)}, bf16[128,512]{1,0:T(8,128)(2,1)S(1)}, u32[]{:S(2)}, u32[]{:S(2)}) %collective-permute-start.6) | collective-permute-done | bytes 131104 | tf_op jit(solution)/shard_map/ppermute | solution.py:273
  20.3 0.0 collective-permute-start.7
  20.3 1.4 %load.1.refs_4_.refs_6_ = bf16[3,1024,256]{2,1,0:T(8,128)(2,1)S(1)} custom-call(bf16[3,1024,256]{2,1,0:T(8,128)(2,1)} %bitcast.3), custom_call_target="tpu_custom_call" | custom-call | tf_op jit(solution)/shard_map/load/pallas_call | solution.py:284
  21.7 0.7 %own.1 = (bf16[256,512]{1,0:T(8,128)(2,1)S(1)}, f32[3,256,256]{2,1,0:T(8,128)S(1)}) custom-call(bf16[128,512]{1,0:T(8,128)(2,1)S(1)} %collective-permute-done.refs_0_, bf16[128,512]{1,0:T(8,128)(2,1)S(1)} %collective-permute-done.2.refs_1_, bf16[128,512]{1,0:T(8,128)(2,1)S(1)} %collective-permute-done.4.refs_2_, ...), custom_call_target="tpu_custom_call" | custom-call | tf_op jit(solution)/shard_map/own/pallas_call | solution.py:293
  22.4 0.0 collective-permute-done.1.refs_0_
  22.4 0.0 collective-permute-done.3.refs_1_
  22.4 0.0 collective-permute-done.5.refs_2_
  22.4 0.0 collective-permute-done.7.refs_3_
  22.4 1.4 %rest.1 = (s16[656,128]{1,0:T(8,128)(2,1)S(1)}, s16[656,128]{1,0:T(8,128)(2,1)S(1)}, s16[656,128]{1,0:T(8,128)(2,1)S(1)}, s16[656,128]{1,0:T(8,128)(2,1)S(1)}) custom-call(bf16[128,512]{1,0:T(8,128)(2,1)S(1)} %collective-permute-done.1.refs_0_, bf16[128,512]{1,0:T(8,128)(2,1)S(1)} %collective-permute-done.3.refs_1_, ...), custom_call_target="tpu_custom_call" | custom-call | tf_op jit(solution)/shard_map/rest/pallas_call | solution.py:306
  23.8 2.4 %collective-permute-start.10 = (s16[656,128]{1,0:T(8,128)(2,1)S(1)}, s16[656,128]{1,0:T(8,128)(2,1)S(1)}, u32[]{:S(2)}, u32[]{:S(2)}) collective-permute-start(s16[656,128]{1,0:T(8,128)(2,1)S(1)} %get-tuple-element.18), channel_id=1, source_target_pairs={{0,24},{8,0},{16,8},{24,16},{1,25},{9,1},{17,9},{25,17},{2,26},{10... | collective-permute-start | bytes 503816 | tf_op jit(solution)/shard_map/ppermute | solution.py:317
  26.2 1.4 %collective-permute-start.8 = (s16[656,128]{1,0:T(8,128)(2,1)S(1)}, s16[656,128]{1,0:T(8,128)(2,1)S(1)}, u32[]{:S(2)}, u32[]{:S(2)}) collective-permute-start(s16[656,128]{1,0:T(8,128)(2,1)S(1)} %get-tuple-element.16), channel_id=1, source_target_pairs={{0,8},{8,16},{16,24},{24,0},{1,9},{9,17},{17,25},{25,1},{2,10},{10... | collective-permute-start | bytes 503816 | tf_op jit(solution)/shard_map/ppermute | solution.py:317
  27.6 2.4 %collective-permute-start.9 = (s16[656,128]{1,0:T(8,128)(2,1)S(1)}, s16[656,128]{1,0:T(8,128)(2,1)S(1)}, u32[]{:S(2)}, u32[]{:S(2)}) collective-permute-start(s16[656,128]{1,0:T(8,128)(2,1)S(1)} %get-tuple-element.17), channel_id=1, source_target_pairs={{0,16},{8,24},{16,0},{24,8},{1,17},{9,25},{17,1},{25,9},{2,18},{10... | collective-permute-start | bytes 503816 | tf_op jit(solution)/shard_map/ppermute | solution.py:317
  30.0 2.6 %collective-permute-done.10.refs_3_ = s16[656,128]{1,0:T(8,128)(2,1)S(1)} collective-permute-done((s16[656,128]{1,0:T(8,128)(2,1)S(1)}, s16[656,128]{1,0:T(8,128)(2,1)S(1)}, u32[]{:S(2)}, u32[]{:S(2)}) %collective-permute-start.10) | collective-permute-done | bytes 167968 | tf_op jit(solution)/shard_map/ppermute | solution.py:317
  32.6 5.2 %collective-permute-done.8.refs_1_ = s16[656,128]{1,0:T(8,128)(2,1)S(1)} collective-permute-done((s16[656,128]{1,0:T(8,128)(2,1)S(1)}, s16[656,128]{1,0:T(8,128)(2,1)S(1)}, u32[]{:S(2)}, u32[]{:S(2)}) %collective-permute-start.8) | collective-permute-done | bytes 167968 | tf_op jit(solution)/shard_map/ppermute | solution.py:317
  37.8 0.2 collective-permute-done.9.refs_2_
  38.0 0.4 %attend.1 = (bf16[64,128]{1,0:T(8,128)(2,1)S(1)}, bf16[64,128]{1,0:T(8,128)(2,1)S(1)}) custom-call(s16[656,128]{1,0:T(8,128)(2,1)S(1)} %get-tuple-element.15.refs_0_, s16[656,128]{1,0:T(8,128)(2,1)S(1)} %collective-permute-done.8.refs_1_, s16[656,128]{1,0:T(8,128)(2,1)S(1)} %collective-permute-done.9.refs_2_, s16[656,128]{1,0:T(8,128)(2,1)S(1)} %collective-permute-done.10.refs_3_), custom_call_target="tpu_custom_call" | custom-call | tf_op jit(solution)/shard_map/attend/pallas_call | solution.py:318
  38.4 0.8 %collective-permute-start.11 = (bf16[64,128]{1,0:T(8,128)(2,1)S(1)}, bf16[64,128]{1,0:T(8,128)(2,1)S(1)}, u32[]{:S(2)}, u32[]{:S(2)}) collective-permute-start(bf16[64,128]{1,0:T(8,128)(2,1)S(1)} %get-tuple-element.19), channel_id=1, source_target_pairs={{0,8},{8,0},{16,24},{24,16},{1,9},{9,1},{17,25},{25,17},{2,10},{10... | collective-permute-start | bytes 49160 | tf_op jit(solution)/shard_map/ppermute | solution.py:331
  39.2 3.0 %collective-permute-done.11 = bf16[64,128]{1,0:T(8,128)(2,1)S(1)} collective-permute-done((bf16[64,128]{1,0:T(8,128)(2,1)S(1)}, bf16[64,128]{1,0:T(8,128)(2,1)S(1)}, u32[]{:S(2)}, u32[]{:S(2)}) %collective-permute-start.11) | collective-permute-done | bytes 16416 | tf_op jit(solution)/shard_map/ppermute | solution.py:331
  42.2 0.6 %pad_maximum_fusion = bf16[64,256]{1,0:T(8,128)(2,1)} fusion(bf16[64,128]{1,0:T(8,128)(2,1)S(1)} %get-tuple-element.22, bf16[64,128]{1,0:T(8,128)(2,1)S(1)} %get-tuple-element.21), kind=kLoop, calls=%fused_computation.4 | loop fusion | flops 65536 | bytes 65536 | tf_op jit(solution)/shard_map/concatenate | solution.py:339
  (2 shorter events, 0.0 us)
Async XLA Ops:
  0.0 1.0 %copy-start = (bf16[256,512]{1,0:T(8,128)(2,1)S(1)}, bf16[256,512]{1,0:T(8,128)(2,1)}, u32[]{:S(2)}) copy-start(bf16[256,512]{1,0:T(8,128)(2,1)} %param.4) | copy-start | bytes 786436
  1.9 14.2 %collective-permute-start = (bf16[128,512]{1,0:T(8,128)(2,1)S(1)}, bf16[128,512]{1,0:T(8,128)(2,1)S(1)}, u32[]{:S(2)}, u32[]{:S(2)}) collective-permute-start(bf16[128,512]{1,0:T(8,128)(2,1)S(1)} %fusion), channel_id=1, source_target_pairs={{0,0},{1,5},{2,8},{3,13},{4,16},{5,21},{6,24},{7,29},{8,2},{9,7},{... | collective-permute-start | bytes 393224 | tf_op jit(solution)/shard_map/ppermute | solution.py:273
  2.5 13.5 %collective-permute-start.2 = (bf16[128,512]{1,0:T(8,128)(2,1)S(1)}, bf16[128,512]{1,0:T(8,128)(2,1)S(1)}, u32[]{:S(2)}, u32[]{:S(2)}) collective-permute-start(bf16[128,512]{1,0:T(8,128)(2,1)S(1)} %fusion), channel_id=1, source_target_pairs={{0,2},{1,7},{2,10},{3,15},{4,18},{5,23},{6,26},{7,31},{8,4},{9,1},... | collective-permute-start | bytes 393224 | tf_op jit(solution)/shard_map/ppermute | solution.py:273
  8.3 10.4 %collective-permute-start.4 = (bf16[128,512]{1,0:T(8,128)(2,1)S(1)}, bf16[128,512]{1,0:T(8,128)(2,1)S(1)}, u32[]{:S(2)}, u32[]{:S(2)}) collective-permute-start(bf16[128,512]{1,0:T(8,128)(2,1)S(1)} %fusion), channel_id=1, source_target_pairs={{0,4},{1,1},{2,12},{3,9},{4,20},{5,17},{6,28},{7,25},{8,6},{9,3},{... | collective-permute-start | bytes 393224 | tf_op jit(solution)/shard_map/ppermute | solution.py:273
  13.6 6.6 %collective-permute-start.6 = (bf16[128,512]{1,0:T(8,128)(2,1)S(1)}, bf16[128,512]{1,0:T(8,128)(2,1)S(1)}, u32[]{:S(2)}, u32[]{:S(2)}) collective-permute-start(bf16[128,512]{1,0:T(8,128)(2,1)S(1)} %fusion), channel_id=1, source_target_pairs={{0,6},{1,3},{2,14},{3,11},{4,22},{5,19},{6,30},{7,27},{8,0},{9,5},... | collective-permute-start | bytes 393224 | tf_op jit(solution)/shard_map/ppermute | solution.py:273
  16.0 6.3 %collective-permute-start.1 = (bf16[128,512]{1,0:T(8,128)(2,1)S(1)}, bf16[128,512]{1,0:T(8,128)(2,1)S(1)}, u32[]{:S(2)}, u32[]{:S(2)}) collective-permute-start(bf16[128,512]{1,0:T(8,128)(2,1)S(1)} %collective-permute-done.refs_0_), channel_id=1, source_target_pairs={{1,0},{0,1},{3,2},{2,3},{5,4},{4,5},{7,6},{6,7},{9,8},{8,9},{11,10... | collective-permute-start | bytes 393224 | tf_op jit(solution)/shard_map/ppermute | solution.py:282
  16.0 6.3 %collective-permute-start.3 = (bf16[128,512]{1,0:T(8,128)(2,1)S(1)}, bf16[128,512]{1,0:T(8,128)(2,1)S(1)}, u32[]{:S(2)}, u32[]{:S(2)}) collective-permute-start(bf16[128,512]{1,0:T(8,128)(2,1)S(1)} %collective-permute-done.2.refs_1_), channel_id=1, source_target_pairs={{1,0},{0,1},{3,2},{2,3},{5,4},{4,5},{7,6},{6,7},{9,8},{8,9},{11,10... | collective-permute-start | bytes 393224 | tf_op jit(solution)/shard_map/ppermute | solution.py:282
  18.7 3.7 %collective-permute-start.5 = (bf16[128,512]{1,0:T(8,128)(2,1)S(1)}, bf16[128,512]{1,0:T(8,128)(2,1)S(1)}, u32[]{:S(2)}, u32[]{:S(2)}) collective-permute-start(bf16[128,512]{1,0:T(8,128)(2,1)S(1)} %collective-permute-done.4.refs_2_), channel_id=1, source_target_pairs={{1,0},{0,1},{3,2},{2,3},{5,4},{4,5},{7,6},{6,7},{9,8},{8,9},{11,10... | collective-permute-start | bytes 393224 | tf_op jit(solution)/shard_map/ppermute | solution.py:282
  20.3 2.1 %collective-permute-start.7 = (bf16[128,512]{1,0:T(8,128)(2,1)S(1)}, bf16[128,512]{1,0:T(8,128)(2,1)S(1)}, u32[]{:S(2)}, u32[]{:S(2)}) collective-permute-start(bf16[128,512]{1,0:T(8,128)(2,1)S(1)} %collective-permute-done.6.refs_3_), channel_id=1, source_target_pairs={{1,0},{0,1},{3,2},{2,3},{5,4},{4,5},{7,6},{6,7},{9,8},{8,9},{11,10... | collective-permute-start | bytes 393224 | tf_op jit(solution)/shard_map/ppermute | solution.py:282
  23.8 8.8 %collective-permute-start.10 = (s16[656,128]{1,0:T(8,128)(2,1)S(1)}, s16[656,128]{1,0:T(8,128)(2,1)S(1)}, u32[]{:S(2)}, u32[]{:S(2)}) collective-permute-start(s16[656,128]{1,0:T(8,128)(2,1)S(1)} %get-tuple-element.18), channel_id=1, source_target_pairs={{0,24},{8,0},{16,8},{24,16},{1,25},{9,1},{17,9},{25,17},{2,26},{10... | collective-permute-start | bytes 503816 | tf_op jit(solution)/shard_map/ppermute | solution.py:317
  26.2 11.6 %collective-permute-start.8 = (s16[656,128]{1,0:T(8,128)(2,1)S(1)}, s16[656,128]{1,0:T(8,128)(2,1)S(1)}, u32[]{:S(2)}, u32[]{:S(2)}) collective-permute-start(s16[656,128]{1,0:T(8,128)(2,1)S(1)} %get-tuple-element.16), channel_id=1, source_target_pairs={{0,8},{8,16},{16,24},{24,0},{1,9},{9,17},{17,25},{25,1},{2,10},{10... | collective-permute-start | bytes 503816 | tf_op jit(solution)/shard_map/ppermute | solution.py:317
  27.6 10.4 %collective-permute-start.9 = (s16[656,128]{1,0:T(8,128)(2,1)S(1)}, s16[656,128]{1,0:T(8,128)(2,1)S(1)}, u32[]{:S(2)}, u32[]{:S(2)}) collective-permute-start(s16[656,128]{1,0:T(8,128)(2,1)S(1)} %get-tuple-element.17), channel_id=1, source_target_pairs={{0,16},{8,24},{16,0},{24,8},{1,17},{9,25},{17,1},{25,9},{2,18},{10... | collective-permute-start | bytes 503816 | tf_op jit(solution)/shard_map/ppermute | solution.py:317
  38.4 3.8 %collective-permute-start.11 = (bf16[64,128]{1,0:T(8,128)(2,1)S(1)}, bf16[64,128]{1,0:T(8,128)(2,1)S(1)}, u32[]{:S(2)}, u32[]{:S(2)}) collective-permute-start(bf16[64,128]{1,0:T(8,128)(2,1)S(1)} %get-tuple-element.19), channel_id=1, source_target_pairs={{0,8},{8,0},{16,24},{24,16},{1,9},{9,1},{17,25},{25,17},{2,10},{10... | collective-permute-start | bytes 49160 | tf_op jit(solution)/shard_map/ppermute | solution.py:331

commit v5 on v4

--- a/solution.py
+++ b/solution.py
@@ -89,15 +89,32 @@
 VMEM = pl.BlockSpec(memory_space=pltpu.VMEM)
 HBM = pl.BlockSpec(memory_space=pltpu.HBM)
 TOP_BITS = 14
-
-
-def gather(tokens, keep_list, counts):
-    slots = keep_list.shape[0]
-    token = lax.broadcasted_iota(jnp.int32, (tokens.shape[0], slots), 0)
-    pick = (token == keep_list[None, :]).astype(jnp.bfloat16)
-    rows = lax.dot_general(pick, tokens, (((0,), (0,)), ((), ())), preferred_element_type=jnp.float32)
+CORES = 2
+FIRST = 2
+
+
+def gather_kernel(counts_ref, keep_ref, tokens_ref, pick_ref, out_ref):
+    slots = out_ref.shape[0]
+    token = lax.broadcasted_iota(jnp.int32, (tokens_ref.shape[0], slots), 0)
+    pick = (token == keep_ref[...]).astype(jnp.bfloat16)
+    pick_ref[...] = pick
+    rows = lax.dot_general(
+        pick, tokens_ref[...], (((0,), (0,)), ((), ())), preferred_element_type=jnp.float32
+    )
+    count = counts_ref[0].astype(jnp.float32)
     last = lax.broadcasted_iota(jnp.int32, rows.shape, 0) == slots - 1
-    return jnp.where(last, counts[0].astype(jnp.float32), rows).astype(jnp.bfloat16)
+    out_ref[...] = jnp.where(last, count, rows).astype(jnp.bfloat16)
+
+
+def join_kernel(pick_ref, own_ref, other_ref, out_ref):
+    slots = own_ref.shape[0]
+    rows = lax.dot_general(
+        pick_ref[...], other_ref[...], (((0,), (0,)), ((), ())), preferred_element_type=jnp.float32
+    )
+    last = lax.broadcasted_iota(jnp.int32, rows.shape, 0) == slots - 1
+    count = own_ref[slots - 1 : slots, :].astype(jnp.float32)
+    out_ref[:slots, :] = own_ref[...]
+    out_ref[slots:, :] = jnp.where(last, count, rows).astype(jnp.bfloat16)
 
 
 def load_kernel(w_hbm, out_ref, sem):
@@ -106,21 +123,19 @@
     copy.wait()
 
 
-def core_stride(shards, group):
-    return shards // group if shards % group == 0 else 0
-
-
-def own_kernel(shards, group, *refs):
-    chunks, w_ref, (pick_ref, acc_ref) = refs[:shards], refs[shards], refs[shards + 1 :]
-    slots, width = chunks[0].shape
-    capacity = slots // 2
-    kept = capacity * shards
+def early_kernel(shards, *refs):
+    ops = shards // CORES
+    chunks, w_ref, (pick_ref, acc_ref) = refs[: shards - 1], refs[shards - 1], refs[shards:]
+    slots, width = pick_ref.shape[1], chunks[0].shape[1]
+    kept = pick_ref.shape[0]
+    capacity = kept // shards
     tp = lax.axis_index("tp")
-    core = lax.rem(tp, group)
-    line = lax.div(tp, group)
-    stride = core_stride(shards, group)
-    shard = [lax.rem(line - k - core * stride + 2 * shards, shards) for k in range(shards)]
-    count = [chunks[k][slots - 1 : slots, :slots].astype(jnp.float32) for k in range(shards)]
+    core = lax.rem(tp, CORES)
+    line = lax.div(tp, CORES)
+    own_shard = [lax.rem(line - shift(k, core, shards) + 4 * shards, shards) for k in range(ops)]
+    shard = own_shard + [lax.rem(o + ops, shards) for o in own_shard]
+    count = [chunk[slots - 1 : slots, :slots].astype(jnp.float32) for chunk in chunks]
+    count.append(kept - functools.reduce(lambda x, y: x + y, count))
     row = lax.broadcasted_iota(jnp.int32, (kept, slots), 0)
     rank = ((row % capacity) * shards + row // capacity).astype(jnp.float32)
     slot = lax.broadcasted_iota(jnp.int32, (kept, slots), 1).astype(jnp.float32)
@@ -133,48 +148,53 @@
                 start += jnp.where(shard[j] < shard[k], count[j], 0.0)
         hit = (first == start) & (slot < count[k])
         picks.append(jnp.where(hit, 1.0, 0.0).astype(jnp.bfloat16))
-        pick_ref[:, k * slots : (k + 1) * slots] = picks[k]
-    rows = jnp.dot(
-        jnp.concatenate(picks, axis=1),
-        jnp.concatenate([chunk[...] for chunk in chunks], axis=0),
-        preferred_element_type=jnp.float32,
-    ).astype(jnp.bfloat16)
-    where = pl.multiple_of(core * width, width)
+    pick_ref[...] = picks[-1]
+    pick = jnp.concatenate(picks[:-1], axis=1)
+    rows = []
+    for q in range(CORES):
+        block = jnp.concatenate(
+            [
+                chunk[at * slots : (at + 1) * slots, :]
+                for chunk, at in zip(chunks, [q] * ops + [1 - q] * (ops - 1))
+            ],
+            axis=0,
+        )
+        rows.append(jnp.dot(pick, block, preferred_element_type=jnp.float32).astype(jnp.bfloat16))
     for kind in range(3):
-        acc_ref[kind] = jnp.dot(
-            rows, w_ref[kind, pl.ds(where, width), :], preferred_element_type=jnp.float32
+        acc_ref[kind] = times(rows, w_ref, kind, core, width)
+
+
+def times(rows, w_ref, kind, core, width):
+    acc = None
+    for q in range(CORES):
+        where = pl.multiple_of(lax.rem(core + q, CORES) * width, width)
+        part = jnp.dot(
+            rows[q], w_ref[kind, pl.ds(where, width), :], preferred_element_type=jnp.float32
         )
-
-
-def rest_kernel(shards, group, heads, *refs):
-    count = shards * (group - 1)
-    halves = [refs[shards * p : shards * (p + 1)] for p in range(group - 1)]
-    pick_ref, acc_ref, w_ref = refs[count : count + 3]
-    outs = refs[count + 3 :]
-    slots = pick_ref.shape[1] // shards
-    width = w_ref.shape[1] // group
-    kept = slots // 2 * shards
+        acc = part if acc is None else acc + part
+    return acc
+
+
+def rest_kernel(shards, heads, chunk_ref, pick_ref, acc_ref, w_ref, *outs):
+    kept, slots = pick_ref.shape
+    width = chunk_ref.shape[1]
     blocks = shards // heads
     block_rows = kept // blocks
-    stride = core_stride(shards, group)
-    core = lax.rem(lax.axis_index("tp"), group)
+    core = lax.rem(lax.axis_index("tp"), CORES)
     me = lax.axis_index("seq")
-    rows = []
-    for p in range(1, group):
-        order = [(k + p * stride) % shards for k in range(shards)]
-        pick = jnp.concatenate([pick_ref[:, o * slots : (o + 1) * slots] for o in order], axis=1)
-        block = jnp.concatenate([half[...] for half in halves[p - 1]], axis=0)
-        rows.append(jnp.dot(pick, block, preferred_element_type=jnp.float32).astype(jnp.bfloat16))
+    rows = [
+        jnp.dot(
+            pick_ref[...],
+            chunk_ref[(1 - q) * slots : (2 - q) * slots, :],
+            preferred_element_type=jnp.float32,
+        ).astype(jnp.bfloat16)
+        for q in range(CORES)
+    ]
     total = 2 * kept + block_rows
     pad = outs[0].shape[0] - total
     exponents = []
     for at, kind in enumerate((1, 2, 0)):
-        acc = acc_ref[kind]
-        for p in range(1, group):
-            where = pl.multiple_of(lax.rem(core + p, group) * width, width)
-            acc += jnp.dot(
-                rows[p - 1], w_ref[kind, pl.ds(where, width), :], preferred_element_type=jnp.float32
-            )
+        acc = acc_ref[kind] + times(rows, w_ref, kind, core, width)
         most = jnp.maximum(jnp.max(jnp.abs(acc), axis=0, keepdims=True), 2.0**-100)
         exponent = jnp.floor(jnp.log2(most)) + 1.0
         exponents.append(exponent)
@@ -249,37 +269,55 @@
                 outs[k][...] = result[o * capacity : (o + 1) * capacity, :]
 
 
-def by_features(shards, tp, tokens, w_qkv, keep_list, counts):
-    group = tp // shards
+def shift(k, core, shards):
+    return FIRST + k + core * (shards // CORES)
+
+
+def by_features(shards, tokens, w_qkv, keep_list, counts):
+    tp = shards * CORES
     slots = keep_list.shape[0]
     capacity = slots // 2
     kept = capacity * shards
+    width = tokens.shape[1]
     heads = w_qkv.shape[2] // HD
-    axes = ("seq", "tp")
+    ops = shards // CORES
     params = pltpu.CompilerParams(vmem_limit_bytes=32 * 1024 * 1024)
 
     def device(s, line, core):
-        return s * tp + line * group + core
-
-    packed = gather(tokens, keep_list, counts)
-    stride = core_stride(shards, group)
-    every = [(s, line, c) for s in range(shards) for line in range(shards) for c in range(group)]
+        return s * tp + line * CORES + core
+
+    swap = [(line * CORES + c, line * CORES + 1 - c) for line in range(shards) for c in range(CORES)]
+    other = lax.ppermute(tokens, "tp", swap)
+    pick, mine = pl.pallas_call(
+        gather_kernel,
+        out_shape=[
+            jax.ShapeDtypeStruct((tokens.shape[0], slots), jnp.bfloat16),
+            jax.ShapeDtypeStruct((slots, width), jnp.bfloat16),
+        ],
+        in_specs=[pl.BlockSpec(memory_space=pltpu.SMEM), VMEM, VMEM],
+        out_specs=[VMEM] * 2,
+        compiler_params=params,
+        name="gather",
+    )(counts, keep_list.reshape(1, slots), tokens)
+    packed = pl.pallas_call(
+        join_kernel,
+        out_shape=jax.ShapeDtypeStruct((CORES * slots, width), jnp.bfloat16),
+        in_specs=[VMEM] * 3,
+        out_specs=VMEM,
+        compiler_params=params,
+        name="join",
+    )(pick, mine, other)
+    every = [(s, line, c) for s in range(shards) for line in range(shards) for c in range(CORES)]
     own = []
-    for k in range(shards):
+    for k in range(ops):
         pairs = [
-            (device(s, line, c), device(line, (s + k + c * stride) % shards, c))
+            (device(s, line, c), device(line, (s + shift(k, c, shards)) % shards, c))
             for s, line, c in every
         ]
-        own.append(lax.ppermute(packed, axes, pairs))
+        own.append(lax.ppermute(packed, ("seq", "tp"), pairs))
     others = []
-    for p in range(1, group):
-        pairs = [
-            (line * group + (c + p) % group, line * group + c)
-            for line in range(shards)
-            for c in range(group)
-        ]
-        for k in range(shards):
-            others.append(lax.ppermute(own[k], "tp", pairs))
+    for k in range(ops):
+        others.append(lax.ppermute(own[k], "tp", swap))
     weights = jnp.transpose(w_qkv, (1, 0, 2))
     weights = pl.pallas_call(
         load_kernel,
@@ -291,26 +329,26 @@
         name="load",
     )(weights)
     pick, acc = pl.pallas_call(
-        functools.partial(own_kernel, shards, group),
+        functools.partial(early_kernel, shards),
         out_shape=[
-            jax.ShapeDtypeStruct((kept, shards * slots), jnp.bfloat16),
+            jax.ShapeDtypeStruct((kept, slots), jnp.bfloat16),
             jax.ShapeDtypeStruct((3, kept, heads * HD), jnp.float32),
         ],
-        in_specs=[VMEM] * (shards + 1),
+        in_specs=[VMEM] * shards,
         out_specs=[VMEM] * 2,
         compiler_params=params,
-        name="own",
-    )(*own, weights)
+        name="early",
+    )(*own, *others[:-1], weights)
     blocks = shards // heads
     payload = 2 * kept + kept // blocks + 16
     partial = pl.pallas_call(
-        functools.partial(rest_kernel, shards, group, heads),
+        functools.partial(rest_kernel, shards, heads),
         out_shape=[jax.ShapeDtypeStruct((payload, HD), jnp.int16)] * shards,
-        in_specs=[VMEM] * (shards * (group - 1) + 3),
+        in_specs=[VMEM] * 4,
         out_specs=[VMEM] * shards,
         compiler_params=params,
         name="rest",
-    )(*others, pick, acc, weights)
+    )(others[-1], pick, acc, weights)
     parts = [partial[0]]
     for k in range(1, shards):
         pairs = [(s, (s + k) % shards) for s in range(shards)]
@@ -341,16 +379,16 @@
 
 def fits(mesh):
     shards, tp = mesh.shape["seq"], mesh.shape["tp"]
-    return tp % shards == 0 and tp > shards
+    return tp == shards * CORES and shards % CORES == 0
 
 
 def solution(mesh):
-    shards, tp = mesh.shape["seq"], mesh.shape["tp"]
+    shards = mesh.shape["seq"]
 
     def on_device(tokens, w_qkv, keep_list, counts):
         heads = w_qkv.shape[2] // HD
         if fits(mesh) and shards % heads == 0:
-            return by_features(shards, tp, tokens, w_qkv, keep_list, counts)
+            return by_features(shards, tokens, w_qkv, keep_list, counts)
         return by_rows(tokens, w_qkv, keep_list, counts)
 
     in_specs = (P("seq", "tp"), P("seq", None, "tp"), P("seq"), P("seq"))

time: 43.1 us -> 43.9 us (1.019)
  local copies, waits for them, and re-layouts: 0.26 us -> 1.6 us
  Pallas kernels: 3.92 us -> 5.05 us
  matrix products: 0.88 us -> 0 us
  starting transfers between devices: 21.6 us -> 21 us
    ppermute x8 -> x5, starting transfers between devices: 14.7 us -> 9.38 us  [the longest x2 8.88 us: by_features(): own.append(lax.ppermute(packed, ('seq', 'tp'), pairs))]
    ppermute x3, starting transfers between devices: 6.15 us -> 9.81 us  [by_features(): parts.append(lax.ppermute(partial[k], 'seq', pairs))]
    ppermute x8 -> x5, waiting for transfers between devices: 3.74 us -> 5.83 us  [the longest x2 5.82 us: by_features(): own.append(lax.ppermute(packed, ('seq', 'tp'), pairs))]
    unnamed x2 -> x4, local copies, waits for them, and re-layouts: 0.26 us -> 1.6 us
    ppermute x3, waiting for transfers between devices: 7.99 us -> 6.86 us  [by_features(): parts.append(lax.ppermute(partial[k], 'seq', pairs))]
    pallas_call x2 -> x4, Pallas kernels: 2.07 us -> 3.2 us  [the longest x1 1.81 us: by_features(): pl.pallas_call(functools.partial(rest_kernel, shards, heads), out_shape=[...]
    ppermute x1, waiting for transfers between devices: 3.03 us -> 2.04 us  [by_features(): arrived.append(lax.ppermute(pieces[k], 'seq', pairs))]
    ppermute x1, starting transfers between devices: 0.77 us -> 1.77 us  [by_features(): arrived.append(lax.ppermute(pieces[k], 'seq', pairs))]
  transfers between devices with their start and end apart: 12 -> 9, of which waited for: 6 -> 5; matrix products, arithmetic and copies ran while one was open for 0% -> 0% of each run, Pallas kernels for 5% -> 6%
where the time goes in v5:
time: 43.9 us; the launch traced here: 43.7 us
  starting transfers between devices  21 us (48%)
  waiting for transfers between devices  14.7 us (33%)
  Pallas kernels  5.05 us (12%)
  local copies, waits for them, and re-layouts  1.6 us (4%)
  between operations  0.75 us (2%)
  other arithmetic  0.63 us (1%)
    ppermute x3, starting transfers between devices, by_features(): parts.append(lax.ppermute(partial[k], 'seq', pairs))  9.81 us
    ppermute x2, starting transfers between devices, by_features(): own.append(lax.ppermute(packed, ('seq', 'tp'), pairs))  8.88 us
    ppermute x3, waiting for transfers between devices, by_features(): parts.append(lax.ppermute(partial[k], 'seq', pairs))  6.86 us
    ppermute x2, waiting for transfers between devices, by_features(): own.append(lax.ppermute(packed, ('seq', 'tp'), pairs))  5.82 us
    ppermute x1, waiting for transfers between devices, by_features(): arrived.append(lax.ppermute(pieces[k], 'seq', pairs))  2.04 us
    pallas_call x1, Pallas kernels, by_features(): pl.pallas_call(functools.partial(rest_kernel, shards, heads), out_shape=[...  1.81 us
    ppermute x1, starting transfers between devices, by_features(): arrived.append(lax.ppermute(pieces[k], 'seq', pairs))  1.77 us
    unnamed x4, local copies, waits for them, and re-layouts  1.6 us
  transfers between devices with their start and end apart: 9, of which 5 were waited for; matrix products, arithmetic and copies ran while one was open for 0% of the time, Pallas kernels for 6%

profile of v5, /device:TPU:0, one launch (start us, length us, event | category | flops | bytes accessed | tf_op | source)
XLA Modules:
  0.0 43.7 jit_solution(3234679686182395994)
XLA Ops:
  0.0 0.5 %collective-permute-start = (bf16[256,512]{1,0:T(8,128)(2,1)}, bf16[256,512]{1,0:T(8,128)(2,1)S(1)}, u32[]{:S(2)}, u32[]{:S(2)}) collective-permute-start(bf16[256,512]{1,0:T(8,128)(2,1)} %tokens_ref.1), channel_id=1, source_target_pairs={{0,1},{1,0},{2,3},{3,2},{4,5},{5,4},{6,7},{7,6},{8,9},{9,8},{10,11... | collective-permute-start | bytes 786440 | tf_op jit(solution)/shard_map/ppermute | solution.py:290
  1.1 0.0 copy-start
  1.2 0.9 %copy-done = bf16[256,512]{1,0:T(8,128)(2,1)S(1)} copy-done((bf16[256,512]{1,0:T(8,128)(2,1)S(1)}, bf16[256,512]{1,0:T(8,128)(2,1)}, u32[]{:S(2)}) %copy-start) | copy-done | bytes 262168
  2.1 0.0 copy-start.1
  2.1 0.7 %copy-done.1 = s32[128]{0:T(128)S(1)} copy-done((s32[128]{0:T(128)S(1)}, s32[128]{0:T(128)}, u32[]{:S(2)}) %copy-start.1) | copy-done | bytes 536
  2.8 0.2 gather.1
  3.0 0.0 collective-permute-done.other_ref
  3.0 0.2 join.1
  3.2 5.5 %collective-permute-start.3 = (bf16[256,512]{1,0:T(8,128)(2,1)S(1)}, bf16[256,512]{1,0:T(8,128)(2,1)S(1)}, u32[]{:S(2)}, u32[]{:S(2)}) collective-permute-start(bf16[256,512]{1,0:T(8,128)(2,1)S(1)} %join.1), channel_id=1, source_target_pairs={{0,4},{1,1},{2,12},{3,9},{4,20},{5,17},{6,28},{7,25},{8,6},{9,3},{... | collective-permute-start | bytes 786440 | tf_op jit(solution)/shard_map/ppermute | solution.py:317
  8.7 3.4 %collective-permute-start.1 = (bf16[256,512]{1,0:T(8,128)(2,1)S(1)}, bf16[256,512]{1,0:T(8,128)(2,1)S(1)}, u32[]{:S(2)}, u32[]{:S(2)}) collective-permute-start(bf16[256,512]{1,0:T(8,128)(2,1)S(1)} %join.1), channel_id=1, source_target_pairs={{0,6},{1,3},{2,14},{3,11},{4,22},{5,19},{6,30},{7,27},{8,0},{9,5},... | collective-permute-start | bytes 786440 | tf_op jit(solution)/shard_map/ppermute | solution.py:317
  12.1 3.0 %collective-permute-done.3.refs_0_ = bf16[256,512]{1,0:T(8,128)(2,1)S(1)} collective-permute-done((bf16[256,512]{1,0:T(8,128)(2,1)S(1)}, bf16[256,512]{1,0:T(8,128)(2,1)S(1)}, u32[]{:S(2)}, u32[]{:S(2)}) %collective-permute-start.3) | collective-permute-done | bytes 262176 | tf_op jit(solution)/shard_map/ppermute | solution.py:317
  15.1 0.0 collective-permute-start.4
  15.1 2.8 %collective-permute-done.1.refs_1_ = bf16[256,512]{1,0:T(8,128)(2,1)S(1)} collective-permute-done((bf16[256,512]{1,0:T(8,128)(2,1)S(1)}, bf16[256,512]{1,0:T(8,128)(2,1)S(1)}, u32[]{:S(2)}, u32[]{:S(2)}) %collective-permute-start.1) | collective-permute-done | bytes 262176 | tf_op jit(solution)/shard_map/ppermute | solution.py:317
  17.9 0.0 collective-permute-start.2
  17.9 1.4 %load.1.refs_3_.w_ref = bf16[3,1024,256]{2,1,0:T(8,128)(2,1)S(1)} custom-call(bf16[3,1024,256]{2,1,0:T(8,128)(2,1)} %bitcast.3), custom_call_target="tpu_custom_call" | custom-call | tf_op jit(solution)/shard_map/load/pallas_call | solution.py:322
  19.3 0.0 collective-permute-done.4.refs_2_
  19.4 1.0 %early.1 = (bf16[256,128]{1,0:T(8,128)(2,1)S(1)}, f32[3,256,256]{2,1,0:T(8,128)S(1)}) custom-call(bf16[256,512]{1,0:T(8,128)(2,1)S(1)} %collective-permute-done.3.refs_0_, bf16[256,512]{1,0:T(8,128)(2,1)S(1)} %collective-permute-done.1.refs_1_, bf16[256,512]{1,0:T(8,128)(2,1)S(1)} %collective-permute-done.4.refs_2_, bf16[3,1024,256]{2,1,0:T(8,128)(2,1)S(1)} %load.1.refs_3_.w_ref), custom_call_target="tpu_custom_call" | custom-call | tf_op jit(solution)/shard_map/early/pallas_call | solution.py:331
  20.3 0.0 collective-permute-done.2.chunk_ref
  20.3 1.8 %rest.1 = (s16[656,128]{1,0:T(8,128)(2,1)S(1)}, s16[656,128]{1,0:T(8,128)(2,1)S(1)}, s16[656,128]{1,0:T(8,128)(2,1)S(1)}, s16[656,128]{1,0:T(8,128)(2,1)S(1)}) custom-call(bf16[256,512]{1,0:T(8,128)(2,1)S(1)} %collective-permute-done.2.chunk_ref, bf16[256,128]{1,0:T(8,128)(2,1)S(1)} %get-tuple-element.17.pick_ref, ...), custom_call_target="tpu_custom_call" | custom-call | tf_op jit(solution)/shard_map/rest/pallas_call | solution.py:344
  22.2 4.0 %collective-permute-start.5 = (s16[656,128]{1,0:T(8,128)(2,1)S(1)}, s16[656,128]{1,0:T(8,128)(2,1)S(1)}, u32[]{:S(2)}, u32[]{:S(2)}) collective-permute-start(s16[656,128]{1,0:T(8,128)(2,1)S(1)} %get-tuple-element.20), channel_id=1, source_target_pairs={{0,8},{8,16},{16,24},{24,0},{1,9},{9,17},{17,25},{25,1},{2,10},{10... | collective-permute-start | bytes 503816 | tf_op jit(solution)/shard_map/ppermute | solution.py:355
  26.2 3.0 %collective-permute-start.6 = (s16[656,128]{1,0:T(8,128)(2,1)S(1)}, s16[656,128]{1,0:T(8,128)(2,1)S(1)}, u32[]{:S(2)}, u32[]{:S(2)}) collective-permute-start(s16[656,128]{1,0:T(8,128)(2,1)S(1)} %get-tuple-element.21), channel_id=1, source_target_pairs={{0,16},{8,24},{16,0},{24,8},{1,17},{9,25},{17,1},{25,9},{2,18},{10... | collective-permute-start | bytes 503816 | tf_op jit(solution)/shard_map/ppermute | solution.py:355
  29.1 2.8 %collective-permute-start.7 = (s16[656,128]{1,0:T(8,128)(2,1)S(1)}, s16[656,128]{1,0:T(8,128)(2,1)S(1)}, u32[]{:S(2)}, u32[]{:S(2)}) collective-permute-start(s16[656,128]{1,0:T(8,128)(2,1)S(1)} %get-tuple-element.22), channel_id=1, source_target_pairs={{0,24},{8,0},{16,8},{24,16},{1,25},{9,1},{17,9},{25,17},{2,26},{10... | collective-permute-start | bytes 503816 | tf_op jit(solution)/shard_map/ppermute | solution.py:355
  32.0 0.0 collective-permute-done.5.refs_1_
  32.0 5.0 %collective-permute-done.6.refs_2_ = s16[656,128]{1,0:T(8,128)(2,1)S(1)} collective-permute-done((s16[656,128]{1,0:T(8,128)(2,1)S(1)}, s16[656,128]{1,0:T(8,128)(2,1)S(1)}, u32[]{:S(2)}, u32[]{:S(2)}) %collective-permute-start.6) | collective-permute-done | bytes 167968 | tf_op jit(solution)/shard_map/ppermute | solution.py:355
  36.9 1.9 %collective-permute-done.7.refs_3_ = s16[656,128]{1,0:T(8,128)(2,1)S(1)} collective-permute-done((s16[656,128]{1,0:T(8,128)(2,1)S(1)}, s16[656,128]{1,0:T(8,128)(2,1)S(1)}, u32[]{:S(2)}, u32[]{:S(2)}) %collective-permute-start.7) | collective-permute-done | bytes 167968 | tf_op jit(solution)/shard_map/ppermute | solution.py:355
  38.8 0.4 %attend.1 = (bf16[64,128]{1,0:T(8,128)(2,1)S(1)}, bf16[64,128]{1,0:T(8,128)(2,1)S(1)}) custom-call(s16[656,128]{1,0:T(8,128)(2,1)S(1)} %get-tuple-element.19.refs_0_, s16[656,128]{1,0:T(8,128)(2,1)S(1)} %collective-permute-done.5.refs_1_, s16[656,128]{1,0:T(8,128)(2,1)S(1)} %collective-permute-done.6.refs_2_, s16[656,128]{1,0:T(8,128)(2,1)S(1)} %collective-permute-done.7.refs_3_), custom_call_target="tpu_custom_call" | custom-call | tf_op jit(solution)/shard_map/attend/pallas_call | solution.py:356
  39.3 1.8 %collective-permute-start.8 = (bf16[64,128]{1,0:T(8,128)(2,1)S(1)}, bf16[64,128]{1,0:T(8,128)(2,1)S(1)}, u32[]{:S(2)}, u32[]{:S(2)}) collective-permute-start(bf16[64,128]{1,0:T(8,128)(2,1)S(1)} %get-tuple-element.23), channel_id=1, source_target_pairs={{0,8},{8,0},{16,24},{24,16},{1,9},{9,1},{17,25},{25,17},{2,10},{10... | collective-permute-start | bytes 49160 | tf_op jit(solution)/shard_map/ppermute | solution.py:369
  41.0 2.0 %collective-permute-done.8 = bf16[64,128]{1,0:T(8,128)(2,1)S(1)} collective-permute-done((bf16[64,128]{1,0:T(8,128)(2,1)S(1)}, bf16[64,128]{1,0:T(8,128)(2,1)S(1)}, u32[]{:S(2)}, u32[]{:S(2)}) %collective-permute-start.8) | collective-permute-done | bytes 16416 | tf_op jit(solution)/shard_map/ppermute | solution.py:369
  43.1 0.6 %pad_maximum_fusion = bf16[64,256]{1,0:T(8,128)(2,1)} fusion(bf16[64,128]{1,0:T(8,128)(2,1)S(1)} %get-tuple-element.26, bf16[64,128]{1,0:T(8,128)(2,1)S(1)} %get-tuple-element.25), kind=kLoop, calls=%fused_computation | loop fusion | flops 65536 | bytes 65536 | tf_op jit(solution)/shard_map/concatenate | solution.py:377
  (1 shorter events, 0.0 us)
Async XLA Ops:
  0.0 3.0 %collective-permute-start = (bf16[256,512]{1,0:T(8,128)(2,1)}, bf16[256,512]{1,0:T(8,128)(2,1)S(1)}, u32[]{:S(2)}, u32[]{:S(2)}) collective-permute-start(bf16[256,512]{1,0:T(8,128)(2,1)} %tokens_ref.1), channel_id=1, source_target_pairs={{0,1},{1,0},{2,3},{3,2},{4,5},{5,4},{6,7},{7,6},{8,9},{9,8},{10,11... | collective-permute-start | bytes 786440 | tf_op jit(solution)/shard_map/ppermute | solution.py:290
  1.1 1.0 %copy-start = (bf16[256,512]{1,0:T(8,128)(2,1)S(1)}, bf16[256,512]{1,0:T(8,128)(2,1)}, u32[]{:S(2)}) copy-start(bf16[256,512]{1,0:T(8,128)(2,1)} %tokens_ref.1) | copy-start | bytes 786436
  2.1 0.7 %copy-start.1 = (s32[128]{0:T(128)S(1)}, s32[128]{0:T(128)}, u32[]{:S(2)}) copy-start(s32[128]{0:T(128)} %param.6) | copy-start | bytes 1540
  3.2 11.9 %collective-permute-start.3 = (bf16[256,512]{1,0:T(8,128)(2,1)S(1)}, bf16[256,512]{1,0:T(8,128)(2,1)S(1)}, u32[]{:S(2)}, u32[]{:S(2)}) collective-permute-start(bf16[256,512]{1,0:T(8,128)(2,1)S(1)} %join.1), channel_id=1, source_target_pairs={{0,4},{1,1},{2,12},{3,9},{4,20},{5,17},{6,28},{7,25},{8,6},{9,3},{... | collective-permute-start | bytes 786440 | tf_op jit(solution)/shard_map/ppermute | solution.py:317
  8.7 9.2 %collective-permute-start.1 = (bf16[256,512]{1,0:T(8,128)(2,1)S(1)}, bf16[256,512]{1,0:T(8,128)(2,1)S(1)}, u32[]{:S(2)}, u32[]{:S(2)}) collective-permute-start(bf16[256,512]{1,0:T(8,128)(2,1)S(1)} %join.1), channel_id=1, source_target_pairs={{0,6},{1,3},{2,14},{3,11},{4,22},{5,19},{6,30},{7,27},{8,0},{9,5},... | collective-permute-start | bytes 786440 | tf_op jit(solution)/shard_map/ppermute | solution.py:317
  15.1 4.3 %collective-permute-start.4 = (bf16[256,512]{1,0:T(8,128)(2,1)S(1)}, bf16[256,512]{1,0:T(8,128)(2,1)S(1)}, u32[]{:S(2)}, u32[]{:S(2)}) collective-permute-start(bf16[256,512]{1,0:T(8,128)(2,1)S(1)} %collective-permute-done.3.refs_0_), channel_id=1, source_target_pairs={{0,1},{1,0},{2,3},{3,2},{4,5},{5,4},{6,7},{7,6},{8,9},{9,8},{10,11... | collective-permute-start | bytes 786440 | tf_op jit(solution)/shard_map/ppermute | solution.py:320
  17.9 2.4 %collective-permute-start.2 = (bf16[256,512]{1,0:T(8,128)(2,1)S(1)}, bf16[256,512]{1,0:T(8,128)(2,1)S(1)}, u32[]{:S(2)}, u32[]{:S(2)}) collective-permute-start(bf16[256,512]{1,0:T(8,128)(2,1)S(1)} %collective-permute-done.1.refs_1_), channel_id=1, source_target_pairs={{0,1},{1,0},{2,3},{3,2},{4,5},{5,4},{6,7},{7,6},{8,9},{9,8},{10,11... | collective-permute-start | bytes 786440 | tf_op jit(solution)/shard_map/ppermute | solution.py:320
  22.2 9.8 %collective-permute-start.5 = (s16[656,128]{1,0:T(8,128)(2,1)S(1)}, s16[656,128]{1,0:T(8,128)(2,1)S(1)}, u32[]{:S(2)}, u32[]{:S(2)}) collective-permute-start(s16[656,128]{1,0:T(8,128)(2,1)S(1)} %get-tuple-element.20), channel_id=1, source_target_pairs={{0,8},{8,16},{16,24},{24,0},{1,9},{9,17},{17,25},{25,1},{2,10},{10... | collective-permute-start | bytes 503816 | tf_op jit(solution)/shard_map/ppermute | solution.py:355
  26.2 10.8 %collective-permute-start.6 = (s16[656,128]{1,0:T(8,128)(2,1)S(1)}, s16[656,128]{1,0:T(8,128)(2,1)S(1)}, u32[]{:S(2)}, u32[]{:S(2)}) collective-permute-start(s16[656,128]{1,0:T(8,128)(2,1)S(1)} %get-tuple-element.21), channel_id=1, source_target_pairs={{0,16},{8,24},{16,0},{24,8},{1,17},{9,25},{17,1},{25,9},{2,18},{10... | collective-permute-start | bytes 503816 | tf_op jit(solution)/shard_map/ppermute | solution.py:355
  29.1 9.7 %collective-permute-start.7 = (s16[656,128]{1,0:T(8,128)(2,1)S(1)}, s16[656,128]{1,0:T(8,128)(2,1)S(1)}, u32[]{:S(2)}, u32[]{:S(2)}) collective-permute-start(s16[656,128]{1,0:T(8,128)(2,1)S(1)} %get-tuple-element.22), channel_id=1, source_target_pairs={{0,24},{8,0},{16,8},{24,16},{1,25},{9,1},{17,9},{25,17},{2,26},{10... | collective-permute-start | bytes 503816 | tf_op jit(solution)/shard_map/ppermute | solution.py:355
  39.3 3.8 %collective-permute-start.8 = (bf16[64,128]{1,0:T(8,128)(2,1)S(1)}, bf16[64,128]{1,0:T(8,128)(2,1)S(1)}, u32[]{:S(2)}, u32[]{:S(2)}) collective-permute-start(bf16[64,128]{1,0:T(8,128)(2,1)S(1)} %get-tuple-element.23), channel_id=1, source_target_pairs={{0,8},{8,0},{16,24},{24,16},{1,9},{9,1},{17,25},{25,17},{2,10},{10... | collective-permute-start | bytes 49160 | tf_op jit(solution)/shard_map/ppermute | solution.py:369

commit v6 on v4

--- a/solution.py
+++ b/solution.py
@@ -94,7 +94,7 @@
 def gather(tokens, keep_list, counts):
     slots = keep_list.shape[0]
     token = lax.broadcasted_iota(jnp.int32, (tokens.shape[0], slots), 0)
-    pick = (token == keep_list[None, :]).astype(jnp.bfloat16)
+    pick = lax.optimization_barrier((token == keep_list[None, :]).astype(jnp.bfloat16))
     rows = lax.dot_general(pick, tokens, (((0,), (0,)), ((), ())), preferred_element_type=jnp.float32)
     last = lax.broadcasted_iota(jnp.int32, rows.shape, 0) == slots - 1
     return jnp.where(last, counts[0].astype(jnp.float32), rows).astype(jnp.bfloat16)
@@ -119,7 +119,7 @@
     core = lax.rem(tp, group)
     line = lax.div(tp, group)
     stride = core_stride(shards, group)
-    shard = [lax.rem(line - k - core * stride + 2 * shards, shards) for k in range(shards)]
+    shard = [lax.rem(k + core * stride - line + shards, shards) for k in range(shards)]
     count = [chunks[k][slots - 1 : slots, :slots].astype(jnp.float32) for k in range(shards)]
     row = lax.broadcasted_iota(jnp.int32, (kept, slots), 0)
     rank = ((row % capacity) * shards + row // capacity).astype(jnp.float32)
@@ -178,34 +178,37 @@
         most = jnp.maximum(jnp.max(jnp.abs(acc), axis=0, keepdims=True), 2.0**-100)
         exponent = jnp.floor(jnp.log2(most)) + 1.0
         exponents.append(exponent)
-        value = jnp.round(acc * jnp.exp2(TOP_BITS - exponent)).astype(jnp.int32).astype(jnp.int16)
-        for k in range(shards):
-            dest = lax.rem(me + k, shards)
-            for head in range(heads):
-                mine = value[:, head * HD : (head + 1) * HD]
-                if kind:
-
-                    @pl.when(lax.rem(dest, heads) == head)
-                    def _(k=k, at=at, mine=mine):
-                        outs[k][at * kept : (at + 1) * kept, :] = mine
-                else:
-                    for b in range(blocks):
-
-                        @pl.when(dest == b * heads + head)
-                        def _(k=k, b=b, mine=mine):
-                            outs[k][2 * kept : total, :] = mine[b * block_rows : (b + 1) * block_rows, :]
-
-    index = lax.broadcasted_iota(jnp.int32, (pad, HD), 0)
-    for head in range(heads):
-        tail = jnp.zeros((pad, HD), jnp.float32)
-        for at, exponent in enumerate(exponents):
-            tail = jnp.where(index == at, exponent[:, head * HD : (head + 1) * HD], tail)
-        tail = tail.astype(jnp.int32).astype(jnp.int16)
-        for k in range(shards):
-
-            @pl.when(lax.rem(lax.rem(me + k, shards), heads) == head)
-            def _(k=k, tail=tail):
-                outs[k][total:, :] = tail
+        value = jnp.round(acc * jnp.exp2(TOP_BITS - exponent)).astype(jnp.int32)
+        for r in range(heads):
+            mine = of_head(value, lax.rem(me + r, heads), heads)
+            if kind:
+                mine = mine.astype(jnp.int16)
+                for k in range(r, shards, heads):
+                    outs[k][at * kept : (at + 1) * kept, :] = mine
+            else:
+                for k in range(r, shards, heads):
+                    block = lax.div(lax.rem(me + k, shards), heads)
+                    part = mine[:block_rows, :]
+                    for b in range(1, blocks):
+                        part = jnp.where(block == b, mine[b * block_rows : (b + 1) * block_rows, :], part)
+                    outs[k][2 * kept : total, :] = part.astype(jnp.int16)
+
+    index = lax.broadcasted_iota(jnp.int32, (pad, heads * HD), 0)
+    tail = jnp.zeros((pad, heads * HD), jnp.float32)
+    for at, exponent in enumerate(exponents):
+        tail = jnp.where(index == at, exponent, tail)
+    tail = tail.astype(jnp.int32)
+    for r in range(heads):
+        mine = of_head(tail, lax.rem(me + r, heads), heads).astype(jnp.int16)
+        for k in range(r, shards, heads):
+            outs[k][total:, :] = mine
+
+
+def of_head(value, head, heads):
+    mine = value[:, :HD]
+    for h in range(1, heads):
+        mine = jnp.where(head == h, value[:, h * HD : (h + 1) * HD], mine)
+    return mine
 
 
 def attend_kernel(shards, heads, kept, *refs):
@@ -238,15 +241,14 @@
     top = jnp.max(scores, axis=1, keepdims=True)
     expo = jnp.exp(scores - top)
     numer = jnp.dot(expo.astype(jnp.bfloat16), value, preferred_element_type=jnp.float32)
-    result = (numer / jnp.sum(expo, axis=1, keepdims=True)).astype(jnp.bfloat16)
+    result = numer / jnp.sum(expo, axis=1, keepdims=True)
     head = lax.rem(me, heads)
     for k in range(heads):
         owner = lax.rem(head + k, heads)
-        for o in range(heads):
-
-            @pl.when(owner == o)
-            def _(k=k, o=o):
-                outs[k][...] = result[o * capacity : (o + 1) * capacity, :]
+        piece = result[:capacity, :]
+        for o in range(1, heads):
+            piece = jnp.where(owner == o, result[o * capacity : (o + 1) * capacity, :], piece)
+        outs[k][...] = piece.astype(jnp.bfloat16)
 
 
 def by_features(shards, tp, tokens, w_qkv, keep_list, counts):
@@ -267,7 +269,7 @@
     own = []
     for k in range(shards):
         pairs = [
-            (device(s, line, c), device(line, (s + k + c * stride) % shards, c))
+            (device(s, line, c), device(line, (k + c * stride - s) % shards, c))
             for s, line, c in every
         ]
         own.append(lax.ppermute(packed, axes, pairs))

time: 43.1 us -> 41.2 us (0.956)
  starting transfers between devices: 21.6 us -> 18.2 us
  waiting for transfers between devices: 14.8 us -> 17.2 us
  other arithmetic: 0.63 us -> 1.35 us
  Pallas kernels: 3.92 us -> 3.24 us
  matrix products: 0.88 us -> 0.21 us
    ppermute x4, starting transfers between devices: 14.2 us -> 11.8 us  [by_features(): own.append(lax.ppermute(packed, axes, pairs))]
    ppermute x4, waiting for transfers between devices: 3.73 us -> 5.99 us  [by_features(): own.append(lax.ppermute(packed, axes, pairs))]
    convert_element_type x0 -> x1, other arithmetic: none -> 0.72 us  [gather(): (token == keep_list[None, :]).astype(jnp.bfloat16)]
    ppermute x1, starting transfers between devices: 0.77 us -> 0.07 us  [by_features(): arrived.append(lax.ppermute(pieces[k], 'seq', pairs))]
    ppermute x1, waiting for transfers between devices: 3.03 us -> 3.72 us  [by_features(): arrived.append(lax.ppermute(pieces[k], 'seq', pairs))]
    dot_general x1, matrix products: 0.88 us -> 0.21 us  [gather(): lax.dot_general(pick, tokens, (((0,), (0,)), ((), ())), preferred_element...]
    pallas_call x1, Pallas kernels: 1.41 us -> 0.74 us  [by_features(): pl.pallas_call(functools.partial(rest_kernel, shards, group, heads), out_...]
    ppermute x3, waiting for transfers between devices: 7.99 us -> 7.51 us  [by_features(): parts.append(lax.ppermute(partial[k], 'seq', pairs))]
where the time goes in v6:
time: 41.2 us; the launch traced here: 41 us
  starting transfers between devices  18.2 us (44%)
  waiting for transfers between devices  17.2 us (42%)
  Pallas kernels  3.24 us (8%)
  other arithmetic  1.35 us (3%)
  between operations  0.8 us (2%)
    ppermute x4, starting transfers between devices, by_features(): own.append(lax.ppermute(packed, axes, pairs))  11.8 us
    ppermute x3, waiting for transfers between devices, by_features(): parts.append(lax.ppermute(partial[k], 'seq', pairs))  7.51 us
    ppermute x4, waiting for transfers between devices, by_features(): own.append(lax.ppermute(packed, axes, pairs))  5.99 us
    ppermute x3, starting transfers between devices, by_features(): parts.append(lax.ppermute(partial[k], 'seq', pairs))  5.72 us
    ppermute x1, waiting for transfers between devices, by_features(): arrived.append(lax.ppermute(pieces[k], 'seq', pairs))  3.72 us
    pallas_call x1, Pallas kernels, by_features(): pl.pallas_call(load_kernel, out_shape=jax.ShapeDtypeStruct(weights.shape,...  1.42 us
  transfers between devices with their start and end apart: 12, of which 6 were waited for; matrix products, arithmetic and copies ran while one was open for 0% of the time, Pallas kernels for 5%

profile of v6, /device:TPU:0, one launch (start us, length us, event | category | flops | bytes accessed | tf_op | source)
XLA Modules:
  0.0 41.0 jit_solution(14145465370037904971)
XLA Ops:
  0.0 0.0 copy-start
  0.0 0.7 %fusion.1 = bf16[256,128]{1,0:T(8,128)(2,1)S(1)} fusion(s32[128]{0:T(128)} %param.6), kind=kLoop, calls=%fused_computation.3 | loop fusion | flops 65536 | bytes 66048 | tf_op jit(solution)/shard_map/convert_element_type | solution.py:97
  1.4 0.2 fusion
  1.6 0.7 %collective-permute-start = (bf16[128,512]{1,0:T(8,128)(2,1)S(1)}, bf16[128,512]{1,0:T(8,128)(2,1)S(1)}, u32[]{:S(2)}, u32[]{:S(2)}) collective-permute-start(bf16[128,512]{1,0:T(8,128)(2,1)S(1)} %fusion), channel_id=1, source_target_pairs={{0,0},{1,5},{2,8},{3,13},{4,16},{5,21},{6,24},{7,29},{8,6},{9,3},{... | collective-permute-start | bytes 393224 | tf_op jit(solution)/shard_map/ppermute | solution.py:275
  2.3 5.7 %collective-permute-start.2 = (bf16[128,512]{1,0:T(8,128)(2,1)S(1)}, bf16[128,512]{1,0:T(8,128)(2,1)S(1)}, u32[]{:S(2)}, u32[]{:S(2)}) collective-permute-start(bf16[128,512]{1,0:T(8,128)(2,1)S(1)} %fusion), channel_id=1, source_target_pairs={{0,2},{1,7},{2,10},{3,15},{4,18},{5,23},{6,26},{7,31},{8,0},{9,5},... | collective-permute-start | bytes 393224 | tf_op jit(solution)/shard_map/ppermute | solution.py:275
  8.0 5.4 %collective-permute-start.4 = (bf16[128,512]{1,0:T(8,128)(2,1)S(1)}, bf16[128,512]{1,0:T(8,128)(2,1)S(1)}, u32[]{:S(2)}, u32[]{:S(2)}) collective-permute-start(bf16[128,512]{1,0:T(8,128)(2,1)S(1)} %fusion), channel_id=1, source_target_pairs={{0,4},{1,1},{2,12},{3,9},{4,20},{5,17},{6,28},{7,25},{8,2},{9,7},{... | collective-permute-start | bytes 393224 | tf_op jit(solution)/shard_map/ppermute | solution.py:275
  13.4 0.1 collective-permute-start.6
  13.5 0.0 collective-permute-done.refs_0_
  13.5 0.1 collective-permute-start.1
  13.6 0.0 collective-permute-done.2.refs_1_
  13.6 0.5 %collective-permute-start.3 = (bf16[128,512]{1,0:T(8,128)(2,1)S(1)}, bf16[128,512]{1,0:T(8,128)(2,1)S(1)}, u32[]{:S(2)}, u32[]{:S(2)}) collective-permute-start(bf16[128,512]{1,0:T(8,128)(2,1)S(1)} %collective-permute-done.2.refs_1_), channel_id=1, source_target_pairs={{1,0},{0,1},{3,2},{2,3},{5,4},{4,5},{7,6},{6,7},{9,8},{8,9},{11,10... | collective-permute-start | bytes 393224 | tf_op jit(solution)/shard_map/ppermute | solution.py:284
  14.1 3.0 %collective-permute-done.4.refs_2_ = bf16[128,512]{1,0:T(8,128)(2,1)S(1)} collective-permute-done((bf16[128,512]{1,0:T(8,128)(2,1)S(1)}, bf16[128,512]{1,0:T(8,128)(2,1)S(1)}, u32[]{:S(2)}, u32[]{:S(2)}) %collective-permute-start.4) | collective-permute-done | bytes 131104 | tf_op jit(solution)/shard_map/ppermute | solution.py:275
  17.1 0.0 collective-permute-start.5
  17.1 3.0 %collective-permute-done.6.refs_3_ = bf16[128,512]{1,0:T(8,128)(2,1)S(1)} collective-permute-done((bf16[128,512]{1,0:T(8,128)(2,1)S(1)}, bf16[128,512]{1,0:T(8,128)(2,1)S(1)}, u32[]{:S(2)}, u32[]{:S(2)}) %collective-permute-start.6) | collective-permute-done | bytes 131104 | tf_op jit(solution)/shard_map/ppermute | solution.py:275
  20.1 0.0 collective-permute-start.7
  20.1 1.4 %load.1.refs_4_.refs_6_ = bf16[3,1024,256]{2,1,0:T(8,128)(2,1)S(1)} custom-call(bf16[3,1024,256]{2,1,0:T(8,128)(2,1)} %bitcast.4), custom_call_target="tpu_custom_call" | custom-call | tf_op jit(solution)/shard_map/load/pallas_call | solution.py:286
  21.5 0.7 %own.1 = (bf16[256,512]{1,0:T(8,128)(2,1)S(1)}, f32[3,256,256]{2,1,0:T(8,128)S(1)}) custom-call(bf16[128,512]{1,0:T(8,128)(2,1)S(1)} %collective-permute-done.refs_0_, bf16[128,512]{1,0:T(8,128)(2,1)S(1)} %collective-permute-done.2.refs_1_, bf16[128,512]{1,0:T(8,128)(2,1)S(1)} %collective-permute-done.4.refs_2_, ...), custom_call_target="tpu_custom_call" | custom-call | tf_op jit(solution)/shard_map/own/pallas_call | solution.py:295
  22.1 0.0 collective-permute-done.1.refs_0_
  22.2 0.0 collective-permute-done.3.refs_1_
  22.2 0.0 collective-permute-done.5.refs_2_
  22.2 0.0 collective-permute-done.7.refs_3_
  22.2 0.7 %rest.1 = (s16[656,128]{1,0:T(8,128)(2,1)S(1)}, s16[656,128]{1,0:T(8,128)(2,1)S(1)}, s16[656,128]{1,0:T(8,128)(2,1)S(1)}, s16[656,128]{1,0:T(8,128)(2,1)S(1)}) custom-call(bf16[128,512]{1,0:T(8,128)(2,1)S(1)} %collective-permute-done.1.refs_0_, bf16[128,512]{1,0:T(8,128)(2,1)S(1)} %collective-permute-done.3.refs_1_, ...), custom_call_target="tpu_custom_call" | custom-call | tf_op jit(solution)/shard_map/rest/pallas_call | solution.py:308
  22.9 2.7 %collective-permute-start.10 = (s16[656,128]{1,0:T(8,128)(2,1)S(1)}, s16[656,128]{1,0:T(8,128)(2,1)S(1)}, u32[]{:S(2)}, u32[]{:S(2)}) collective-permute-start(s16[656,128]{1,0:T(8,128)(2,1)S(1)} %get-tuple-element.18), channel_id=1, source_target_pairs={{0,24},{8,0},{16,8},{24,16},{1,25},{9,1},{17,9},{25,17},{2,26},{10... | collective-permute-start | bytes 503816 | tf_op jit(solution)/shard_map/ppermute | solution.py:319
  25.6 0.0 collective-permute-start.8
  25.7 3.0 %collective-permute-start.9 = (s16[656,128]{1,0:T(8,128)(2,1)S(1)}, s16[656,128]{1,0:T(8,128)(2,1)S(1)}, u32[]{:S(2)}, u32[]{:S(2)}) collective-permute-start(s16[656,128]{1,0:T(8,128)(2,1)S(1)} %get-tuple-element.17), channel_id=1, source_target_pairs={{0,16},{8,24},{16,0},{24,8},{1,17},{9,25},{17,1},{25,9},{2,18},{10... | collective-permute-start | bytes 503816 | tf_op jit(solution)/shard_map/ppermute | solution.py:319
  28.7 1.7 %collective-permute-done.10.refs_3_ = s16[656,128]{1,0:T(8,128)(2,1)S(1)} collective-permute-done((s16[656,128]{1,0:T(8,128)(2,1)S(1)}, s16[656,128]{1,0:T(8,128)(2,1)S(1)}, u32[]{:S(2)}, u32[]{:S(2)}) %collective-permute-start.10) | collective-permute-done | bytes 167968 | tf_op jit(solution)/shard_map/ppermute | solution.py:319
  30.3 5.6 %collective-permute-done.8.refs_1_ = s16[656,128]{1,0:T(8,128)(2,1)S(1)} collective-permute-done((s16[656,128]{1,0:T(8,128)(2,1)S(1)}, s16[656,128]{1,0:T(8,128)(2,1)S(1)}, u32[]{:S(2)}, u32[]{:S(2)}) %collective-permute-start.8) | collective-permute-done | bytes 167968 | tf_op jit(solution)/shard_map/ppermute | solution.py:319
  36.0 0.2 collective-permute-done.9.refs_2_
  36.2 0.4 %attend.1 = (bf16[64,128]{1,0:T(8,128)(2,1)S(1)}, bf16[64,128]{1,0:T(8,128)(2,1)S(1)}) custom-call(s16[656,128]{1,0:T(8,128)(2,1)S(1)} %get-tuple-element.15.refs_0_, s16[656,128]{1,0:T(8,128)(2,1)S(1)} %collective-permute-done.8.refs_1_, s16[656,128]{1,0:T(8,128)(2,1)S(1)} %collective-permute-done.9.refs_2_, s16[656,128]{1,0:T(8,128)(2,1)S(1)} %collective-permute-done.10.refs_3_), custom_call_target="tpu_custom_call" | custom-call | tf_op jit(solution)/shard_map/attend/pallas_call | solution.py:320
  36.6 0.1 collective-permute-start.11
  36.7 3.7 %collective-permute-done.11 = bf16[64,128]{1,0:T(8,128)(2,1)S(1)} collective-permute-done((bf16[64,128]{1,0:T(8,128)(2,1)S(1)}, bf16[64,128]{1,0:T(8,128)(2,1)S(1)}, u32[]{:S(2)}, u32[]{:S(2)}) %collective-permute-start.11) | collective-permute-done | bytes 16416 | tf_op jit(solution)/shard_map/ppermute | solution.py:333
  40.4 0.6 %pad_maximum_fusion = bf16[64,256]{1,0:T(8,128)(2,1)} fusion(bf16[64,128]{1,0:T(8,128)(2,1)S(1)} %get-tuple-element.22, bf16[64,128]{1,0:T(8,128)(2,1)S(1)} %get-tuple-element.21), kind=kLoop, calls=%fused_computation.4 | loop fusion | flops 65536 | bytes 65536 | tf_op jit(solution)/shard_map/concatenate | solution.py:341
  (3 shorter events, 0.0 us)
Async XLA Ops:
  0.0 1.4 %copy-start = (bf16[256,512]{1,0:T(8,128)(2,1)S(1)}, bf16[256,512]{1,0:T(8,128)(2,1)}, u32[]{:S(2)}) copy-start(bf16[256,512]{1,0:T(8,128)(2,1)} %param.4) | copy-start | bytes 786436
  1.6 11.9 %collective-permute-start = (bf16[128,512]{1,0:T(8,128)(2,1)S(1)}, bf16[128,512]{1,0:T(8,128)(2,1)S(1)}, u32[]{:S(2)}, u32[]{:S(2)}) collective-permute-start(bf16[128,512]{1,0:T(8,128)(2,1)S(1)} %fusion), channel_id=1, source_target_pairs={{0,0},{1,5},{2,8},{3,13},{4,16},{5,21},{6,24},{7,29},{8,6},{9,3},{... | collective-permute-start | bytes 393224 | tf_op jit(solution)/shard_map/ppermute | solution.py:275
  2.3 11.3 %collective-permute-start.2 = (bf16[128,512]{1,0:T(8,128)(2,1)S(1)}, bf16[128,512]{1,0:T(8,128)(2,1)S(1)}, u32[]{:S(2)}, u32[]{:S(2)}) collective-permute-start(bf16[128,512]{1,0:T(8,128)(2,1)S(1)} %fusion), channel_id=1, source_target_pairs={{0,2},{1,7},{2,10},{3,15},{4,18},{5,23},{6,26},{7,31},{8,0},{9,5},... | collective-permute-start | bytes 393224 | tf_op jit(solution)/shard_map/ppermute | solution.py:275
  8.0 9.1 %collective-permute-start.4 = (bf16[128,512]{1,0:T(8,128)(2,1)S(1)}, bf16[128,512]{1,0:T(8,128)(2,1)S(1)}, u32[]{:S(2)}, u32[]{:S(2)}) collective-permute-start(bf16[128,512]{1,0:T(8,128)(2,1)S(1)} %fusion), channel_id=1, source_target_pairs={{0,4},{1,1},{2,12},{3,9},{4,20},{5,17},{6,28},{7,25},{8,2},{9,7},{... | collective-permute-start | bytes 393224 | tf_op jit(solution)/shard_map/ppermute | solution.py:275
  13.4 6.6 %collective-permute-start.6 = (bf16[128,512]{1,0:T(8,128)(2,1)S(1)}, bf16[128,512]{1,0:T(8,128)(2,1)S(1)}, u32[]{:S(2)}, u32[]{:S(2)}) collective-permute-start(bf16[128,512]{1,0:T(8,128)(2,1)S(1)} %fusion), channel_id=1, source_target_pairs={{0,6},{1,3},{2,14},{3,11},{4,22},{5,19},{6,30},{7,27},{8,4},{9,1},... | collective-permute-start | bytes 393224 | tf_op jit(solution)/shard_map/ppermute | solution.py:275
  13.5 8.7 %collective-permute-start.1 = (bf16[128,512]{1,0:T(8,128)(2,1)S(1)}, bf16[128,512]{1,0:T(8,128)(2,1)S(1)}, u32[]{:S(2)}, u32[]{:S(2)}) collective-permute-start(bf16[128,512]{1,0:T(8,128)(2,1)S(1)} %collective-permute-done.refs_0_), channel_id=1, source_target_pairs={{1,0},{0,1},{3,2},{2,3},{5,4},{4,5},{7,6},{6,7},{9,8},{8,9},{11,10... | collective-permute-start | bytes 393224 | tf_op jit(solution)/shard_map/ppermute | solution.py:284
  13.6 8.6 %collective-permute-start.3 = (bf16[128,512]{1,0:T(8,128)(2,1)S(1)}, bf16[128,512]{1,0:T(8,128)(2,1)S(1)}, u32[]{:S(2)}, u32[]{:S(2)}) collective-permute-start(bf16[128,512]{1,0:T(8,128)(2,1)S(1)} %collective-permute-done.2.refs_1_), channel_id=1, source_target_pairs={{1,0},{0,1},{3,2},{2,3},{5,4},{4,5},{7,6},{6,7},{9,8},{8,9},{11,10... | collective-permute-start | bytes 393224 | tf_op jit(solution)/shard_map/ppermute | solution.py:284
  17.1 5.1 %collective-permute-start.5 = (bf16[128,512]{1,0:T(8,128)(2,1)S(1)}, bf16[128,512]{1,0:T(8,128)(2,1)S(1)}, u32[]{:S(2)}, u32[]{:S(2)}) collective-permute-start(bf16[128,512]{1,0:T(8,128)(2,1)S(1)} %collective-permute-done.4.refs_2_), channel_id=1, source_target_pairs={{1,0},{0,1},{3,2},{2,3},{5,4},{4,5},{7,6},{6,7},{9,8},{8,9},{11,10... | collective-permute-start | bytes 393224 | tf_op jit(solution)/shard_map/ppermute | solution.py:284
  20.1 2.1 %collective-permute-start.7 = (bf16[128,512]{1,0:T(8,128)(2,1)S(1)}, bf16[128,512]{1,0:T(8,128)(2,1)S(1)}, u32[]{:S(2)}, u32[]{:S(2)}) collective-permute-start(bf16[128,512]{1,0:T(8,128)(2,1)S(1)} %collective-permute-done.6.refs_3_), channel_id=1, source_target_pairs={{1,0},{0,1},{3,2},{2,3},{5,4},{4,5},{7,6},{6,7},{9,8},{8,9},{11,10... | collective-permute-start | bytes 393224 | tf_op jit(solution)/shard_map/ppermute | solution.py:284
  22.9 7.4 %collective-permute-start.10 = (s16[656,128]{1,0:T(8,128)(2,1)S(1)}, s16[656,128]{1,0:T(8,128)(2,1)S(1)}, u32[]{:S(2)}, u32[]{:S(2)}) collective-permute-start(s16[656,128]{1,0:T(8,128)(2,1)S(1)} %get-tuple-element.18), channel_id=1, source_target_pairs={{0,24},{8,0},{16,8},{24,16},{1,25},{9,1},{17,9},{25,17},{2,26},{10... | collective-permute-start | bytes 503816 | tf_op jit(solution)/shard_map/ppermute | solution.py:319
  25.6 10.3 %collective-permute-start.8 = (s16[656,128]{1,0:T(8,128)(2,1)S(1)}, s16[656,128]{1,0:T(8,128)(2,1)S(1)}, u32[]{:S(2)}, u32[]{:S(2)}) collective-permute-start(s16[656,128]{1,0:T(8,128)(2,1)S(1)} %get-tuple-element.16), channel_id=1, source_target_pairs={{0,8},{8,16},{16,24},{24,0},{1,9},{9,17},{17,25},{25,1},{2,10},{10... | collective-permute-start | bytes 503816 | tf_op jit(solution)/shard_map/ppermute | solution.py:319
  25.7 10.5 %collective-permute-start.9 = (s16[656,128]{1,0:T(8,128)(2,1)S(1)}, s16[656,128]{1,0:T(8,128)(2,1)S(1)}, u32[]{:S(2)}, u32[]{:S(2)}) collective-permute-start(s16[656,128]{1,0:T(8,128)(2,1)S(1)} %get-tuple-element.17), channel_id=1, source_target_pairs={{0,16},{8,24},{16,0},{24,8},{1,17},{9,25},{17,1},{25,9},{2,18},{10... | collective-permute-start | bytes 503816 | tf_op jit(solution)/shard_map/ppermute | solution.py:319
  36.6 3.8 %collective-permute-start.11 = (bf16[64,128]{1,0:T(8,128)(2,1)S(1)}, bf16[64,128]{1,0:T(8,128)(2,1)S(1)}, u32[]{:S(2)}, u32[]{:S(2)}) collective-permute-start(bf16[64,128]{1,0:T(8,128)(2,1)S(1)} %get-tuple-element.19), channel_id=1, source_target_pairs={{0,8},{8,0},{16,24},{24,16},{1,9},{9,1},{17,25},{25,17},{2,10},{10... | collective-permute-start | bytes 49160 | tf_op jit(solution)/shard_map/ppermute | solution.py:333

commit v7 on v6

--- a/solution.py
+++ b/solution.py
@@ -108,6 +108,14 @@
 
 def core_stride(shards, group):
     return shards // group if shards % group == 0 else 0
+
+
+def toward(me, k, shards):
+    return me ^ k if shards & (shards - 1) == 0 else (me + k) % shards
+
+
+def step(j, core, shards):
+    return shards - j if j and core % 2 else j
 
 
 def own_kernel(shards, group, *refs):
@@ -167,6 +175,12 @@
         rows.append(jnp.dot(pick, block, preferred_element_type=jnp.float32).astype(jnp.bfloat16))
     total = 2 * kept + block_rows
     pad = outs[0].shape[0] - total
+    dests = [me]
+    for k in range(1, shards):
+        dest = toward(me, step(k, 0, shards), shards)
+        for c in range(1, group):
+            dest = jnp.where(core == c, toward(me, step(k, c, shards), shards), dest)
+        dests.append(dest)
     exponents = []
     for at, kind in enumerate((1, 2, 0)):
         acc = acc_ref[kind]
@@ -179,29 +193,24 @@
         exponent = jnp.floor(jnp.log2(most)) + 1.0
         exponents.append(exponent)
         value = jnp.round(acc * jnp.exp2(TOP_BITS - exponent)).astype(jnp.int32)
-        for r in range(heads):
-            mine = of_head(value, lax.rem(me + r, heads), heads)
+        for k, dest in enumerate(dests):
+            mine = of_head(value, lax.rem(dest, heads), heads)
             if kind:
-                mine = mine.astype(jnp.int16)
-                for k in range(r, shards, heads):
-                    outs[k][at * kept : (at + 1) * kept, :] = mine
+                outs[k][at * kept : (at + 1) * kept, :] = mine.astype(jnp.int16)
             else:
-                for k in range(r, shards, heads):
-                    block = lax.div(lax.rem(me + k, shards), heads)
-                    part = mine[:block_rows, :]
-                    for b in range(1, blocks):
-                        part = jnp.where(block == b, mine[b * block_rows : (b + 1) * block_rows, :], part)
-                    outs[k][2 * kept : total, :] = part.astype(jnp.int16)
+                block = lax.div(dest, heads)
+                part = mine[:block_rows, :]
+                for b in range(1, blocks):
+                    part = jnp.where(block == b, mine[b * block_rows : (b + 1) * block_rows, :], part)
+                outs[k][2 * kept : total, :] = part.astype(jnp.int16)
 
     index = lax.broadcasted_iota(jnp.int32, (pad, heads * HD), 0)
     tail = jnp.zeros((pad, heads * HD), jnp.float32)
     for at, exponent in enumerate(exponents):
         tail = jnp.where(index == at, exponent, tail)
     tail = tail.astype(jnp.int32)
-    for r in range(heads):
-        mine = of_head(tail, lax.rem(me + r, heads), heads).astype(jnp.int16)
-        for k in range(r, shards, heads):
-            outs[k][total:, :] = mine
+    for k, dest in enumerate(dests):
+        outs[k][total:, :] = of_head(tail, lax.rem(dest, heads), heads).astype(jnp.int16)
 
 
 def of_head(value, head, heads):
@@ -315,8 +324,11 @@
     )(*others, pick, acc, weights)
     parts = [partial[0]]
     for k in range(1, shards):
-        pairs = [(s, (s + k) % shards) for s in range(shards)]
-        parts.append(lax.ppermute(partial[k], "seq", pairs))
+        pairs = [
+            (device(s, line, c), device(toward(s, step(k, c, shards), shards), line, c))
+            for s, line, c in every
+        ]
+        parts.append(lax.ppermute(partial[k], ("seq", "tp"), pairs))
     pieces = pl.pallas_call(
         functools.partial(attend_kernel, shards, heads, kept),
         out_shape=[jax.ShapeDtypeStruct((capacity, HD), jnp.bfloat16)] * heads,

time: 41.2 us -> 40.6 us (0.985)
  waiting for transfers between devices: 17.2 us -> 15.5 us
  starting transfers between devices: 18.2 us -> 19.4 us
    ppermute x1, starting transfers between devices: 0.07 us -> 1.79 us  [by_features(): arrived.append(lax.ppermute(pieces[k], 'seq', pairs))]
    ppermute x1, waiting for transfers between devices: 3.72 us -> 2.02 us  [by_features(): arrived.append(lax.ppermute(pieces[k], 'seq', pairs))]
    ppermute x3, starting transfers between devices: 5.72 us -> 5.17 us  [by_features(): parts.append(lax.ppermute(partial[k], ('seq', 'tp'), pairs))]
where the time goes in v7:
time: 40.6 us; the launch traced here: 40.4 us
  starting transfers between devices  19.4 us (48%)
  waiting for transfers between devices  15.5 us (38%)
  Pallas kernels  3.25 us (8%)
  other arithmetic  1.35 us (3%)
  between operations  0.79 us (2%)
    ppermute x4, starting transfers between devices, by_features(): own.append(lax.ppermute(packed, axes, pairs))  11.8 us
    ppermute x3, waiting for transfers between devices, by_features(): parts.append(lax.ppermute(partial[k], ('seq', 'tp'), pairs))  7.45 us
    ppermute x4, waiting for transfers between devices, by_features(): own.append(lax.ppermute(packed, axes, pairs))  5.99 us
    ppermute x3, starting transfers between devices, by_features(): parts.append(lax.ppermute(partial[k], ('seq', 'tp'), pairs))  5.17 us
    ppermute x1, waiting for transfers between devices, by_features(): arrived.append(lax.ppermute(pieces[k], 'seq', pairs))  2.02 us
    ppermute x1, starting transfers between devices, by_features(): arrived.append(lax.ppermute(pieces[k], 'seq', pairs))  1.79 us
    pallas_call x1, Pallas kernels, by_features(): pl.pallas_call(load_kernel, out_shape=jax.ShapeDtypeStruct(weights.shape,...  1.42 us
  transfers between devices with their start and end apart: 12, of which 6 were waited for; matrix products, arithmetic and copies ran while one was open for 0% of the time, Pallas kernels for 5%

profile of v7, /device:TPU:0, one launch (start us, length us, event | category | flops | bytes accessed | tf_op | source)
XLA Modules:
  0.0 40.4 jit_solution(14448235778362918795)
XLA Ops:
  0.0 0.0 copy-start
  0.0 0.7 %fusion.1 = bf16[256,128]{1,0:T(8,128)(2,1)S(1)} fusion(s32[128]{0:T(128)} %param.6), kind=kLoop, calls=%fused_computation.3 | loop fusion | flops 65536 | bytes 66048 | tf_op jit(solution)/shard_map/convert_element_type | solution.py:97
  1.4 0.2 fusion
  1.6 0.7 %collective-permute-start = (bf16[128,512]{1,0:T(8,128)(2,1)S(1)}, bf16[128,512]{1,0:T(8,128)(2,1)S(1)}, u32[]{:S(2)}, u32[]{:S(2)}) collective-permute-start(bf16[128,512]{1,0:T(8,128)(2,1)S(1)} %fusion), channel_id=1, source_target_pairs={{0,0},{1,5},{2,8},{3,13},{4,16},{5,21},{6,24},{7,29},{8,6},{9,3},{... | collective-permute-start | bytes 393224 | tf_op jit(solution)/shard_map/ppermute | solution.py:284
  2.3 5.7 %collective-permute-start.2 = (bf16[128,512]{1,0:T(8,128)(2,1)S(1)}, bf16[128,512]{1,0:T(8,128)(2,1)S(1)}, u32[]{:S(2)}, u32[]{:S(2)}) collective-permute-start(bf16[128,512]{1,0:T(8,128)(2,1)S(1)} %fusion), channel_id=1, source_target_pairs={{0,2},{1,7},{2,10},{3,15},{4,18},{5,23},{6,26},{7,31},{8,0},{9,5},... | collective-permute-start | bytes 393224 | tf_op jit(solution)/shard_map/ppermute | solution.py:284
  8.0 5.4 %collective-permute-start.4 = (bf16[128,512]{1,0:T(8,128)(2,1)S(1)}, bf16[128,512]{1,0:T(8,128)(2,1)S(1)}, u32[]{:S(2)}, u32[]{:S(2)}) collective-permute-start(bf16[128,512]{1,0:T(8,128)(2,1)S(1)} %fusion), channel_id=1, source_target_pairs={{0,4},{1,1},{2,12},{3,9},{4,20},{5,17},{6,28},{7,25},{8,2},{9,7},{... | collective-permute-start | bytes 393224 | tf_op jit(solution)/shard_map/ppermute | solution.py:284
  13.4 0.1 collective-permute-start.6
  13.5 0.0 collective-permute-done.refs_0_
  13.5 0.1 collective-permute-start.1
  13.6 0.0 collective-permute-done.2.refs_1_
  13.6 0.5 %collective-permute-start.3 = (bf16[128,512]{1,0:T(8,128)(2,1)S(1)}, bf16[128,512]{1,0:T(8,128)(2,1)S(1)}, u32[]{:S(2)}, u32[]{:S(2)}) collective-permute-start(bf16[128,512]{1,0:T(8,128)(2,1)S(1)} %collective-permute-done.2.refs_1_), channel_id=1, source_target_pairs={{1,0},{0,1},{3,2},{2,3},{5,4},{4,5},{7,6},{6,7},{9,8},{8,9},{11,10... | collective-permute-start | bytes 393224 | tf_op jit(solution)/shard_map/ppermute | solution.py:293
  14.1 3.0 %collective-permute-done.4.refs_2_ = bf16[128,512]{1,0:T(8,128)(2,1)S(1)} collective-permute-done((bf16[128,512]{1,0:T(8,128)(2,1)S(1)}, bf16[128,512]{1,0:T(8,128)(2,1)S(1)}, u32[]{:S(2)}, u32[]{:S(2)}) %collective-permute-start.4) | collective-permute-done | bytes 131104 | tf_op jit(solution)/shard_map/ppermute | solution.py:284
  17.1 0.0 collective-permute-start.5
  17.1 3.0 %collective-permute-done.6.refs_3_ = bf16[128,512]{1,0:T(8,128)(2,1)S(1)} collective-permute-done((bf16[128,512]{1,0:T(8,128)(2,1)S(1)}, bf16[128,512]{1,0:T(8,128)(2,1)S(1)}, u32[]{:S(2)}, u32[]{:S(2)}) %collective-permute-start.6) | collective-permute-done | bytes 131104 | tf_op jit(solution)/shard_map/ppermute | solution.py:284
  20.1 0.0 collective-permute-start.7
  20.1 1.4 %load.1.refs_4_.refs_6_ = bf16[3,1024,256]{2,1,0:T(8,128)(2,1)S(1)} custom-call(bf16[3,1024,256]{2,1,0:T(8,128)(2,1)} %bitcast.4), custom_call_target="tpu_custom_call" | custom-call | tf_op jit(solution)/shard_map/load/pallas_call | solution.py:295
  21.5 0.7 %own.1 = (bf16[256,512]{1,0:T(8,128)(2,1)S(1)}, f32[3,256,256]{2,1,0:T(8,128)S(1)}) custom-call(bf16[128,512]{1,0:T(8,128)(2,1)S(1)} %collective-permute-done.refs_0_, bf16[128,512]{1,0:T(8,128)(2,1)S(1)} %collective-permute-done.2.refs_1_, bf16[128,512]{1,0:T(8,128)(2,1)S(1)} %collective-permute-done.4.refs_2_, ...), custom_call_target="tpu_custom_call" | custom-call | tf_op jit(solution)/shard_map/own/pallas_call | solution.py:304
  22.1 0.0 collective-permute-done.1.refs_0_
  22.2 0.0 collective-permute-done.3.refs_1_
  22.2 0.0 collective-permute-done.5.refs_2_
  22.2 0.0 collective-permute-done.7.refs_3_
  22.2 0.7 %rest.1 = (s16[656,128]{1,0:T(8,128)(2,1)S(1)}, s16[656,128]{1,0:T(8,128)(2,1)S(1)}, s16[656,128]{1,0:T(8,128)(2,1)S(1)}, s16[656,128]{1,0:T(8,128)(2,1)S(1)}) custom-call(bf16[128,512]{1,0:T(8,128)(2,1)S(1)} %collective-permute-done.1.refs_0_, bf16[128,512]{1,0:T(8,128)(2,1)S(1)} %collective-permute-done.3.refs_1_, ...), custom_call_target="tpu_custom_call" | custom-call | tf_op jit(solution)/shard_map/rest/pallas_call | solution.py:317
  22.9 2.7 %collective-permute-start.10 = (s16[656,128]{1,0:T(8,128)(2,1)S(1)}, s16[656,128]{1,0:T(8,128)(2,1)S(1)}, u32[]{:S(2)}, u32[]{:S(2)}) collective-permute-start(s16[656,128]{1,0:T(8,128)(2,1)S(1)} %get-tuple-element.18), channel_id=1, source_target_pairs={{0,24},{1,9},{2,26},{3,11},{4,28},{5,13},{6,30},{7,15},{8,16},{9,1... | collective-permute-start | bytes 503816 | tf_op jit(solution)/shard_map/ppermute | solution.py:331
  25.7 2.4 %collective-permute-start.8 = (s16[656,128]{1,0:T(8,128)(2,1)S(1)}, s16[656,128]{1,0:T(8,128)(2,1)S(1)}, u32[]{:S(2)}, u32[]{:S(2)}) collective-permute-start(s16[656,128]{1,0:T(8,128)(2,1)S(1)} %get-tuple-element.16), channel_id=1, source_target_pairs={{0,8},{1,25},{2,10},{3,27},{4,12},{5,29},{6,14},{7,31},{8,0},{9,17... | collective-permute-start | bytes 503816 | tf_op jit(solution)/shard_map/ppermute | solution.py:331
  28.1 0.0 collective-permute-start.9
  28.1 1.7 %collective-permute-done.10.refs_3_ = s16[656,128]{1,0:T(8,128)(2,1)S(1)} collective-permute-done((s16[656,128]{1,0:T(8,128)(2,1)S(1)}, s16[656,128]{1,0:T(8,128)(2,1)S(1)}, u32[]{:S(2)}, u32[]{:S(2)}) %collective-permute-start.10) | collective-permute-done | bytes 167968 | tf_op jit(solution)/shard_map/ppermute | solution.py:331
  29.8 4.4 %collective-permute-done.8.refs_1_ = s16[656,128]{1,0:T(8,128)(2,1)S(1)} collective-permute-done((s16[656,128]{1,0:T(8,128)(2,1)S(1)}, s16[656,128]{1,0:T(8,128)(2,1)S(1)}, u32[]{:S(2)}, u32[]{:S(2)}) %collective-permute-start.8) | collective-permute-done | bytes 167968 | tf_op jit(solution)/shard_map/ppermute | solution.py:331
  34.2 1.3 %collective-permute-done.9.refs_2_ = s16[656,128]{1,0:T(8,128)(2,1)S(1)} collective-permute-done((s16[656,128]{1,0:T(8,128)(2,1)S(1)}, s16[656,128]{1,0:T(8,128)(2,1)S(1)}, u32[]{:S(2)}, u32[]{:S(2)}) %collective-permute-start.9) | collective-permute-done | bytes 167968 | tf_op jit(solution)/shard_map/ppermute | solution.py:331
  35.6 0.4 %attend.1 = (bf16[64,128]{1,0:T(8,128)(2,1)S(1)}, bf16[64,128]{1,0:T(8,128)(2,1)S(1)}) custom-call(s16[656,128]{1,0:T(8,128)(2,1)S(1)} %get-tuple-element.15.refs_0_, s16[656,128]{1,0:T(8,128)(2,1)S(1)} %collective-permute-done.8.refs_1_, s16[656,128]{1,0:T(8,128)(2,1)S(1)} %collective-permute-done.9.refs_2_, s16[656,128]{1,0:T(8,128)(2,1)S(1)} %collective-permute-done.10.refs_3_), custom_call_target="tpu_custom_call" | custom-call | tf_op jit(solution)/shard_map/attend/pallas_call | solution.py:332
  36.0 1.8 %collective-permute-start.11 = (bf16[64,128]{1,0:T(8,128)(2,1)S(1)}, bf16[64,128]{1,0:T(8,128)(2,1)S(1)}, u32[]{:S(2)}, u32[]{:S(2)}) collective-permute-start(bf16[64,128]{1,0:T(8,128)(2,1)S(1)} %get-tuple-element.19), channel_id=1, source_target_pairs={{0,8},{8,0},{16,24},{24,16},{1,9},{9,1},{17,25},{25,17},{2,10},{10... | collective-permute-start | bytes 49160 | tf_op jit(solution)/shard_map/ppermute | solution.py:345
  37.8 2.0 %collective-permute-done.11 = bf16[64,128]{1,0:T(8,128)(2,1)S(1)} collective-permute-done((bf16[64,128]{1,0:T(8,128)(2,1)S(1)}, bf16[64,128]{1,0:T(8,128)(2,1)S(1)}, u32[]{:S(2)}, u32[]{:S(2)}) %collective-permute-start.11) | collective-permute-done | bytes 16416 | tf_op jit(solution)/shard_map/ppermute | solution.py:345
  39.8 0.6 %pad_maximum_fusion = bf16[64,256]{1,0:T(8,128)(2,1)} fusion(bf16[64,128]{1,0:T(8,128)(2,1)S(1)} %get-tuple-element.22, bf16[64,128]{1,0:T(8,128)(2,1)S(1)} %get-tuple-element.21), kind=kLoop, calls=%fused_computation.4 | loop fusion | flops 65536 | bytes 65536 | tf_op jit(solution)/shard_map/concatenate | solution.py:353
  (3 shorter events, 0.0 us)
Async XLA Ops:
  0.0 1.4 %copy-start = (bf16[256,512]{1,0:T(8,128)(2,1)S(1)}, bf16[256,512]{1,0:T(8,128)(2,1)}, u32[]{:S(2)}) copy-start(bf16[256,512]{1,0:T(8,128)(2,1)} %param.4) | copy-start | bytes 786436
  1.6 11.9 %collective-permute-start = (bf16[128,512]{1,0:T(8,128)(2,1)S(1)}, bf16[128,512]{1,0:T(8,128)(2,1)S(1)}, u32[]{:S(2)}, u32[]{:S(2)}) collective-permute-start(bf16[128,512]{1,0:T(8,128)(2,1)S(1)} %fusion), channel_id=1, source_target_pairs={{0,0},{1,5},{2,8},{3,13},{4,16},{5,21},{6,24},{7,29},{8,6},{9,3},{... | collective-permute-start | bytes 393224 | tf_op jit(solution)/shard_map/ppermute | solution.py:284
  2.3 11.3 %collective-permute-start.2 = (bf16[128,512]{1,0:T(8,128)(2,1)S(1)}, bf16[128,512]{1,0:T(8,128)(2,1)S(1)}, u32[]{:S(2)}, u32[]{:S(2)}) collective-permute-start(bf16[128,512]{1,0:T(8,128)(2,1)S(1)} %fusion), channel_id=1, source_target_pairs={{0,2},{1,7},{2,10},{3,15},{4,18},{5,23},{6,26},{7,31},{8,0},{9,5},... | collective-permute-start | bytes 393224 | tf_op jit(solution)/shard_map/ppermute | solution.py:284
  8.0 9.1 %collective-permute-start.4 = (bf16[128,512]{1,0:T(8,128)(2,1)S(1)}, bf16[128,512]{1,0:T(8,128)(2,1)S(1)}, u32[]{:S(2)}, u32[]{:S(2)}) collective-permute-start(bf16[128,512]{1,0:T(8,128)(2,1)S(1)} %fusion), channel_id=1, source_target_pairs={{0,4},{1,1},{2,12},{3,9},{4,20},{5,17},{6,28},{7,25},{8,2},{9,7},{... | collective-permute-start | bytes 393224 | tf_op jit(solution)/shard_map/ppermute | solution.py:284
  13.4 6.6 %collective-permute-start.6 = (bf16[128,512]{1,0:T(8,128)(2,1)S(1)}, bf16[128,512]{1,0:T(8,128)(2,1)S(1)}, u32[]{:S(2)}, u32[]{:S(2)}) collective-permute-start(bf16[128,512]{1,0:T(8,128)(2,1)S(1)} %fusion), channel_id=1, source_target_pairs={{0,6},{1,3},{2,14},{3,11},{4,22},{5,19},{6,30},{7,27},{8,4},{9,1},... | collective-permute-start | bytes 393224 | tf_op jit(solution)/shard_map/ppermute | solution.py:284
  13.5 8.7 %collective-permute-start.1 = (bf16[128,512]{1,0:T(8,128)(2,1)S(1)}, bf16[128,512]{1,0:T(8,128)(2,1)S(1)}, u32[]{:S(2)}, u32[]{:S(2)}) collective-permute-start(bf16[128,512]{1,0:T(8,128)(2,1)S(1)} %collective-permute-done.refs_0_), channel_id=1, source_target_pairs={{1,0},{0,1},{3,2},{2,3},{5,4},{4,5},{7,6},{6,7},{9,8},{8,9},{11,10... | collective-permute-start | bytes 393224 | tf_op jit(solution)/shard_map/ppermute | solution.py:293
  13.6 8.6 %collective-permute-start.3 = (bf16[128,512]{1,0:T(8,128)(2,1)S(1)}, bf16[128,512]{1,0:T(8,128)(2,1)S(1)}, u32[]{:S(2)}, u32[]{:S(2)}) collective-permute-start(bf16[128,512]{1,0:T(8,128)(2,1)S(1)} %collective-permute-done.2.refs_1_), channel_id=1, source_target_pairs={{1,0},{0,1},{3,2},{2,3},{5,4},{4,5},{7,6},{6,7},{9,8},{8,9},{11,10... | collective-permute-start | bytes 393224 | tf_op jit(solution)/shard_map/ppermute | solution.py:293
  17.1 5.1 %collective-permute-start.5 = (bf16[128,512]{1,0:T(8,128)(2,1)S(1)}, bf16[128,512]{1,0:T(8,128)(2,1)S(1)}, u32[]{:S(2)}, u32[]{:S(2)}) collective-permute-start(bf16[128,512]{1,0:T(8,128)(2,1)S(1)} %collective-permute-done.4.refs_2_), channel_id=1, source_target_pairs={{1,0},{0,1},{3,2},{2,3},{5,4},{4,5},{7,6},{6,7},{9,8},{8,9},{11,10... | collective-permute-start | bytes 393224 | tf_op jit(solution)/shard_map/ppermute | solution.py:293
  20.1 2.1 %collective-permute-start.7 = (bf16[128,512]{1,0:T(8,128)(2,1)S(1)}, bf16[128,512]{1,0:T(8,128)(2,1)S(1)}, u32[]{:S(2)}, u32[]{:S(2)}) collective-permute-start(bf16[128,512]{1,0:T(8,128)(2,1)S(1)} %collective-permute-done.6.refs_3_), channel_id=1, source_target_pairs={{1,0},{0,1},{3,2},{2,3},{5,4},{4,5},{7,6},{6,7},{9,8},{8,9},{11,10... | collective-permute-start | bytes 393224 | tf_op jit(solution)/shard_map/ppermute | solution.py:293
  22.9 6.9 %collective-permute-start.10 = (s16[656,128]{1,0:T(8,128)(2,1)S(1)}, s16[656,128]{1,0:T(8,128)(2,1)S(1)}, u32[]{:S(2)}, u32[]{:S(2)}) collective-permute-start(s16[656,128]{1,0:T(8,128)(2,1)S(1)} %get-tuple-element.18), channel_id=1, source_target_pairs={{0,24},{1,9},{2,26},{3,11},{4,28},{5,13},{6,30},{7,15},{8,16},{9,1... | collective-permute-start | bytes 503816 | tf_op jit(solution)/shard_map/ppermute | solution.py:331
  25.7 8.6 %collective-permute-start.8 = (s16[656,128]{1,0:T(8,128)(2,1)S(1)}, s16[656,128]{1,0:T(8,128)(2,1)S(1)}, u32[]{:S(2)}, u32[]{:S(2)}) collective-permute-start(s16[656,128]{1,0:T(8,128)(2,1)S(1)} %get-tuple-element.16), channel_id=1, source_target_pairs={{0,8},{1,25},{2,10},{3,27},{4,12},{5,29},{6,14},{7,31},{8,0},{9,17... | collective-permute-start | bytes 503816 | tf_op jit(solution)/shard_map/ppermute | solution.py:331
  28.1 7.5 %collective-permute-start.9 = (s16[656,128]{1,0:T(8,128)(2,1)S(1)}, s16[656,128]{1,0:T(8,128)(2,1)S(1)}, u32[]{:S(2)}, u32[]{:S(2)}) collective-permute-start(s16[656,128]{1,0:T(8,128)(2,1)S(1)} %get-tuple-element.17), channel_id=1, source_target_pairs={{0,16},{1,17},{2,18},{3,19},{4,20},{5,21},{6,22},{7,23},{8,24},{9,... | collective-permute-start | bytes 503816 | tf_op jit(solution)/shard_map/ppermute | solution.py:331
  36.0 3.8 %collective-permute-start.11 = (bf16[64,128]{1,0:T(8,128)(2,1)S(1)}, bf16[64,128]{1,0:T(8,128)(2,1)S(1)}, u32[]{:S(2)}, u32[]{:S(2)}) collective-permute-start(bf16[64,128]{1,0:T(8,128)(2,1)S(1)} %get-tuple-element.19), channel_id=1, source_target_pairs={{0,8},{8,0},{16,24},{24,16},{1,9},{9,1},{17,25},{25,17},{2,10},{10... | collective-permute-start | bytes 49160 | tf_op jit(solution)/shard_map/ppermute | solution.py:345

commit v8 on v7

--- a/solution.py
+++ b/solution.py
@@ -88,7 +88,7 @@
 
 VMEM = pl.BlockSpec(memory_space=pltpu.VMEM)
 HBM = pl.BlockSpec(memory_space=pltpu.HBM)
-TOP_BITS = 14
+TOP_BITS = 14.875
 
 
 def gather(tokens, keep_list, counts):
@@ -189,7 +189,7 @@
             acc += jnp.dot(
                 rows[p - 1], w_ref[kind, pl.ds(where, width), :], preferred_element_type=jnp.float32
             )
-        most = jnp.maximum(jnp.max(jnp.abs(acc), axis=0, keepdims=True), 2.0**-100)
+        most = jnp.maximum(jnp.max(jnp.abs(acc), axis=0, keepdims=True), 2.0**-112)
         exponent = jnp.floor(jnp.log2(most)) + 1.0
         exponents.append(exponent)
         value = jnp.round(acc * jnp.exp2(TOP_BITS - exponent)).astype(jnp.int32)
@@ -220,8 +220,25 @@
     return mine
 
 
-def attend_kernel(shards, heads, kept, *refs):
-    parts, outs = refs[:shards], refs[shards:]
+def attended(query, key, value, first_row, shards):
+    capacity = key.shape[0] // shards
+    scores = lax.dot_general(
+        query, key, (((1,), (1,)), ((), ())), preferred_element_type=jnp.float32
+    ) * (HD ** (-0.5))
+    q_row = lax.broadcasted_iota(jnp.int32, scores.shape, 0) + first_row
+    k_row = lax.broadcasted_iota(jnp.int32, scores.shape, 1)
+    q_rank = lax.rem(q_row, capacity) * shards + lax.div(q_row, capacity)
+    k_rank = lax.rem(k_row, capacity) * shards + lax.div(k_row, capacity)
+    scores = jnp.where(k_rank > q_rank, -jnp.inf, scores)
+    top = jnp.max(scores, axis=1, keepdims=True)
+    expo = jnp.exp(scores - top)
+    numer = jnp.dot(expo.astype(jnp.bfloat16), value, preferred_element_type=jnp.float32)
+    return (numer / jnp.sum(expo, axis=1, keepdims=True)).astype(jnp.bfloat16)
+
+
+def leaving_kernel(shards, heads, kept, *refs):
+    parts, outs = refs[:shards], refs[shards : shards + heads - 1]
+    key_ref, value_ref, query_ref = refs[shards + heads - 1 :]
     capacity = kept // shards
     me = lax.axis_index("seq")
     block_rows = kept // (shards // heads)
@@ -236,28 +253,30 @@
         for p, scale in zip(parts, scales):
             part = p[lo:hi, :].astype(jnp.int32).astype(jnp.float32) * scale[i : i + 1, :]
             acc = part if acc is None else acc + part
-        return acc.astype(jnp.bfloat16)
-
-    key, value, query = summed(0, 0, kept), summed(1, kept, 2 * kept), summed(2, 2 * kept, total)
-    scores = lax.dot_general(
-        query, key, (((1,), (1,)), ((), ())), preferred_element_type=jnp.float32
-    ) * (HD ** (-0.5))
-    q_row = lax.broadcasted_iota(jnp.int32, scores.shape, 0) + block * block_rows
-    k_row = lax.broadcasted_iota(jnp.int32, scores.shape, 1)
-    q_rank = lax.rem(q_row, capacity) * shards + lax.div(q_row, capacity)
-    k_rank = lax.rem(k_row, capacity) * shards + lax.div(k_row, capacity)
-    scores = jnp.where(k_rank > q_rank, -jnp.inf, scores)
-    top = jnp.max(scores, axis=1, keepdims=True)
-    expo = jnp.exp(scores - top)
-    numer = jnp.dot(expo.astype(jnp.bfloat16), value, preferred_element_type=jnp.float32)
-    result = numer / jnp.sum(expo, axis=1, keepdims=True)
+        return acc
+
+    def rows_of(owner, rows):
+        mine = rows[:capacity, :]
+        for o in range(1, heads):
+            mine = jnp.where(owner == o, rows[o * capacity : (o + 1) * capacity, :], mine)
+        return mine.astype(jnp.bfloat16)
+
+    query = summed(2, 2 * kept, total)
+    key = summed(0, 0, kept).astype(jnp.bfloat16)
+    value = summed(1, kept, 2 * kept).astype(jnp.bfloat16)
+    key_ref[...] = key
+    value_ref[...] = value
     head = lax.rem(me, heads)
-    for k in range(heads):
+    query_ref[...] = rows_of(head, query)
+    for k in range(1, heads):
         owner = lax.rem(head + k, heads)
-        piece = result[:capacity, :]
-        for o in range(1, heads):
-            piece = jnp.where(owner == o, result[o * capacity : (o + 1) * capacity, :], piece)
-        outs[k][...] = piece.astype(jnp.bfloat16)
+        first_row = block * block_rows + owner * capacity
+        outs[k - 1][...] = attended(rows_of(owner, query), key, value, first_row, shards)
+
+
+def staying_kernel(shards, key_ref, value_ref, query_ref, out_ref):
+    first_row = lax.axis_index("seq") * query_ref.shape[0]
+    out_ref[...] = attended(query_ref[...], key_ref[...], value_ref[...], first_row, shards)
 
 
 def by_features(shards, tp, tokens, w_qkv, keep_list, counts):
@@ -313,7 +332,7 @@
         name="own",
     )(*own, weights)
     blocks = shards // heads
-    payload = 2 * kept + kept // blocks + 16
+    payload = 2 * kept + kept // blocks + 8
     partial = pl.pallas_call(
         functools.partial(rest_kernel, shards, group, heads),
         out_shape=[jax.ShapeDtypeStruct((payload, HD), jnp.int16)] * shards,
@@ -329,20 +348,31 @@
             for s, line, c in every
         ]
         parts.append(lax.ppermute(partial[k], ("seq", "tp"), pairs))
-    pieces = pl.pallas_call(
-        functools.partial(attend_kernel, shards, heads, kept),
-        out_shape=[jax.ShapeDtypeStruct((capacity, HD), jnp.bfloat16)] * heads,
+    *leaving, key, value, query = pl.pallas_call(
+        functools.partial(leaving_kernel, shards, heads, kept),
+        out_shape=[
+            jax.ShapeDtypeStruct((rows, HD), jnp.bfloat16)
+            for rows in (capacity,) * (heads - 1) + (kept, kept, capacity)
+        ],
         in_specs=[VMEM] * shards,
-        out_specs=[VMEM] * heads,
+        out_specs=[VMEM] * (heads + 2),
         compiler_params=params,
-        name="attend",
+        name="leaving",
     )(*parts)
-    arrived = [pieces[0]]
+    staying = pl.pallas_call(
+        functools.partial(staying_kernel, shards),
+        out_shape=jax.ShapeDtypeStruct((capacity, HD), jnp.bfloat16),
+        in_specs=[VMEM] * 3,
+        out_specs=VMEM,
+        compiler_params=params,
+        name="staying",
+    )(key, value, query)
+    arrived = [staying]
     for k in range(1, heads):
         pairs = [
             (b * heads + h, b * heads + (h + k) % heads) for b in range(blocks) for h in range(heads)
         ]
-        arrived.append(lax.ppermute(pieces[k], "seq", pairs))
+        arrived.append(lax.ppermute(leaving[k - 1], "seq", pairs))
     mine = lax.rem(lax.axis_index("seq"), heads)
     columns = []
     for h in range(heads):

time: 40.6 us -> 40.6 us (level)
  transfers between devices with their start and end apart: 12 -> 12, of which waited for: 6 -> 6; matrix products, arithmetic and copies ran while one was open for 0% -> 0% of each run, Pallas kernels for 5% -> 6%
where the time goes in v8:
time: 40.6 us; the launch traced here: 40.4 us
  starting transfers between devices  19.3 us (48%)
  waiting for transfers between devices  15.1 us (37%)
  Pallas kernels  3.6 us (9%)
  other arithmetic  1.35 us (3%)
  between operations  0.8 us (2%)
    ppermute x4, starting transfers between devices, by_features(): own.append(lax.ppermute(packed, axes, pairs))  11.8 us
    ppermute x3, waiting for transfers between devices, by_features(): parts.append(lax.ppermute(partial[k], ('seq', 'tp'), pairs))  7.39 us
    ppermute x4, waiting for transfers between devices, by_features(): own.append(lax.ppermute(packed, axes, pairs))  5.99 us
    ppermute x3, starting transfers between devices, by_features(): parts.append(lax.ppermute(partial[k], ('seq', 'tp'), pairs))  5.17 us
    ppermute x1, starting transfers between devices, by_features(): arrived.append(lax.ppermute(leaving[k - 1], 'seq', pairs))  1.76 us
    ppermute x1, waiting for transfers between devices, by_features(): arrived.append(lax.ppermute(leaving[k - 1], 'seq', pairs))  1.67 us
    pallas_call x1, Pallas kernels, by_features(): pl.pallas_call(load_kernel, out_shape=jax.ShapeDtypeStruct(weights.shape,...  1.42 us
  transfers between devices with their start and end apart: 12, of which 6 were waited for; matrix products, arithmetic and copies ran while one was open for 0% of the time, Pallas kernels for 6%

profile of v8, /device:TPU:0, one launch (start us, length us, event | category | flops | bytes accessed | tf_op | source)
XLA Modules:
  0.0 40.4 jit_solution(11062386851375434801)
XLA Ops:
  0.0 0.7 %fusion.1 = bf16[256,128]{1,0:T(8,128)(2,1)S(1)} fusion(s32[128]{0:T(128)} %param.6), kind=kLoop, calls=%fused_computation.3 | loop fusion | flops 65536 | bytes 66048 | tf_op jit(solution)/shard_map/convert_element_type | solution.py:97
  1.4 0.2 fusion
  1.6 0.7 %collective-permute-start = (bf16[128,512]{1,0:T(8,128)(2,1)S(1)}, bf16[128,512]{1,0:T(8,128)(2,1)S(1)}, u32[]{:S(2)}, u32[]{:S(2)}) collective-permute-start(bf16[128,512]{1,0:T(8,128)(2,1)S(1)} %fusion), channel_id=1, source_target_pairs={{0,0},{1,5},{2,8},{3,13},{4,16},{5,21},{6,24},{7,29},{8,6},{9,3},{... | collective-permute-start | bytes 393224 | tf_op jit(solution)/shard_map/ppermute | solution.py:303
  2.3 5.7 %collective-permute-start.2 = (bf16[128,512]{1,0:T(8,128)(2,1)S(1)}, bf16[128,512]{1,0:T(8,128)(2,1)S(1)}, u32[]{:S(2)}, u32[]{:S(2)}) collective-permute-start(bf16[128,512]{1,0:T(8,128)(2,1)S(1)} %fusion), channel_id=1, source_target_pairs={{0,2},{1,7},{2,10},{3,15},{4,18},{5,23},{6,26},{7,31},{8,0},{9,5},... | collective-permute-start | bytes 393224 | tf_op jit(solution)/shard_map/ppermute | solution.py:303
  8.0 5.4 %collective-permute-start.4 = (bf16[128,512]{1,0:T(8,128)(2,1)S(1)}, bf16[128,512]{1,0:T(8,128)(2,1)S(1)}, u32[]{:S(2)}, u32[]{:S(2)}) collective-permute-start(bf16[128,512]{1,0:T(8,128)(2,1)S(1)} %fusion), channel_id=1, source_target_pairs={{0,4},{1,1},{2,12},{3,9},{4,20},{5,17},{6,28},{7,25},{8,2},{9,7},{... | collective-permute-start | bytes 393224 | tf_op jit(solution)/shard_map/ppermute | solution.py:303
  13.4 0.1 collective-permute-start.6
  13.5 0.0 collective-permute-done.refs_0_
  13.5 0.1 collective-permute-start.1
  13.6 0.0 collective-permute-done.2.refs_1_
  13.6 0.5 %collective-permute-start.3 = (bf16[128,512]{1,0:T(8,128)(2,1)S(1)}, bf16[128,512]{1,0:T(8,128)(2,1)S(1)}, u32[]{:S(2)}, u32[]{:S(2)}) collective-permute-start(bf16[128,512]{1,0:T(8,128)(2,1)S(1)} %collective-permute-done.2.refs_1_), channel_id=1, source_target_pairs={{1,0},{0,1},{3,2},{2,3},{5,4},{4,5},{7,6},{6,7},{9,8},{8,9},{11,10... | collective-permute-start | bytes 393224 | tf_op jit(solution)/shard_map/ppermute | solution.py:312
  14.1 3.0 %collective-permute-done.4.refs_2_ = bf16[128,512]{1,0:T(8,128)(2,1)S(1)} collective-permute-done((bf16[128,512]{1,0:T(8,128)(2,1)S(1)}, bf16[128,512]{1,0:T(8,128)(2,1)S(1)}, u32[]{:S(2)}, u32[]{:S(2)}) %collective-permute-start.4) | collective-permute-done | bytes 131104 | tf_op jit(solution)/shard_map/ppermute | solution.py:303
  17.1 0.0 collective-permute-start.5
  17.1 3.0 %collective-permute-done.6.refs_3_ = bf16[128,512]{1,0:T(8,128)(2,1)S(1)} collective-permute-done((bf16[128,512]{1,0:T(8,128)(2,1)S(1)}, bf16[128,512]{1,0:T(8,128)(2,1)S(1)}, u32[]{:S(2)}, u32[]{:S(2)}) %collective-permute-start.6) | collective-permute-done | bytes 131104 | tf_op jit(solution)/shard_map/ppermute | solution.py:303
  20.1 0.0 collective-permute-start.7
  20.1 1.4 %load.1.refs_4_.refs_6_ = bf16[3,1024,256]{2,1,0:T(8,128)(2,1)S(1)} custom-call(bf16[3,1024,256]{2,1,0:T(8,128)(2,1)} %bitcast.4), custom_call_target="tpu_custom_call" | custom-call | tf_op jit(solution)/shard_map/load/pallas_call | solution.py:314
  21.5 0.7 %own.1 = (bf16[256,512]{1,0:T(8,128)(2,1)S(1)}, f32[3,256,256]{2,1,0:T(8,128)S(1)}) custom-call(bf16[128,512]{1,0:T(8,128)(2,1)S(1)} %collective-permute-done.refs_0_, bf16[128,512]{1,0:T(8,128)(2,1)S(1)} %collective-permute-done.2.refs_1_, bf16[128,512]{1,0:T(8,128)(2,1)S(1)} %collective-permute-done.4.refs_2_, ...), custom_call_target="tpu_custom_call" | custom-call | tf_op jit(solution)/shard_map/own/pallas_call | solution.py:323
  22.1 0.0 collective-permute-done.1.refs_0_
  22.2 0.0 collective-permute-done.3.refs_1_
  22.2 0.0 collective-permute-done.5.refs_2_
  22.2 0.0 collective-permute-done.7.refs_3_
  22.2 0.7 %rest.1 = (s16[648,128]{1,0:T(8,128)(2,1)S(1)}, s16[648,128]{1,0:T(8,128)(2,1)S(1)}, s16[648,128]{1,0:T(8,128)(2,1)S(1)}, s16[648,128]{1,0:T(8,128)(2,1)S(1)}) custom-call(bf16[128,512]{1,0:T(8,128)(2,1)S(1)} %collective-permute-done.1.refs_0_, bf16[128,512]{1,0:T(8,128)(2,1)S(1)} %collective-permute-done.3.refs_1_, ...), custom_call_target="tpu_custom_call" | custom-call | tf_op jit(solution)/shard_map/rest/pallas_call | solution.py:336
  22.9 2.7 %collective-permute-start.10 = (s16[648,128]{1,0:T(8,128)(2,1)S(1)}, s16[648,128]{1,0:T(8,128)(2,1)S(1)}, u32[]{:S(2)}, u32[]{:S(2)}) collective-permute-start(s16[648,128]{1,0:T(8,128)(2,1)S(1)} %get-tuple-element.20), channel_id=1, source_target_pairs={{0,24},{1,9},{2,26},{3,11},{4,28},{5,13},{6,30},{7,15},{8,16},{9,1... | collective-permute-start | bytes 497672 | tf_op jit(solution)/shard_map/ppermute | solution.py:350
  25.7 2.4 %collective-permute-start.8 = (s16[648,128]{1,0:T(8,128)(2,1)S(1)}, s16[648,128]{1,0:T(8,128)(2,1)S(1)}, u32[]{:S(2)}, u32[]{:S(2)}) collective-permute-start(s16[648,128]{1,0:T(8,128)(2,1)S(1)} %get-tuple-element.18), channel_id=1, source_target_pairs={{0,8},{1,25},{2,10},{3,27},{4,12},{5,29},{6,14},{7,31},{8,0},{9,17... | collective-permute-start | bytes 497672 | tf_op jit(solution)/shard_map/ppermute | solution.py:350
  28.1 0.0 collective-permute-start.9
  28.1 1.7 %collective-permute-done.10.refs_3_ = s16[648,128]{1,0:T(8,128)(2,1)S(1)} collective-permute-done((s16[648,128]{1,0:T(8,128)(2,1)S(1)}, s16[648,128]{1,0:T(8,128)(2,1)S(1)}, u32[]{:S(2)}, u32[]{:S(2)}) %collective-permute-start.10) | collective-permute-done | bytes 165920 | tf_op jit(solution)/shard_map/ppermute | solution.py:350
  29.8 4.4 %collective-permute-done.8.refs_1_ = s16[648,128]{1,0:T(8,128)(2,1)S(1)} collective-permute-done((s16[648,128]{1,0:T(8,128)(2,1)S(1)}, s16[648,128]{1,0:T(8,128)(2,1)S(1)}, u32[]{:S(2)}, u32[]{:S(2)}) %collective-permute-start.8) | collective-permute-done | bytes 165920 | tf_op jit(solution)/shard_map/ppermute | solution.py:350
  34.2 1.3 %collective-permute-done.9.refs_2_ = s16[648,128]{1,0:T(8,128)(2,1)S(1)} collective-permute-done((s16[648,128]{1,0:T(8,128)(2,1)S(1)}, s16[648,128]{1,0:T(8,128)(2,1)S(1)}, u32[]{:S(2)}, u32[]{:S(2)}) %collective-permute-start.9) | collective-permute-done | bytes 165920 | tf_op jit(solution)/shard_map/ppermute | solution.py:350
  35.5 0.4 %leaving.1 = (bf16[64,128]{1,0:T(8,128)(2,1)S(1)}, bf16[256,128]{1,0:T(8,128)(2,1)S(1)}, bf16[256,128]{1,0:T(8,128)(2,1)S(1)}, bf16[64,128]{1,0:T(8,128)(2,1)S(1)}) custom-call(s16[648,128]{1,0:T(8,128)(2,1)S(1)} %get-tuple-element.17.refs_0_, s16[648,128]{1,0:T(8,128)(2,1)S(1)} %collective-permute-done.8.refs_1_, ...), custom_call_target="tpu_custom_call" | custom-call | tf_op jit(solution)/shard_map/leaving/pallas_call | solution.py:351
  35.9 1.8 %collective-permute-start.11 = (bf16[64,128]{1,0:T(8,128)(2,1)S(1)}, bf16[64,128]{1,0:T(8,128)(2,1)S(1)}, u32[]{:S(2)}, u32[]{:S(2)}) collective-permute-start(bf16[64,128]{1,0:T(8,128)(2,1)S(1)} %get-tuple-element.21), channel_id=1, source_target_pairs={{0,8},{8,0},{16,24},{24,16},{1,9},{9,1},{17,25},{25,17},{2,10},{10... | collective-permute-start | bytes 49160 | tf_op jit(solution)/shard_map/ppermute | solution.py:375
  37.7 0.4 staying.1
  38.1 1.7 %collective-permute-done.11 = bf16[64,128]{1,0:T(8,128)(2,1)S(1)} collective-permute-done((bf16[64,128]{1,0:T(8,128)(2,1)S(1)}, bf16[64,128]{1,0:T(8,128)(2,1)S(1)}, u32[]{:S(2)}, u32[]{:S(2)}) %collective-permute-start.11) | collective-permute-done | bytes 16416 | tf_op jit(solution)/shard_map/ppermute | solution.py:375
  39.7 0.6 %pad_maximum_fusion = bf16[64,256]{1,0:T(8,128)(2,1)} fusion(bf16[64,128]{1,0:T(8,128)(2,1)S(1)} %get-tuple-element.26, bf16[64,128]{1,0:T(8,128)(2,1)S(1)} %get-tuple-element.25), kind=kLoop, calls=%fused_computation.4 | loop fusion | flops 65536 | bytes 65536 | tf_op jit(solution)/shard_map/concatenate | solution.py:383
  (4 shorter events, 0.0 us)
Async XLA Ops:
  0.0 1.4 %copy-start = (bf16[256,512]{1,0:T(8,128)(2,1)S(1)}, bf16[256,512]{1,0:T(8,128)(2,1)}, u32[]{:S(2)}) copy-start(bf16[256,512]{1,0:T(8,128)(2,1)} %param.4) | copy-start | bytes 786436
  1.6 11.9 %collective-permute-start = (bf16[128,512]{1,0:T(8,128)(2,1)S(1)}, bf16[128,512]{1,0:T(8,128)(2,1)S(1)}, u32[]{:S(2)}, u32[]{:S(2)}) collective-permute-start(bf16[128,512]{1,0:T(8,128)(2,1)S(1)} %fusion), channel_id=1, source_target_pairs={{0,0},{1,5},{2,8},{3,13},{4,16},{5,21},{6,24},{7,29},{8,6},{9,3},{... | collective-permute-start | bytes 393224 | tf_op jit(solution)/shard_map/ppermute | solution.py:303
  2.3 11.3 %collective-permute-start.2 = (bf16[128,512]{1,0:T(8,128)(2,1)S(1)}, bf16[128,512]{1,0:T(8,128)(2,1)S(1)}, u32[]{:S(2)}, u32[]{:S(2)}) collective-permute-start(bf16[128,512]{1,0:T(8,128)(2,1)S(1)} %fusion), channel_id=1, source_target_pairs={{0,2},{1,7},{2,10},{3,15},{4,18},{5,23},{6,26},{7,31},{8,0},{9,5},... | collective-permute-start | bytes 393224 | tf_op jit(solution)/shard_map/ppermute | solution.py:303
  8.0 9.1 %collective-permute-start.4 = (bf16[128,512]{1,0:T(8,128)(2,1)S(1)}, bf16[128,512]{1,0:T(8,128)(2,1)S(1)}, u32[]{:S(2)}, u32[]{:S(2)}) collective-permute-start(bf16[128,512]{1,0:T(8,128)(2,1)S(1)} %fusion), channel_id=1, source_target_pairs={{0,4},{1,1},{2,12},{3,9},{4,20},{5,17},{6,28},{7,25},{8,2},{9,7},{... | collective-permute-start | bytes 393224 | tf_op jit(solution)/shard_map/ppermute | solution.py:303
  13.4 6.6 %collective-permute-start.6 = (bf16[128,512]{1,0:T(8,128)(2,1)S(1)}, bf16[128,512]{1,0:T(8,128)(2,1)S(1)}, u32[]{:S(2)}, u32[]{:S(2)}) collective-permute-start(bf16[128,512]{1,0:T(8,128)(2,1)S(1)} %fusion), channel_id=1, source_target_pairs={{0,6},{1,3},{2,14},{3,11},{4,22},{5,19},{6,30},{7,27},{8,4},{9,1},... | collective-permute-start | bytes 393224 | tf_op jit(solution)/shard_map/ppermute | solution.py:303
  13.5 8.7 %collective-permute-start.1 = (bf16[128,512]{1,0:T(8,128)(2,1)S(1)}, bf16[128,512]{1,0:T(8,128)(2,1)S(1)}, u32[]{:S(2)}, u32[]{:S(2)}) collective-permute-start(bf16[128,512]{1,0:T(8,128)(2,1)S(1)} %collective-permute-done.refs_0_), channel_id=1, source_target_pairs={{1,0},{0,1},{3,2},{2,3},{5,4},{4,5},{7,6},{6,7},{9,8},{8,9},{11,10... | collective-permute-start | bytes 393224 | tf_op jit(solution)/shard_map/ppermute | solution.py:312
  13.6 8.6 %collective-permute-start.3 = (bf16[128,512]{1,0:T(8,128)(2,1)S(1)}, bf16[128,512]{1,0:T(8,128)(2,1)S(1)}, u32[]{:S(2)}, u32[]{:S(2)}) collective-permute-start(bf16[128,512]{1,0:T(8,128)(2,1)S(1)} %collective-permute-done.2.refs_1_), channel_id=1, source_target_pairs={{1,0},{0,1},{3,2},{2,3},{5,4},{4,5},{7,6},{6,7},{9,8},{8,9},{11,10... | collective-permute-start | bytes 393224 | tf_op jit(solution)/shard_map/ppermute | solution.py:312
  17.1 5.1 %collective-permute-start.5 = (bf16[128,512]{1,0:T(8,128)(2,1)S(1)}, bf16[128,512]{1,0:T(8,128)(2,1)S(1)}, u32[]{:S(2)}, u32[]{:S(2)}) collective-permute-start(bf16[128,512]{1,0:T(8,128)(2,1)S(1)} %collective-permute-done.4.refs_2_), channel_id=1, source_target_pairs={{1,0},{0,1},{3,2},{2,3},{5,4},{4,5},{7,6},{6,7},{9,8},{8,9},{11,10... | collective-permute-start | bytes 393224 | tf_op jit(solution)/shard_map/ppermute | solution.py:312
  20.1 2.1 %collective-permute-start.7 = (bf16[128,512]{1,0:T(8,128)(2,1)S(1)}, bf16[128,512]{1,0:T(8,128)(2,1)S(1)}, u32[]{:S(2)}, u32[]{:S(2)}) collective-permute-start(bf16[128,512]{1,0:T(8,128)(2,1)S(1)} %collective-permute-done.6.refs_3_), channel_id=1, source_target_pairs={{1,0},{0,1},{3,2},{2,3},{5,4},{4,5},{7,6},{6,7},{9,8},{8,9},{11,10... | collective-permute-start | bytes 393224 | tf_op jit(solution)/shard_map/ppermute | solution.py:312
  22.9 6.8 %collective-permute-start.10 = (s16[648,128]{1,0:T(8,128)(2,1)S(1)}, s16[648,128]{1,0:T(8,128)(2,1)S(1)}, u32[]{:S(2)}, u32[]{:S(2)}) collective-permute-start(s16[648,128]{1,0:T(8,128)(2,1)S(1)} %get-tuple-element.20), channel_id=1, source_target_pairs={{0,24},{1,9},{2,26},{3,11},{4,28},{5,13},{6,30},{7,15},{8,16},{9,1... | collective-permute-start | bytes 497672 | tf_op jit(solution)/shard_map/ppermute | solution.py:350
  25.7 8.5 %collective-permute-start.8 = (s16[648,128]{1,0:T(8,128)(2,1)S(1)}, s16[648,128]{1,0:T(8,128)(2,1)S(1)}, u32[]{:S(2)}, u32[]{:S(2)}) collective-permute-start(s16[648,128]{1,0:T(8,128)(2,1)S(1)} %get-tuple-element.18), channel_id=1, source_target_pairs={{0,8},{1,25},{2,10},{3,27},{4,12},{5,29},{6,14},{7,31},{8,0},{9,17... | collective-permute-start | bytes 497672 | tf_op jit(solution)/shard_map/ppermute | solution.py:350
  28.1 7.4 %collective-permute-start.9 = (s16[648,128]{1,0:T(8,128)(2,1)S(1)}, s16[648,128]{1,0:T(8,128)(2,1)S(1)}, u32[]{:S(2)}, u32[]{:S(2)}) collective-permute-start(s16[648,128]{1,0:T(8,128)(2,1)S(1)} %get-tuple-element.19), channel_id=1, source_target_pairs={{0,16},{1,17},{2,18},{3,19},{4,20},{5,21},{6,22},{7,23},{8,24},{9,... | collective-permute-start | bytes 497672 | tf_op jit(solution)/shard_map/ppermute | solution.py:350
  35.9 3.8 %collective-permute-start.11 = (bf16[64,128]{1,0:T(8,128)(2,1)S(1)}, bf16[64,128]{1,0:T(8,128)(2,1)S(1)}, u32[]{:S(2)}, u32[]{:S(2)}) collective-permute-start(bf16[64,128]{1,0:T(8,128)(2,1)S(1)} %get-tuple-element.21), channel_id=1, source_target_pairs={{0,8},{8,0},{16,24},{24,16},{1,9},{9,1},{17,25},{25,17},{2,10},{10... | collective-permute-start | bytes 49160 | tf_op jit(solution)/shard_map/ppermute | solution.py:375

commit v9 on v7

--- a/solution.py
+++ b/solution.py
@@ -88,7 +88,7 @@
 
 VMEM = pl.BlockSpec(memory_space=pltpu.VMEM)
 HBM = pl.BlockSpec(memory_space=pltpu.HBM)
-TOP_BITS = 14
+TOP_BITS = 14.875
 
 
 def gather(tokens, keep_list, counts):
@@ -111,7 +111,7 @@
 
 
 def toward(me, k, shards):
-    return me ^ k if shards & (shards - 1) == 0 else (me + k) % shards
+    return (me + k) % shards
 
 
 def step(j, core, shards):
@@ -189,7 +189,7 @@
             acc += jnp.dot(
                 rows[p - 1], w_ref[kind, pl.ds(where, width), :], preferred_element_type=jnp.float32
             )
-        most = jnp.maximum(jnp.max(jnp.abs(acc), axis=0, keepdims=True), 2.0**-100)
+        most = jnp.maximum(jnp.max(jnp.abs(acc), axis=0, keepdims=True), 2.0**-112)
         exponent = jnp.floor(jnp.log2(most)) + 1.0
         exponents.append(exponent)
         value = jnp.round(acc * jnp.exp2(TOP_BITS - exponent)).astype(jnp.int32)
@@ -313,7 +313,7 @@
         name="own",
     )(*own, weights)
     blocks = shards // heads
-    payload = 2 * kept + kept // blocks + 16
+    payload = 2 * kept + kept // blocks + 8
     partial = pl.pallas_call(
         functools.partial(rest_kernel, shards, group, heads),
         out_shape=[jax.ShapeDtypeStruct((payload, HD), jnp.int16)] * shards,

time: 40.6 us -> 40.4 us (level)
  waiting for transfers between devices: 15.5 us -> 14.3 us
  starting transfers between devices: 19.4 us -> 20.1 us
    ppermute x3, waiting for transfers between devices: 7.45 us -> 6.54 us  [by_features(): parts.append(lax.ppermute(partial[k], ('seq', 'tp'), pairs))]
    ppermute x3, starting transfers between devices: 5.17 us -> 5.72 us  [by_features(): parts.append(lax.ppermute(partial[k], ('seq', 'tp'), pairs))]
where the time goes in v9:
time: 40.4 us; the launch traced here: 40.1 us
  starting transfers between devices  20.1 us (50%)
  waiting for transfers between devices  14.3 us (35%)
  Pallas kernels  3.25 us (8%)
  other arithmetic  1.35 us (3%)
  between operations  0.79 us (2%)
    ppermute x4, starting transfers between devices, by_features(): own.append(lax.ppermute(packed, axes, pairs))  11.8 us
    ppermute x3, waiting for transfers between devices, by_features(): parts.append(lax.ppermute(partial[k], ('seq', 'tp'), pairs))  6.54 us
    ppermute x4, waiting for transfers between devices, by_features(): own.append(lax.ppermute(packed, axes, pairs))  5.99 us
    ppermute x3, starting transfers between devices, by_features(): parts.append(lax.ppermute(partial[k], ('seq', 'tp'), pairs))  5.72 us
    ppermute x1, starting transfers between devices, by_features(): arrived.append(lax.ppermute(pieces[k], 'seq', pairs))  2.01 us
    ppermute x1, waiting for transfers between devices, by_features(): arrived.append(lax.ppermute(pieces[k], 'seq', pairs))  1.8 us
    pallas_call x1, Pallas kernels, by_features(): pl.pallas_call(load_kernel, out_shape=jax.ShapeDtypeStruct(weights.shape,...  1.42 us
  transfers between devices with their start and end apart: 12, of which 6 were waited for; matrix products, arithmetic and copies ran while one was open for 0% of the time, Pallas kernels for 5%

profile of v9, /device:TPU:0, one launch (start us, length us, event | category | flops | bytes accessed | tf_op | source)
XLA Modules:
  0.0 40.1 jit_solution(5742674805499680587)
XLA Ops:
  0.0 0.0 copy-start
  0.0 0.7 %fusion.1 = bf16[256,128]{1,0:T(8,128)(2,1)S(1)} fusion(s32[128]{0:T(128)} %param.6), kind=kLoop, calls=%fused_computation.3 | loop fusion | flops 65536 | bytes 66048 | tf_op jit(solution)/shard_map/convert_element_type | solution.py:97
  1.4 0.2 fusion
  1.6 0.7 %collective-permute-start = (bf16[128,512]{1,0:T(8,128)(2,1)S(1)}, bf16[128,512]{1,0:T(8,128)(2,1)S(1)}, u32[]{:S(2)}, u32[]{:S(2)}) collective-permute-start(bf16[128,512]{1,0:T(8,128)(2,1)S(1)} %fusion), channel_id=1, source_target_pairs={{0,0},{1,5},{2,8},{3,13},{4,16},{5,21},{6,24},{7,29},{8,6},{9,3},{... | collective-permute-start | bytes 393224 | tf_op jit(solution)/shard_map/ppermute | solution.py:284
  2.3 5.7 %collective-permute-start.2 = (bf16[128,512]{1,0:T(8,128)(2,1)S(1)}, bf16[128,512]{1,0:T(8,128)(2,1)S(1)}, u32[]{:S(2)}, u32[]{:S(2)}) collective-permute-start(bf16[128,512]{1,0:T(8,128)(2,1)S(1)} %fusion), channel_id=1, source_target_pairs={{0,2},{1,7},{2,10},{3,15},{4,18},{5,23},{6,26},{7,31},{8,0},{9,5},... | collective-permute-start | bytes 393224 | tf_op jit(solution)/shard_map/ppermute | solution.py:284
  8.0 5.4 %collective-permute-start.4 = (bf16[128,512]{1,0:T(8,128)(2,1)S(1)}, bf16[128,512]{1,0:T(8,128)(2,1)S(1)}, u32[]{:S(2)}, u32[]{:S(2)}) collective-permute-start(bf16[128,512]{1,0:T(8,128)(2,1)S(1)} %fusion), channel_id=1, source_target_pairs={{0,4},{1,1},{2,12},{3,9},{4,20},{5,17},{6,28},{7,25},{8,2},{9,7},{... | collective-permute-start | bytes 393224 | tf_op jit(solution)/shard_map/ppermute | solution.py:284
  13.4 0.1 collective-permute-start.6
  13.5 0.0 collective-permute-done.refs_0_
  13.5 0.1 collective-permute-start.1
  13.6 0.0 collective-permute-done.2.refs_1_
  13.6 0.5 %collective-permute-start.3 = (bf16[128,512]{1,0:T(8,128)(2,1)S(1)}, bf16[128,512]{1,0:T(8,128)(2,1)S(1)}, u32[]{:S(2)}, u32[]{:S(2)}) collective-permute-start(bf16[128,512]{1,0:T(8,128)(2,1)S(1)} %collective-permute-done.2.refs_1_), channel_id=1, source_target_pairs={{1,0},{0,1},{3,2},{2,3},{5,4},{4,5},{7,6},{6,7},{9,8},{8,9},{11,10... | collective-permute-start | bytes 393224 | tf_op jit(solution)/shard_map/ppermute | solution.py:293
  14.1 3.0 %collective-permute-done.4.refs_2_ = bf16[128,512]{1,0:T(8,128)(2,1)S(1)} collective-permute-done((bf16[128,512]{1,0:T(8,128)(2,1)S(1)}, bf16[128,512]{1,0:T(8,128)(2,1)S(1)}, u32[]{:S(2)}, u32[]{:S(2)}) %collective-permute-start.4) | collective-permute-done | bytes 131104 | tf_op jit(solution)/shard_map/ppermute | solution.py:284
  17.1 0.0 collective-permute-start.5
  17.1 3.0 %collective-permute-done.6.refs_3_ = bf16[128,512]{1,0:T(8,128)(2,1)S(1)} collective-permute-done((bf16[128,512]{1,0:T(8,128)(2,1)S(1)}, bf16[128,512]{1,0:T(8,128)(2,1)S(1)}, u32[]{:S(2)}, u32[]{:S(2)}) %collective-permute-start.6) | collective-permute-done | bytes 131104 | tf_op jit(solution)/shard_map/ppermute | solution.py:284
  20.1 0.0 collective-permute-start.7
  20.1 1.4 %load.1.refs_4_.refs_6_ = bf16[3,1024,256]{2,1,0:T(8,128)(2,1)S(1)} custom-call(bf16[3,1024,256]{2,1,0:T(8,128)(2,1)} %bitcast.4), custom_call_target="tpu_custom_call" | custom-call | tf_op jit(solution)/shard_map/load/pallas_call | solution.py:295
  21.5 0.7 %own.1 = (bf16[256,512]{1,0:T(8,128)(2,1)S(1)}, f32[3,256,256]{2,1,0:T(8,128)S(1)}) custom-call(bf16[128,512]{1,0:T(8,128)(2,1)S(1)} %collective-permute-done.refs_0_, bf16[128,512]{1,0:T(8,128)(2,1)S(1)} %collective-permute-done.2.refs_1_, bf16[128,512]{1,0:T(8,128)(2,1)S(1)} %collective-permute-done.4.refs_2_, ...), custom_call_target="tpu_custom_call" | custom-call | tf_op jit(solution)/shard_map/own/pallas_call | solution.py:304
  22.1 0.0 collective-permute-done.1.refs_0_
  22.2 0.0 collective-permute-done.3.refs_1_
  22.2 0.0 collective-permute-done.5.refs_2_
  22.2 0.0 collective-permute-done.7.refs_3_
  22.2 0.7 %rest.1 = (s16[648,128]{1,0:T(8,128)(2,1)S(1)}, s16[648,128]{1,0:T(8,128)(2,1)S(1)}, s16[648,128]{1,0:T(8,128)(2,1)S(1)}, s16[648,128]{1,0:T(8,128)(2,1)S(1)}) custom-call(bf16[128,512]{1,0:T(8,128)(2,1)S(1)} %collective-permute-done.1.refs_0_, bf16[128,512]{1,0:T(8,128)(2,1)S(1)} %collective-permute-done.3.refs_1_, ...), custom_call_target="tpu_custom_call" | custom-call | tf_op jit(solution)/shard_map/rest/pallas_call | solution.py:317
  22.9 2.7 %collective-permute-start.10 = (s16[648,128]{1,0:T(8,128)(2,1)S(1)}, s16[648,128]{1,0:T(8,128)(2,1)S(1)}, u32[]{:S(2)}, u32[]{:S(2)}) collective-permute-start(s16[648,128]{1,0:T(8,128)(2,1)S(1)} %get-tuple-element.18), channel_id=1, source_target_pairs={{0,24},{1,9},{2,26},{3,11},{4,28},{5,13},{6,30},{7,15},{8,0},{9,17... | collective-permute-start | bytes 497672 | tf_op jit(solution)/shard_map/ppermute | solution.py:331
  25.7 0.0 collective-permute-start.8
  25.7 3.0 %collective-permute-start.9 = (s16[648,128]{1,0:T(8,128)(2,1)S(1)}, s16[648,128]{1,0:T(8,128)(2,1)S(1)}, u32[]{:S(2)}, u32[]{:S(2)}) collective-permute-start(s16[648,128]{1,0:T(8,128)(2,1)S(1)} %get-tuple-element.17), channel_id=1, source_target_pairs={{0,16},{1,17},{2,18},{3,19},{4,20},{5,21},{6,22},{7,23},{8,24},{9,... | collective-permute-start | bytes 497672 | tf_op jit(solution)/shard_map/ppermute | solution.py:331
  28.7 1.2 %collective-permute-done.10.refs_3_ = s16[648,128]{1,0:T(8,128)(2,1)S(1)} collective-permute-done((s16[648,128]{1,0:T(8,128)(2,1)S(1)}, s16[648,128]{1,0:T(8,128)(2,1)S(1)}, u32[]{:S(2)}, u32[]{:S(2)}) %collective-permute-start.10) | collective-permute-done | bytes 165920 | tf_op jit(solution)/shard_map/ppermute | solution.py:331
  29.9 4.3 %collective-permute-done.8.refs_1_ = s16[648,128]{1,0:T(8,128)(2,1)S(1)} collective-permute-done((s16[648,128]{1,0:T(8,128)(2,1)S(1)}, s16[648,128]{1,0:T(8,128)(2,1)S(1)}, u32[]{:S(2)}, u32[]{:S(2)}) %collective-permute-start.8) | collective-permute-done | bytes 165920 | tf_op jit(solution)/shard_map/ppermute | solution.py:331
  34.2 1.0 %collective-permute-done.9.refs_2_ = s16[648,128]{1,0:T(8,128)(2,1)S(1)} collective-permute-done((s16[648,128]{1,0:T(8,128)(2,1)S(1)}, s16[648,128]{1,0:T(8,128)(2,1)S(1)}, u32[]{:S(2)}, u32[]{:S(2)}) %collective-permute-start.9) | collective-permute-done | bytes 165920 | tf_op jit(solution)/shard_map/ppermute | solution.py:331
  35.2 0.4 %attend.1 = (bf16[64,128]{1,0:T(8,128)(2,1)S(1)}, bf16[64,128]{1,0:T(8,128)(2,1)S(1)}) custom-call(s16[648,128]{1,0:T(8,128)(2,1)S(1)} %get-tuple-element.15.refs_0_, s16[648,128]{1,0:T(8,128)(2,1)S(1)} %collective-permute-done.8.refs_1_, s16[648,128]{1,0:T(8,128)(2,1)S(1)} %collective-permute-done.9.refs_2_, s16[648,128]{1,0:T(8,128)(2,1)S(1)} %collective-permute-done.10.refs_3_), custom_call_target="tpu_custom_call" | custom-call | tf_op jit(solution)/shard_map/attend/pallas_call | solution.py:332
  35.6 2.0 %collective-permute-start.11 = (bf16[64,128]{1,0:T(8,128)(2,1)S(1)}, bf16[64,128]{1,0:T(8,128)(2,1)S(1)}, u32[]{:S(2)}, u32[]{:S(2)}) collective-permute-start(bf16[64,128]{1,0:T(8,128)(2,1)S(1)} %get-tuple-element.19), channel_id=1, source_target_pairs={{0,8},{8,0},{16,24},{24,16},{1,9},{9,1},{17,25},{25,17},{2,10},{10... | collective-permute-start | bytes 49160 | tf_op jit(solution)/shard_map/ppermute | solution.py:345
  37.6 1.8 %collective-permute-done.11 = bf16[64,128]{1,0:T(8,128)(2,1)S(1)} collective-permute-done((bf16[64,128]{1,0:T(8,128)(2,1)S(1)}, bf16[64,128]{1,0:T(8,128)(2,1)S(1)}, u32[]{:S(2)}, u32[]{:S(2)}) %collective-permute-start.11) | collective-permute-done | bytes 16416 | tf_op jit(solution)/shard_map/ppermute | solution.py:345
  39.5 0.6 %pad_maximum_fusion = bf16[64,256]{1,0:T(8,128)(2,1)} fusion(bf16[64,128]{1,0:T(8,128)(2,1)S(1)} %get-tuple-element.22, bf16[64,128]{1,0:T(8,128)(2,1)S(1)} %get-tuple-element.21), kind=kLoop, calls=%fused_computation.4 | loop fusion | flops 65536 | bytes 65536 | tf_op jit(solution)/shard_map/concatenate | solution.py:353
  (3 shorter events, 0.0 us)
Async XLA Ops:
  0.0 1.4 %copy-start = (bf16[256,512]{1,0:T(8,128)(2,1)S(1)}, bf16[256,512]{1,0:T(8,128)(2,1)}, u32[]{:S(2)}) copy-start(bf16[256,512]{1,0:T(8,128)(2,1)} %param.4) | copy-start | bytes 786436
  1.6 11.9 %collective-permute-start = (bf16[128,512]{1,0:T(8,128)(2,1)S(1)}, bf16[128,512]{1,0:T(8,128)(2,1)S(1)}, u32[]{:S(2)}, u32[]{:S(2)}) collective-permute-start(bf16[128,512]{1,0:T(8,128)(2,1)S(1)} %fusion), channel_id=1, source_target_pairs={{0,0},{1,5},{2,8},{3,13},{4,16},{5,21},{6,24},{7,29},{8,6},{9,3},{... | collective-permute-start | bytes 393224 | tf_op jit(solution)/shard_map/ppermute | solution.py:284
  2.3 11.3 %collective-permute-start.2 = (bf16[128,512]{1,0:T(8,128)(2,1)S(1)}, bf16[128,512]{1,0:T(8,128)(2,1)S(1)}, u32[]{:S(2)}, u32[]{:S(2)}) collective-permute-start(bf16[128,512]{1,0:T(8,128)(2,1)S(1)} %fusion), channel_id=1, source_target_pairs={{0,2},{1,7},{2,10},{3,15},{4,18},{5,23},{6,26},{7,31},{8,0},{9,5},... | collective-permute-start | bytes 393224 | tf_op jit(solution)/shard_map/ppermute | solution.py:284
  8.0 9.1 %collective-permute-start.4 = (bf16[128,512]{1,0:T(8,128)(2,1)S(1)}, bf16[128,512]{1,0:T(8,128)(2,1)S(1)}, u32[]{:S(2)}, u32[]{:S(2)}) collective-permute-start(bf16[128,512]{1,0:T(8,128)(2,1)S(1)} %fusion), channel_id=1, source_target_pairs={{0,4},{1,1},{2,12},{3,9},{4,20},{5,17},{6,28},{7,25},{8,2},{9,7},{... | collective-permute-start | bytes 393224 | tf_op jit(solution)/shard_map/ppermute | solution.py:284
  13.4 6.6 %collective-permute-start.6 = (bf16[128,512]{1,0:T(8,128)(2,1)S(1)}, bf16[128,512]{1,0:T(8,128)(2,1)S(1)}, u32[]{:S(2)}, u32[]{:S(2)}) collective-permute-start(bf16[128,512]{1,0:T(8,128)(2,1)S(1)} %fusion), channel_id=1, source_target_pairs={{0,6},{1,3},{2,14},{3,11},{4,22},{5,19},{6,30},{7,27},{8,4},{9,1},... | collective-permute-start | bytes 393224 | tf_op jit(solution)/shard_map/ppermute | solution.py:284
  13.5 8.7 %collective-permute-start.1 = (bf16[128,512]{1,0:T(8,128)(2,1)S(1)}, bf16[128,512]{1,0:T(8,128)(2,1)S(1)}, u32[]{:S(2)}, u32[]{:S(2)}) collective-permute-start(bf16[128,512]{1,0:T(8,128)(2,1)S(1)} %collective-permute-done.refs_0_), channel_id=1, source_target_pairs={{1,0},{0,1},{3,2},{2,3},{5,4},{4,5},{7,6},{6,7},{9,8},{8,9},{11,10... | collective-permute-start | bytes 393224 | tf_op jit(solution)/shard_map/ppermute | solution.py:293
  13.6 8.6 %collective-permute-start.3 = (bf16[128,512]{1,0:T(8,128)(2,1)S(1)}, bf16[128,512]{1,0:T(8,128)(2,1)S(1)}, u32[]{:S(2)}, u32[]{:S(2)}) collective-permute-start(bf16[128,512]{1,0:T(8,128)(2,1)S(1)} %collective-permute-done.2.refs_1_), channel_id=1, source_target_pairs={{1,0},{0,1},{3,2},{2,3},{5,4},{4,5},{7,6},{6,7},{9,8},{8,9},{11,10... | collective-permute-start | bytes 393224 | tf_op jit(solution)/shard_map/ppermute | solution.py:293
  17.1 5.1 %collective-permute-start.5 = (bf16[128,512]{1,0:T(8,128)(2,1)S(1)}, bf16[128,512]{1,0:T(8,128)(2,1)S(1)}, u32[]{:S(2)}, u32[]{:S(2)}) collective-permute-start(bf16[128,512]{1,0:T(8,128)(2,1)S(1)} %collective-permute-done.4.refs_2_), channel_id=1, source_target_pairs={{1,0},{0,1},{3,2},{2,3},{5,4},{4,5},{7,6},{6,7},{9,8},{8,9},{11,10... | collective-permute-start | bytes 393224 | tf_op jit(solution)/shard_map/ppermute | solution.py:293
  20.1 2.1 %collective-permute-start.7 = (bf16[128,512]{1,0:T(8,128)(2,1)S(1)}, bf16[128,512]{1,0:T(8,128)(2,1)S(1)}, u32[]{:S(2)}, u32[]{:S(2)}) collective-permute-start(bf16[128,512]{1,0:T(8,128)(2,1)S(1)} %collective-permute-done.6.refs_3_), channel_id=1, source_target_pairs={{1,0},{0,1},{3,2},{2,3},{5,4},{4,5},{7,6},{6,7},{9,8},{8,9},{11,10... | collective-permute-start | bytes 393224 | tf_op jit(solution)/shard_map/ppermute | solution.py:293
  22.9 6.9 %collective-permute-start.10 = (s16[648,128]{1,0:T(8,128)(2,1)S(1)}, s16[648,128]{1,0:T(8,128)(2,1)S(1)}, u32[]{:S(2)}, u32[]{:S(2)}) collective-permute-start(s16[648,128]{1,0:T(8,128)(2,1)S(1)} %get-tuple-element.18), channel_id=1, source_target_pairs={{0,24},{1,9},{2,26},{3,11},{4,28},{5,13},{6,30},{7,15},{8,0},{9,17... | collective-permute-start | bytes 497672 | tf_op jit(solution)/shard_map/ppermute | solution.py:331
  25.7 8.6 %collective-permute-start.8 = (s16[648,128]{1,0:T(8,128)(2,1)S(1)}, s16[648,128]{1,0:T(8,128)(2,1)S(1)}, u32[]{:S(2)}, u32[]{:S(2)}) collective-permute-start(s16[648,128]{1,0:T(8,128)(2,1)S(1)} %get-tuple-element.16), channel_id=1, source_target_pairs={{0,8},{1,25},{2,10},{3,27},{4,12},{5,29},{6,14},{7,31},{8,16},{9,1... | collective-permute-start | bytes 497672 | tf_op jit(solution)/shard_map/ppermute | solution.py:331
  25.7 9.6 %collective-permute-start.9 = (s16[648,128]{1,0:T(8,128)(2,1)S(1)}, s16[648,128]{1,0:T(8,128)(2,1)S(1)}, u32[]{:S(2)}, u32[]{:S(2)}) collective-permute-start(s16[648,128]{1,0:T(8,128)(2,1)S(1)} %get-tuple-element.17), channel_id=1, source_target_pairs={{0,16},{1,17},{2,18},{3,19},{4,20},{5,21},{6,22},{7,23},{8,24},{9,... | collective-permute-start | bytes 497672 | tf_op jit(solution)/shard_map/ppermute | solution.py:331
  35.6 3.8 %collective-permute-start.11 = (bf16[64,128]{1,0:T(8,128)(2,1)S(1)}, bf16[64,128]{1,0:T(8,128)(2,1)S(1)}, u32[]{:S(2)}, u32[]{:S(2)}) collective-permute-start(bf16[64,128]{1,0:T(8,128)(2,1)S(1)} %get-tuple-element.19), channel_id=1, source_target_pairs={{0,8},{8,0},{16,24},{24,16},{1,9},{9,1},{17,25},{25,17},{2,10},{10... | collective-permute-start | bytes 49160 | tf_op jit(solution)/shard_map/ppermute | solution.py:345
